TPU v7x, 32 devices: a whole 2x2x4 slice. The times are simulated.
32 devices in a mesh: expert: 8 (over y, x, core), row: 4 (over z).
Axes of the slice: x: 2, y: 2, z: 4, core: 2. Of those that a mesh axis runs over, the one named last changes fastest.
Arguments:
- weights: bfloat16 [8, 7168, 2048], P('expert', 'row'), may hold values from -6 to 6
- left_bits: int32 [8, 7168], P('expert', 'row'), may hold values from 0 to 1
- right_bits: int32 [8, 2048], P('expert'), may hold values from 0 to 1
- groups: int32 [8, 2048], P('expert'), may hold values from 0 to 15, never falling along the last dimension, each value on 1 to 256 neighbouring positions
Outputs:
- scaled: bfloat16 [8, 7168, 2048], P('expert', 'row')
- block_error: float32 [8, 7168, 256], P('expert', 'row')
- scales: float32 [8, 16], P('expert')
- expert_error: float32 [8], P('expert')
- total_error: float32 [], replicated
Inputs may be any that keep to these rules, and one draw needn't show every extreme that they name: Along each expert's 2048 columns the group number never falls; each of the 16 groups holds 1 to 256 columns.
All inputs are finite; a program needn't handle non-finite values.
Results may differ from a plain program's by a relative error of at most 0.0091.
Values may be sent and summed in bfloat16 or wider, within the bound.
No kernel may reach another device: no remote copies, remote signals or barrier semaphores. Data moves between devices by JAX's collectives and lax.ppermute only.
A program may use at most 192 MiB of HBM per device.

v0:
```python
import math

import jax
import jax.numpy as jnp
from jax import lax
from jax.experimental import pallas as pl
from jax.experimental.pallas import tpu as pltpu
from jax.sharding import PartitionSpec as P

HB = 128
GROUPS = 16
INNER = 256
LOW = 16
CHUNKS = 4
AHEAD = 2
OCTET = 8


def butterfly(parts):
    parts = list(parts)
    step = 1
    while step < len(parts):
        for base in range(len(parts)):
            if not base & step:
                low, high = parts[base], parts[base | step]
                parts[base], parts[base | step] = low + high, low - high
        step *= 2
    return parts


def column_transform(weights, left_bits, right_bits, place, ring, chunks):
    rows, width = weights.shape
    tile = 2 * HB
    count = width // INNER
    piece = width // (chunks * ring)
    root = 1.0 / math.sqrt(width)

    def kernel(place_ref, w_ref, left_ref, right_ref, *rest):
        outs = rest[: chunks * ring]
        table, stage, left_col, natural = rest[chunks * ring :]
        mine = place_ref[0]

        @pl.when(pl.program_id(0) == 0)
        def _():
            common = lax.broadcasted_iota(jnp.int32, (INNER, INNER), 0) & lax.broadcasted_iota(
                jnp.int32, (INNER, INNER), 1
            )
            for bits in (4, 2, 1):
                common = common ^ (common >> bits)
            table[...] = (1 - 2 * (common & 1)).astype(jnp.float32).astype(jnp.bfloat16)

        eye = lax.broadcasted_iota(jnp.int32, (HB, HB), 0) == lax.broadcasted_iota(jnp.int32, (HB, HB), 1)
        for part in range(tile // HB):
            cols = slice(part * HB, (part + 1) * HB)
            signs = (2 * left_ref[:, cols] - 1).astype(jnp.float32) * root
            left_col[cols, :] = jnp.sum(jnp.where(eye, signs, 0.0), axis=1, keepdims=True)
        right = (2 * right_ref[...] - 1).astype(jnp.float32).astype(jnp.bfloat16)
        signed = [
            w_ref[:, hi * INNER : (hi + 1) * INNER] * right[:, hi * INNER : (hi + 1) * INNER]
            for hi in range(count)
        ]
        turned = jnp.dot(jnp.concatenate(signed, axis=0), table[...], preferred_element_type=jnp.float32)
        stage[...] = turned.reshape(count, tile, INNER)

        def one(group, _):
            start = pl.multiple_of(group * LOW, LOW)
            left = left_col[pl.ds(start, LOW), :]
            parts = butterfly([stage[hi, pl.ds(start, LOW), :] for hi in range(count)])
            for hi, part in enumerate(parts):
                natural[pl.ds(start, LOW), hi * INNER : (hi + 1) * INNER] = (part * left).astype(jnp.bfloat16)
            return 0

        lax.fori_loop(0, tile // LOW, one, 0)
        for chunk in range(chunks):
            for shift in range(ring):
                dest = lax.rem(mine + shift, ring)
                start = pl.multiple_of((chunk * ring + dest) * piece, 128)
                outs[chunk * ring + shift][...] = natural[:, pl.ds(start, piece)]

    pieces = chunks * ring
    outs = pl.pallas_call(
        kernel,
        grid=(rows // tile,),
        in_specs=[
            pl.BlockSpec(memory_space=pltpu.SMEM),
            pl.BlockSpec((tile, width), lambda r: (r, 0)),
            pl.BlockSpec((1, tile), lambda r: (0, r)),
            pl.BlockSpec((1, width), lambda r: (0, 0)),
        ],
        out_specs=[pl.BlockSpec((tile, piece), lambda r: (r, 0))] * pieces,
        out_shape=[jax.ShapeDtypeStruct((rows, piece), jnp.bfloat16)] * pieces,
        scratch_shapes=[
            pltpu.VMEM((INNER, INNER), jnp.bfloat16),
            pltpu.VMEM((count, tile, INNER), jnp.float32),
            pltpu.VMEM((tile, 1), jnp.float32),
            pltpu.VMEM((tile, width), jnp.bfloat16),
        ],
        name="column_transform",
    )(place, weights, left_bits, right_bits)
    return [outs[c * ring : (c + 1) * ring] for c in range(chunks)]


def row_mix(pieces, mixer, own_groups, before):
    ring = len(pieces)
    rows, width = pieces[0].shape
    blocks = rows // HB
    high = HB // LOW
    band = blocks * LOW
    root = 1.0 / math.sqrt(HB)

    def kernel(*refs):
        ins, m_ref, group_ref, before_ref = refs[:ring], refs[ring], refs[ring + 1], refs[ring + 2]
        outs, peak_ref, stage = refs[ring + 3 : 2 * ring + 3], refs[2 * ring + 3], refs[2 * ring + 4]
        for hi in range(high):
            rhs = jnp.concatenate([r[:, hi].reshape(band, width) for r in ins], axis=0)
            stage[hi] = jnp.dot(m_ref[...], rhs, preferred_element_type=jnp.float32)

        peak = jnp.zeros((LOW, width), jnp.float32)
        for shift in range(ring):

            def one(a, peak):
                start = pl.multiple_of(shift * band + a * LOW, LOW)
                parts = butterfly([stage[hi, pl.ds(start, LOW), :] for hi in range(high)])
                for hi, part in enumerate(parts):
                    part = part * root
                    peak = jnp.maximum(peak, jnp.abs(part))
                    outs[shift][a, hi] = part.astype(jnp.bfloat16)
                return peak

            peak = lax.fori_loop(0, blocks, one, peak)
        column_peak = jnp.max(peak, axis=0, keepdims=True)
        ids = lax.broadcasted_iota(jnp.int32, (GROUPS, width), 0)
        held = jnp.max(jnp.where(group_ref[...] == ids, column_peak, 0.0), axis=1, keepdims=True)
        peak_ref[...] = jnp.maximum(before_ref[...], held)

    shaped = [p.reshape(blocks, high, LOW, width) for p in pieces]
    result = pl.pallas_call(
        kernel,
        out_shape=[jax.ShapeDtypeStruct((blocks, high, LOW, width), jnp.bfloat16)] * ring
        + [jax.ShapeDtypeStruct((GROUPS, 128), jnp.float32)],
        scratch_shapes=[pltpu.VMEM((high, ring * band, width), jnp.float32)],
        name="row_mix",
    )(*shaped, mixer, own_groups, before)
    return [y.reshape(rows, width) for y in result[:ring]], result[ring]


def quantize(part_index, pieces, scale_row, scale_octet, spread, numbers, before):
    each = len(pieces)
    ring = len(pieces[0])
    rows, piece = pieces[0][0].shape
    width = each * ring * piece
    lanes = width // OCTET
    parts_in_all = scale_row.shape[1] // width
    tile = 2 * HB
    flat = [p for chunk in pieces for p in chunk]

    def kernel(num_ref, *refs):
        ins = refs[: each * ring]
        row_ref, oct_ref, spread_ref = refs[each * ring : each * ring + 3]
        scaled_ref, error_ref, sum_ref, stage = refs[-4:]
        mine, first, total = num_ref[0], num_ref[1], num_ref[2]
        step = pl.program_id(0)
        stage[...] = jnp.dot(
            jnp.concatenate([r[...] for r in ins], axis=1), spread_ref[...], preferred_element_type=jnp.float32
        )
        starts = []
        for index in range(each * ring):
            owner = lax.rem(mine - index % ring + ring, ring)
            starts.append(pl.multiple_of((index // ring * ring + owner) * piece, 128))
        share = 4.0 / (3.0 * total.astype(jnp.float32))

        def one(group, carry):
            held = pl.ds(pl.multiple_of(group * LOW, LOW), LOW)
            for index in range(each * ring):
                cols = pl.ds(starts[index], piece)
                scaled = ins[index][held, :].astype(jnp.float32) * row_ref[:, cols]
                scaled_ref[held, cols] = scaled.astype(jnp.bfloat16)
            near_sum = low_sum = squares = far_squares = largest = smallest = None
            for i in range(OCTET):
                value = stage[held, i * lanes : (i + 1) * lanes] * oct_ref[i : i + 1, :]
                near = jnp.floor(value + 0.5)
                low = jnp.floor(value)
                gap = jnp.abs(value - near)
                far = 0.5 - gap
                if i == 0:
                    near_sum, low_sum, squares, far_squares = near, low, gap * gap, far * far
                    largest = smallest = gap
                else:
                    near_sum, low_sum = near_sum + near, low_sum + low
                    squares, far_squares = squares + gap * gap, far_squares + far * far
                    largest, smallest = jnp.maximum(largest, gap), jnp.minimum(smallest, gap)
            near_half, low_half = near_sum * 0.5, low_sum * 0.5
            whole = jnp.where(near_half != jnp.floor(near_half), squares + (1.0 - 2.0 * largest), squares)
            shifted = jnp.where(low_half != jnp.floor(low_half), far_squares + 2.0 * smallest, far_squares)
            error = jnp.minimum(whole, shifted)
            error_ref[held, :] = error
            position = lax.broadcasted_iota(jnp.int32, (LOW, lanes), 0) + (first + step * tile + group * LOW)
            weight = (position.astype(jnp.float32) + 0.5) * share + (1.0 / 3.0)
            return carry + error * weight

        part = lax.fori_loop(0, tile // LOW, one, jnp.zeros((LOW, lanes), jnp.float32))

        @pl.when(step == 0)
        def _():
            sum_ref[...] = jnp.zeros_like(sum_ref)

        sum_ref[...] += part

    in_specs = [pl.BlockSpec(memory_space=pltpu.SMEM)]
    in_specs += [pl.BlockSpec((tile, piece), lambda r: (r, 0))] * (each * ring)
    in_specs += [
        pl.BlockSpec((1, width), lambda r: (0, part_index)),
        pl.BlockSpec((OCTET, lanes), lambda r: (0, part_index)),
        pl.BlockSpec((width, width), lambda r: (0, 0)),
    ]
    operands = [numbers, *flat, scale_row, scale_octet, spread]
    aliases = {}
    if before is not None:
        aliases = {len(operands): 0, len(operands) + 1: 1}
        in_specs += [pl.BlockSpec(memory_space=pl.ANY)] * 2
        operands += list(before)
    return pl.pallas_call(
        kernel,
        grid=(rows // tile,),
        in_specs=in_specs,
        out_specs=[
            pl.BlockSpec((tile, width), lambda r: (r, part_index)),
            pl.BlockSpec((tile, lanes), lambda r: (r, part_index)),
            pl.BlockSpec((LOW, lanes), lambda r: (0, 0)),
        ],
        out_shape=[
            jax.ShapeDtypeStruct((rows, parts_in_all * width), jnp.bfloat16),
            jax.ShapeDtypeStruct((rows, parts_in_all * lanes), jnp.float32),
            jax.ShapeDtypeStruct((LOW, lanes), jnp.float32),
        ],
        scratch_shapes=[pltpu.VMEM((tile, width), jnp.float32)],
        input_output_aliases=aliases,
        name="quantize",
    )(*operands)


def mixer_table(mine, ring, blocks):
    side = ring * blocks * LOW
    row = lax.broadcasted_iota(jnp.int32, (side, side), 0)
    col = lax.broadcasted_iota(jnp.int32, (side, side), 1)
    band = blocks * LOW
    first = (((mine + row // band) % ring) * blocks + (row % band) // LOW).astype(jnp.float32)
    second = (((mine - col // band + ring) % ring) * blocks + (col % band) // LOW).astype(jnp.float32)
    order = ring * blocks
    table = math.sqrt(2.0 / order) * jnp.cos(math.pi * (2.0 * second + 1.0) * first / (2.0 * order))
    table = jnp.where(first == 0.0, table * math.sqrt(0.5), table)
    common = (row % LOW) & (col % LOW)
    common = common ^ (common >> 2)
    common = common ^ (common >> 1)
    return jnp.where((common & 1) == 0, table, -table).astype(jnp.bfloat16)


def spread_table(mine, ring, piece, width):
    row = lax.broadcasted_iota(jnp.int32, (width, width), 0)
    col = lax.broadcasted_iota(jnp.int32, (width, width), 1)
    index = row // piece
    natural = (index // ring * ring + (mine - index % ring + ring) % ring) * piece + row % piece
    target = (natural % OCTET) * (width // OCTET) + natural // OCTET
    return (target == col).astype(jnp.bfloat16)


def body(weights, left_bits, right_bits, groups):
    experts, local_rows, width = weights.shape
    assert experts == 1
    ring = lax.axis_size("row")
    mine = lax.axis_index("row").astype(jnp.int32)
    blocks_here = local_rows // HB
    chunks = chunk_count(width, ring)
    piece = width // (chunks * ring)
    unit = OCTET * 128
    each = unit // (ring * piece)
    place = mine.reshape(1)

    def send(x, shift):
        return lax.ppermute(x, "row", [(k, (k + shift) % ring) for k in range(ring)])

    outgoing = column_transform(weights[0], left_bits, right_bits, place, ring, chunks)
    mixer = mixer_table(mine, ring, blocks_here)
    spread = spread_table(mine, ring, piece, unit)
    own_groups = [
        lax.dynamic_slice_in_dim(groups, (chunk * ring + mine) * piece, piece, 1) for chunk in range(chunks)
    ]
    received, returned = [], []
    peak = jnp.zeros((GROUPS, 128), jnp.float32)
    for chunk in range(chunks):
        leaving = outgoing[chunk][1:]
        if chunk >= AHEAD:
            leaving, received[chunk - AHEAD] = lax.optimization_barrier((leaving, received[chunk - AHEAD]))
        received.append([send(leaving[s - 1], s) for s in range(1, ring)])
    peaks = None
    for chunk in range(chunks):
        mixed, peak = row_mix([outgoing[chunk][0]] + received[chunk], mixer, own_groups[chunk], peak)
        if chunk == chunks - 1:
            peaks = [peak] + [send(peak, s) for s in range(1, ring)]
        returned.append([mixed[0]] + [send(mixed[s], s) for s in range(1, ring)])

    group_peak = jnp.max(jnp.stack(peaks), axis=(0, 2))
    group_peak = jnp.maximum(group_peak, 1.0)
    in_group = groups == jnp.arange(GROUPS, dtype=jnp.int32)[:, None]
    scale_row = jnp.sum(jnp.where(in_group, (2.0 / group_peak)[:, None], 0.0), axis=0)
    scale_octet = scale_row.reshape(width // OCTET, OCTET).T

    numbers = jnp.stack([mine, mine * local_rows, jnp.int32(local_rows) * ring])
    before, total = None, 0.0
    for part_index in range(width // unit):
        held = returned[part_index * each : (part_index + 1) * each]
        scaled, errors, part = quantize(
            part_index, held, scale_row[None, :], scale_octet, spread, numbers, before
        )
        before = (scaled, errors)
        total = total + part
    partial_error = jnp.sum(total) / (local_rows * ring * width // OCTET)
    expert_count = experts * lax.axis_size("expert")
    expert = lax.axis_index("expert")
    slots = jnp.where(jnp.arange(expert_count) == expert, partial_error, 0.0)
    every_error = lax.psum(slots, ("expert", "row"))
    expert_error = lax.dynamic_slice_in_dim(every_error, expert, 1)
    total_error = jnp.sum(every_error) / expert_count
    return (scaled[None], errors[None], (group_peak / 2.0)[None], expert_error, total_error)


def chunk_count(width, ring):
    return min(CHUNKS, width // (128 * ring))


def solution(mesh):
    placed = (P("expert", "row", None), P("expert", "row"), P("expert", None), P("expert", None))
    return jax.shard_map(
        body,
        mesh=mesh,
        in_specs=placed,
        out_specs=(
            P("expert", "row", None),
            P("expert", "row", None),
            P("expert", None),
            P("expert"),
            P(),
        ),
        check_vma=False,
    )
```

profile of v0, /device:TPU:0, one launch (start us, length us, event | category | flops | bytes accessed | tf_op | source)
XLA Modules:
  0.0 400.1 jit_solution(11523554221375369527)
XLA Ops:
  0.6 16.5 %column_transform.1 = (bf16[1792,128]{1,0:T(8,128)(2,1)}, bf16[1792,128]{1,0:T(8,128)(2,1)}, bf16[1792,128]{1,0:T(8,128)(2,1)}, bf16[1792,128]{1,0:T(8,128)(2,1)...) custom-call(s32[1]{0:T(128)} %bitcast.place_ref, ...), custom_call_target="tpu_custom_call" | custom-call | tf_op jit(solution)/shard_map/column_transform/pallas_call | solution.py:81
  17.1 3.1 collective-permute-start
  20.2 2.6 collective-permute-start.1
  25.2 8.8 %collective-permute-done = bf16[1792,128]{1,0:T(8,128)(2,1)S(1)} collective-permute-done((bf16[1792,128]{1,0:T(8,128)(2,1)}, bf16[1792,128]{1,0:T(8,128)(2,1)S(1)}, u32[]{:S(2)}, u32[]{:S(2)}) %collective-permute-start) | collective-permute-done | bytes 458784 | tf_op jit(solution)/shard_map/ppermute | solution.py:280
  34.0 2.5 collective-permute-start.8
  36.4 17.2 %collective-permute-done.1 = bf16[1792,128]{1,0:T(8,128)(2,1)S(1)} collective-permute-done((bf16[1792,128]{1,0:T(8,128)(2,1)}, bf16[1792,128]{1,0:T(8,128)(2,1)S(1)}, u32[]{:S(2)}, u32[]{:S(2)}) %collective-permute-start.1) | collective-permute-done | bytes 458784 | tf_op jit(solution)/shard_map/ppermute | solution.py:280
  53.7 30.1 %collective-permute-start.3 = (bf16[1792,128]{1,0:T(8,128)(2,1)}, bf16[1792,128]{1,0:T(8,128)(2,1)S(1)}, u32[]{:S(2)}, u32[]{:S(2)}) collective-permute-start(bf16[1792,128]{1,0:T(8,128)(2,1)} %get-tuple-element.66), channel_id=1, source_target_pairs={{0,1},{1,2},{2,3},{3,0},{4,5},{5,6},{6,7},{7,4},{8,9},{9,10},{10,1... | collective-permute-start | bytes 1376264 | tf_op jit(solution)/shard_map/ppermute | solution.py:280
  86.1 20.4 %fusion.37.refs_4_ = bf16[896,896]{1,0:T(8,128)(2,1)} fusion(s32[896]{0:T(1024)S(1)} %get-tuple-element.120, s32[896]{0:T(1024)S(1)} %get-tuple-element.121, s32[896]{0:T(1024)S(1)} %get-tuple-element.119, s32[896]{0:T(1024)S(1)} %get-tuple-element.126, s32[]{:T(128)} %axis_index.22, s32[896]{0:T(1024)S(1)} %get-tuple-element.122, ...), kind=kLoop, calls=%fused_computation.77 | loop fusion | flops 69042176 | bytes 1629828 | tf_op jit(solution)/shard_map/convert_element_type | solution.py:255
  106.5 5.3 %collective-permute-done.7 = bf16[1792,128]{1,0:T(8,128)(2,1)S(1)} collective-permute-done((bf16[1792,128]{1,0:T(8,128)(2,1)}, bf16[1792,128]{1,0:T(8,128)(2,1)S(1)}, u32[]{:S(2)}, u32[]{:S(2)}) %collective-permute-start.7) | collective-permute-done | bytes 458784 | tf_op jit(solution)/shard_map/ppermute | solution.py:280
  111.8 10.5 %collective-permute-start.12 = (bf16[1792,128]{1,0:T(8,128)(2,1)}, bf16[1792,128]{1,0:T(8,128)(2,1)}, u32[]{:S(2)}, u32[]{:S(2)}) collective-permute-start(bf16[1792,128]{1,0:T(8,128)(2,1)} %get-tuple-element.90), channel_id=1, source_target_pairs={{0,1},{1,2},{2,3},{3,0},{4,5},{5,6},{6,7},{7,4},{8,9},{9,10},{10,1... | collective-permute-start | bytes 1376264 | tf_op jit(solution)/shard_map/ppermute | solution.py:280
  122.3 2.6 collective-permute-start.13
  126.1 7.9 %row_mix.4 = (bf16[14,8,16,128]{3,2,1,0:T(8,128)(2,1)}, bf16[14,8,16,128]{3,2,1,0:T(8,128)(2,1)}, bf16[14,8,16,128]{3,2,1,0:T(8,128)(2,1)}, bf16[14,8,16,128]{3,2,1,0:T(8,128)(2,1)}, f32[16,128]{1,0:T(8,128)}) custom-call(bf16[14,8,16,128]{3,2,1,0:T(8,128)(2,1)} %bitcast.50, bf16[14,8,16,128]{3,2,1,0:T(8,128)(2,1)} %bitcast.51, ...), custom_call_target="tpu_custom_call" | custom-call | tf_op jit(solution)/shard_map/row_mix/pallas_call | solution.py:137
  134.0 7.9 %row_mix.5 = (bf16[14,8,16,128]{3,2,1,0:T(8,128)(2,1)}, bf16[14,8,16,128]{3,2,1,0:T(8,128)(2,1)}, bf16[14,8,16,128]{3,2,1,0:T(8,128)(2,1)}, bf16[14,8,16,128]{3,2,1,0:T(8,128)(2,1)}, f32[16,128]{1,0:T(8,128)}) custom-call(bf16[14,8,16,128]{3,2,1,0:T(8,128)(2,1)} %bitcast.49, bf16[14,8,16,128]{3,2,1,0:T(8,128)(2,1)} %bitcast.52, ...), custom_call_target="tpu_custom_call" | custom-call | tf_op jit(solution)/shard_map/row_mix/pallas_call | solution.py:137
  141.9 9.2 %collective-permute-done.4 = bf16[1792,128]{1,0:T(8,128)(2,1)S(1)} collective-permute-done((bf16[1792,128]{1,0:T(8,128)(2,1)}, bf16[1792,128]{1,0:T(8,128)(2,1)S(1)}, u32[]{:S(2)}, u32[]{:S(2)}) %collective-permute-start.4) | collective-permute-done | bytes 458784 | tf_op jit(solution)/shard_map/ppermute | solution.py:280
  151.1 9.8 %collective-permute-start.24 = (bf16[1792,128]{1,0:T(8,128)(2,1)}, bf16[1792,128]{1,0:T(8,128)(2,1)S(1)}, u32[]{:S(2)}, u32[]{:S(2)}) collective-permute-start(bf16[1792,128]{1,0:T(8,128)(2,1)} %bitcast.72), channel_id=1, source_target_pairs={{0,1},{1,2},{2,3},{3,0},{4,5},{5,6},{6,7},{7,4},{8,9},{9,10},{10,1... | collective-permute-start | bytes 1376264 | tf_op jit(solution)/shard_map/ppermute | solution.py:280
  161.0 3.3 collective-permute-start.25
  164.3 7.9 %row_mix.6 = (bf16[14,8,16,128]{3,2,1,0:T(8,128)(2,1)}, bf16[14,8,16,128]{3,2,1,0:T(8,128)(2,1)}, bf16[14,8,16,128]{3,2,1,0:T(8,128)(2,1)}, bf16[14,8,16,128]{3,2,1,0:T(8,128)(2,1)}, f32[16,128]{1,0:T(8,128)}) custom-call(bf16[14,8,16,128]{3,2,1,0:T(8,128)(2,1)} %bitcast.48, bf16[14,8,16,128]{3,2,1,0:T(8,128)(2,1)} %bitcast.55, ...), custom_call_target="tpu_custom_call" | custom-call | tf_op jit(solution)/shard_map/row_mix/pallas_call | solution.py:137
  172.1 18.4 %collective-permute-done.13 = bf16[1792,128]{1,0:T(8,128)(2,1)} collective-permute-done((bf16[1792,128]{1,0:T(8,128)(2,1)}, bf16[1792,128]{1,0:T(8,128)(2,1)}, u32[]{:S(2)}, u32[]{:S(2)}) %collective-permute-start.13) | collective-permute-done | bytes 458784 | tf_op jit(solution)/shard_map/ppermute | solution.py:280
  190.6 7.9 %row_mix.7 = (bf16[14,8,16,128]{3,2,1,0:T(8,128)(2,1)}, bf16[14,8,16,128]{3,2,1,0:T(8,128)(2,1)}, bf16[14,8,16,128]{3,2,1,0:T(8,128)(2,1)}, bf16[14,8,16,128]{3,2,1,0:T(8,128)(2,1)}, f32[16,128]{1,0:T(8,128)}) custom-call(bf16[14,8,16,128]{3,2,1,0:T(8,128)(2,1)} %bitcast.47, bf16[14,8,16,128]{3,2,1,0:T(8,128)(2,1)} %bitcast.20.refs_1_, ...), custom_call_target="tpu_custom_call" | custom-call | tf_op jit(solution)/shard_map/row_mix/pallas_call | solution.py:137
  198.4 10.4 %collective-permute-start.18 = (f32[16,128]{1,0:T(8,128)}, f32[16,128]{1,0:T(8,128)S(1)}, u32[]{:S(2)}, u32[]{:S(2)}) collective-permute-start(f32[16,128]{1,0:T(8,128)} %get-tuple-element.98), channel_id=1, source_target_pairs={{0,1},{1,2},{2,3},{3,0},{4,5},{5,6},{6,7},{7,4},{8,9},{9,10},{10,1... | collective-permute-start | bytes 24584 | tf_op jit(solution)/shard_map/ppermute | solution.py:280
  208.8 2.4 collective-permute-start.20
  214.0 3.2 collective-permute-start.23
  217.8 4.4 %fusion.18.refs_10_ = bf16[1024,1024]{1,0:T(8,128)(2,1)} fusion(s32[1024]{0:T(1024)S(1)} %get-tuple-element.128, s32[1024]{0:T(1024)S(1)} %get-tuple-element.129, s32[]{:T(128)} %axis_index.22, s32[1024]{0:T(1024)S(1)} %get-tuple-element.127, s32[1024]{0:T(1024)S(1)} %get-tuple-element.130, pred[1024]{0:T(1024)(128)(4,1)S(1)} %get-tuple-element.131, ...), kind=kLoop, calls=%fused_computation.58 | loop fusion | flops 63963136 | bytes 2115588 | tf_op jit(solution)/shard_map/convert_element_type | solution.py:264
  224.0 11.8 %collective-permute-done.26.refs_7_ = bf16[1792,128]{1,0:T(8,128)(2,1)S(1)} collective-permute-done((bf16[1792,128]{1,0:T(8,128)(2,1)}, bf16[1792,128]{1,0:T(8,128)(2,1)S(1)}, u32[]{:S(2)}, u32[]{:S(2)}) %collective-permute-start.26) | collective-permute-done | bytes 458784 | tf_op jit(solution)/shard_map/ppermute | solution.py:280
  235.8 6.0 %collective-permute-start.16 = (bf16[1792,128]{1,0:T(8,128)(2,1)}, bf16[1792,128]{1,0:T(8,128)(2,1)}, u32[]{:S(2)}, u32[]{:S(2)}) collective-permute-start(bf16[1792,128]{1,0:T(8,128)(2,1)} %bitcast.69), channel_id=1, source_target_pairs={{0,2},{1,3},{2,0},{3,1},{4,6},{5,7},{6,4},{7,5},{8,10},{9,11},{10,... | collective-permute-start | bytes 1376264 | tf_op jit(solution)/shard_map/ppermute | solution.py:280
  241.8 3.8 collective-permute-start.17
  245.5 26.6 %collective-permute-done.22.refs_2_ = bf16[1792,128]{1,0:T(8,128)(2,1)S(1)} collective-permute-done((bf16[1792,128]{1,0:T(8,128)(2,1)}, bf16[1792,128]{1,0:T(8,128)(2,1)S(1)}, u32[]{:S(2)}, u32[]{:S(2)}) %collective-permute-start.22) | collective-permute-done | bytes 458784 | tf_op jit(solution)/shard_map/ppermute | solution.py:280
  272.2 40.3 %collective-permute-start.9 = (bf16[1792,128]{1,0:T(8,128)(2,1)}, bf16[1792,128]{1,0:T(8,128)(2,1)}, u32[]{:S(2)}, u32[]{:S(2)}) collective-permute-start(bf16[1792,128]{1,0:T(8,128)(2,1)} %bitcast.65), channel_id=1, source_target_pairs={{0,1},{1,2},{2,3},{3,0},{4,5},{5,6},{6,7},{7,4},{8,9},{9,10},{10,1... | collective-permute-start | bytes 1376264 | tf_op jit(solution)/shard_map/ppermute | solution.py:280
  314.0 14.4 %quantize.2 = (bf16[1792,2048]{1,0:T(8,128)(2,1)}, f32[1792,256]{1,0:T(8,128)}, f32[16,128]{1,0:T(8,128)}) custom-call(s32[3]{0:T(128)} %pad_add_fusion.num_ref, bf16[1792,128]{1,0:T(8,128)(2,1)} %bitcast.45, bf16[1792,128]{1,0:T(8,128)(2,1)} %copy-done.3, bf16[1792,128]{1,0:T(8,128)(2,1)} %copy-done.4, bf16[1792,128]{1,0:T(8,128)(2,1)} %copy-done.5, ...), custom_call_target="tpu_custom_call" | custom-call | tf_op jit(solution)/shard_map/quantize/pallas_call | solution.py:222
  328.5 3.9 collective-permute-done.10.refs_2_
  332.3 14.4 %quantize.3 = (bf16[1792,2048]{1,0:T(8,128)(2,1)}, f32[1792,256]{1,0:T(8,128)}, f32[16,128]{1,0:T(8,128)}) custom-call(s32[3]{0:T(128)} %pad_add_fusion.num_ref, bf16[1792,128]{1,0:T(8,128)(2,1)} %bitcast.58, bf16[1792,128]{1,0:T(8,128)(2,1)} %collective-permute-done.9.refs_1_, ...), custom_call_target="tpu_custom_call", output_to_operand_aliasing={{0}: (12, {}), {1}: (13, {})} | custom-call | tf_op jit(solution)/shard_map/quantize/pallas_call | solution.py:222
  348.7 48.5 %psum.7 = f32[8]{0:T(128)S(1)} all-reduce(f32[8]{0:T(128)S(1)} %compare_select_fusion), channel_id=1, replica_groups=mesh['expert'=8,'row'=4] {'expert','row'}, use_global_device_ids=true, to_apply=%region_6.7 | all-reduce | flops 8 | bytes 64 | tf_op jit(solution)/shard_map/psum | solution.py:321
  (90 shorter events, 15.1 us)
Async XLA Ops:
  0.6 124.3 %copy-start.15 = (s32[1,2048]{1,0:T(1,128)S(1)}, s32[1,2048]{1,0:T(1,128)}, u32[]{:S(2)}) copy-start(s32[1,2048]{1,0:T(1,128)} %param.7) | copy-start | bytes 24580
  17.1 16.9 %collective-permute-start = (bf16[1792,128]{1,0:T(8,128)(2,1)}, bf16[1792,128]{1,0:T(8,128)(2,1)S(1)}, u32[]{:S(2)}, u32[]{:S(2)}) collective-permute-start(bf16[1792,128]{1,0:T(8,128)(2,1)} %get-tuple-element.63), channel_id=1, source_target_pairs={{0,1},{1,2},{2,3},{3,0},{4,5},{5,6},{6,7},{7,4},{8,9},{9,10},{10,1... | collective-permute-start | bytes 1376264 | tf_op jit(solution)/shard_map/ppermute | solution.py:280
  20.2 33.5 %collective-permute-start.1 = (bf16[1792,128]{1,0:T(8,128)(2,1)}, bf16[1792,128]{1,0:T(8,128)(2,1)S(1)}, u32[]{:S(2)}, u32[]{:S(2)}) collective-permute-start(bf16[1792,128]{1,0:T(8,128)(2,1)} %get-tuple-element.64), channel_id=1, source_target_pairs={{0,2},{1,3},{2,0},{3,1},{4,6},{5,7},{6,4},{7,5},{8,10},{9,11},{10,... | collective-permute-start | bytes 1376264 | tf_op jit(solution)/shard_map/ppermute | solution.py:280
  22.8 30.9 %collective-permute-start.2 = (bf16[1792,128]{1,0:T(8,128)(2,1)}, bf16[1792,128]{1,0:T(8,128)(2,1)S(1)}, u32[]{:S(2)}, u32[]{:S(2)}) collective-permute-start(bf16[1792,128]{1,0:T(8,128)(2,1)} %get-tuple-element.65), channel_id=1, source_target_pairs={{0,3},{1,0},{2,1},{3,2},{4,7},{5,4},{6,5},{7,6},{8,11},{9,8},{10,9... | collective-permute-start | bytes 1376264 | tf_op jit(solution)/shard_map/ppermute | solution.py:280
  24.2 61.4 %collective-permute-start.6 = (bf16[1792,128]{1,0:T(8,128)(2,1)}, bf16[1792,128]{1,0:T(8,128)(2,1)S(1)}, u32[]{:S(2)}, u32[]{:S(2)}) collective-permute-start(bf16[1792,128]{1,0:T(8,128)(2,1)} %get-tuple-element.73), channel_id=1, source_target_pairs={{0,1},{1,2},{2,3},{3,0},{4,5},{5,6},{6,7},{7,4},{8,9},{9,10},{10,1... | collective-permute-start | bytes 1376264 | tf_op jit(solution)/shard_map/ppermute | solution.py:280
  24.8 87.0 %collective-permute-start.7 = (bf16[1792,128]{1,0:T(8,128)(2,1)}, bf16[1792,128]{1,0:T(8,128)(2,1)S(1)}, u32[]{:S(2)}, u32[]{:S(2)}) collective-permute-start(bf16[1792,128]{1,0:T(8,128)(2,1)} %get-tuple-element.74), channel_id=1, source_target_pairs={{0,2},{1,3},{2,0},{3,1},{4,6},{5,7},{6,4},{7,5},{8,10},{9,11},{10,... | collective-permute-start | bytes 1376264 | tf_op jit(solution)/shard_map/ppermute | solution.py:280
  34.0 92.2 %copy-start.6 = (bf16[1792,128]{1,0:T(8,128)(2,1)}, bf16[1792,128]{1,0:T(8,128)(2,1)S(1)}, u32[]{:S(2)}) copy-start(bf16[1792,128]{1,0:T(8,128)(2,1)S(1)} %collective-permute-done) | copy-start | bytes 1376260
  34.0 77.8 %collective-permute-start.8 = (bf16[1792,128]{1,0:T(8,128)(2,1)}, bf16[1792,128]{1,0:T(8,128)(2,1)}, u32[]{:S(2)}, u32[]{:S(2)}) collective-permute-start(bf16[1792,128]{1,0:T(8,128)(2,1)} %get-tuple-element.75), channel_id=1, source_target_pairs={{0,3},{1,0},{2,1},{3,2},{4,7},{5,4},{6,5},{7,6},{8,11},{9,8},{10,9... | collective-permute-start | bytes 1376264 | tf_op jit(solution)/shard_map/ppermute | solution.py:280
  53.7 71.2 %collective-permute-start.3 = (bf16[1792,128]{1,0:T(8,128)(2,1)}, bf16[1792,128]{1,0:T(8,128)(2,1)S(1)}, u32[]{:S(2)}, u32[]{:S(2)}) collective-permute-start(bf16[1792,128]{1,0:T(8,128)(2,1)} %get-tuple-element.66), channel_id=1, source_target_pairs={{0,1},{1,2},{2,3},{3,0},{4,5},{5,6},{6,7},{7,4},{8,9},{9,10},{10,1... | collective-permute-start | bytes 1376264 | tf_op jit(solution)/shard_map/ppermute | solution.py:280
  83.7 67.4 %collective-permute-start.4 = (bf16[1792,128]{1,0:T(8,128)(2,1)}, bf16[1792,128]{1,0:T(8,128)(2,1)S(1)}, u32[]{:S(2)}, u32[]{:S(2)}) collective-permute-start(bf16[1792,128]{1,0:T(8,128)(2,1)} %get-tuple-element.67), channel_id=1, source_target_pairs={{0,2},{1,3},{2,0},{3,1},{4,6},{5,7},{6,4},{7,5},{8,10},{9,11},{10,... | collective-permute-start | bytes 1376264 | tf_op jit(solution)/shard_map/ppermute | solution.py:280
  85.6 75.4 %collective-permute-start.5 = (bf16[1792,128]{1,0:T(8,128)(2,1)}, bf16[1792,128]{1,0:T(8,128)(2,1)}, u32[]{:S(2)}, u32[]{:S(2)}) collective-permute-start(bf16[1792,128]{1,0:T(8,128)(2,1)} %get-tuple-element.68), channel_id=1, source_target_pairs={{0,3},{1,0},{2,1},{3,2},{4,7},{5,4},{6,5},{7,6},{8,11},{9,8},{10,9... | collective-permute-start | bytes 1376264 | tf_op jit(solution)/shard_map/ppermute | solution.py:280
  111.8 60.3 %collective-permute-start.12 = (bf16[1792,128]{1,0:T(8,128)(2,1)}, bf16[1792,128]{1,0:T(8,128)(2,1)}, u32[]{:S(2)}, u32[]{:S(2)}) collective-permute-start(bf16[1792,128]{1,0:T(8,128)(2,1)} %get-tuple-element.90), channel_id=1, source_target_pairs={{0,1},{1,2},{2,3},{3,0},{4,5},{5,6},{6,7},{7,4},{8,9},{9,10},{10,1... | collective-permute-start | bytes 1376264 | tf_op jit(solution)/shard_map/ppermute | solution.py:280
  122.3 68.3 %collective-permute-start.13 = (bf16[1792,128]{1,0:T(8,128)(2,1)}, bf16[1792,128]{1,0:T(8,128)(2,1)}, u32[]{:S(2)}, u32[]{:S(2)}) collective-permute-start(bf16[1792,128]{1,0:T(8,128)(2,1)} %get-tuple-element.91), channel_id=1, source_target_pairs={{0,2},{1,3},{2,0},{3,1},{4,6},{5,7},{6,4},{7,5},{8,10},{9,11},{10,... | collective-permute-start | bytes 1376264 | tf_op jit(solution)/shard_map/ppermute | solution.py:280
  124.9 65.7 %collective-permute-start.14 = (bf16[1792,128]{1,0:T(8,128)(2,1)}, bf16[1792,128]{1,0:T(8,128)(2,1)}, u32[]{:S(2)}, u32[]{:S(2)}) collective-permute-start(bf16[1792,128]{1,0:T(8,128)(2,1)} %get-tuple-element.92), channel_id=1, source_target_pairs={{0,3},{1,0},{2,1},{3,2},{4,7},{5,4},{6,5},{7,6},{8,11},{9,8},{10,9... | collective-permute-start | bytes 1376264 | tf_op jit(solution)/shard_map/ppermute | solution.py:280
  151.1 60.1 %collective-permute-start.24 = (bf16[1792,128]{1,0:T(8,128)(2,1)}, bf16[1792,128]{1,0:T(8,128)(2,1)S(1)}, u32[]{:S(2)}, u32[]{:S(2)}) collective-permute-start(bf16[1792,128]{1,0:T(8,128)(2,1)} %bitcast.72), channel_id=1, source_target_pairs={{0,1},{1,2},{2,3},{3,0},{4,5},{5,6},{6,7},{7,4},{8,9},{9,10},{10,1... | collective-permute-start | bytes 1376264 | tf_op jit(solution)/shard_map/ppermute | solution.py:280
  161.0 52.3 %collective-permute-start.25 = (bf16[1792,128]{1,0:T(8,128)(2,1)}, bf16[1792,128]{1,0:T(8,128)(2,1)S(1)}, u32[]{:S(2)}, u32[]{:S(2)}) collective-permute-start(bf16[1792,128]{1,0:T(8,128)(2,1)} %bitcast.71), channel_id=1, source_target_pairs={{0,2},{1,3},{2,0},{3,1},{4,6},{5,7},{6,4},{7,5},{8,10},{9,11},{10,... | collective-permute-start | bytes 1376264 | tf_op jit(solution)/shard_map/ppermute | solution.py:280
  198.4 14.9 %collective-permute-start.18 = (f32[16,128]{1,0:T(8,128)}, f32[16,128]{1,0:T(8,128)S(1)}, u32[]{:S(2)}, u32[]{:S(2)}) collective-permute-start(f32[16,128]{1,0:T(8,128)} %get-tuple-element.98), channel_id=1, source_target_pairs={{0,1},{1,2},{2,3},{3,0},{4,5},{5,6},{6,7},{7,4},{8,9},{9,10},{10,1... | collective-permute-start | bytes 24584 | tf_op jit(solution)/shard_map/ppermute | solution.py:280
  208.8 5.1 %collective-permute-start.19 = (f32[16,128]{1,0:T(8,128)}, f32[16,128]{1,0:T(8,128)S(1)}, u32[]{:S(2)}, u32[]{:S(2)}) collective-permute-start(f32[16,128]{1,0:T(8,128)} %get-tuple-element.98), channel_id=1, source_target_pairs={{0,2},{1,3},{2,0},{3,1},{4,6},{5,7},{6,4},{7,5},{8,10},{9,11},{10,... | collective-permute-start | bytes 24584 | tf_op jit(solution)/shard_map/ppermute | solution.py:280
  208.8 8.4 %collective-permute-start.20 = (f32[16,128]{1,0:T(8,128)}, f32[16,128]{1,0:T(8,128)S(1)}, u32[]{:S(2)}, u32[]{:S(2)}) collective-permute-start(f32[16,128]{1,0:T(8,128)} %get-tuple-element.98), channel_id=1, source_target_pairs={{0,3},{1,0},{2,1},{3,2},{4,7},{5,4},{6,5},{7,6},{8,11},{9,8},{10,9... | collective-permute-start | bytes 24584 | tf_op jit(solution)/shard_map/ppermute | solution.py:280
  211.2 102.8 %copy-start = (bf16[1792,128]{1,0:T(8,128)(2,1)}, bf16[1792,128]{1,0:T(8,128)(2,1)S(1)}, u32[]{:S(2)}) copy-start(bf16[1792,128]{1,0:T(8,128)(2,1)S(1)} %collective-permute-done.24.refs_5_) | copy-start | bytes 1376260
  211.2 24.6 %collective-permute-start.26 = (bf16[1792,128]{1,0:T(8,128)(2,1)}, bf16[1792,128]{1,0:T(8,128)(2,1)S(1)}, u32[]{:S(2)}, u32[]{:S(2)}) collective-permute-start(bf16[1792,128]{1,0:T(8,128)(2,1)} %bitcast.37), channel_id=1, source_target_pairs={{0,3},{1,0},{2,1},{3,2},{4,7},{5,4},{6,5},{7,6},{8,11},{9,8},{10,9... | collective-permute-start | bytes 1376264 | tf_op jit(solution)/shard_map/ppermute | solution.py:280
  213.3 100.7 %copy-start.1 = (bf16[1792,128]{1,0:T(8,128)(2,1)}, bf16[1792,128]{1,0:T(8,128)(2,1)S(1)}, u32[]{:S(2)}) copy-start(bf16[1792,128]{1,0:T(8,128)(2,1)S(1)} %collective-permute-done.25.refs_6_) | copy-start | bytes 1376260
  213.3 28.4 %collective-permute-start.21 = (bf16[1792,128]{1,0:T(8,128)(2,1)}, bf16[1792,128]{1,0:T(8,128)(2,1)S(1)}, u32[]{:S(2)}, u32[]{:S(2)}) collective-permute-start(bf16[1792,128]{1,0:T(8,128)(2,1)} %bitcast.31), channel_id=1, source_target_pairs={{0,1},{1,2},{2,3},{3,0},{4,5},{5,6},{6,7},{7,4},{8,9},{9,10},{10,1... | collective-permute-start | bytes 1376264 | tf_op jit(solution)/shard_map/ppermute | solution.py:280
  213.3 58.8 %collective-permute-start.22 = (bf16[1792,128]{1,0:T(8,128)(2,1)}, bf16[1792,128]{1,0:T(8,128)(2,1)S(1)}, u32[]{:S(2)}, u32[]{:S(2)}) collective-permute-start(bf16[1792,128]{1,0:T(8,128)(2,1)} %bitcast.32), channel_id=1, source_target_pairs={{0,2},{1,3},{2,0},{3,1},{4,6},{5,7},{6,4},{7,5},{8,10},{9,11},{10,... | collective-permute-start | bytes 1376264 | tf_op jit(solution)/shard_map/ppermute | solution.py:280
  214.0 58.2 %collective-permute-start.23 = (bf16[1792,128]{1,0:T(8,128)(2,1)}, bf16[1792,128]{1,0:T(8,128)(2,1)S(1)}, u32[]{:S(2)}, u32[]{:S(2)}) collective-permute-start(bf16[1792,128]{1,0:T(8,128)(2,1)} %bitcast.33), channel_id=1, source_target_pairs={{0,3},{1,0},{2,1},{3,2},{4,7},{5,4},{6,5},{7,6},{8,11},{9,8},{10,9... | collective-permute-start | bytes 1376264 | tf_op jit(solution)/shard_map/ppermute | solution.py:280
  217.2 55.0 %collective-permute-start.15 = (bf16[1792,128]{1,0:T(8,128)(2,1)}, bf16[1792,128]{1,0:T(8,128)(2,1)S(1)}, u32[]{:S(2)}, u32[]{:S(2)}) collective-permute-start(bf16[1792,128]{1,0:T(8,128)(2,1)} %bitcast.70), channel_id=1, source_target_pairs={{0,1},{1,2},{2,3},{3,0},{4,5},{5,6},{6,7},{7,4},{8,9},{9,10},{10,1... | collective-permute-start | bytes 1376264 | tf_op jit(solution)/shard_map/ppermute | solution.py:280
  235.8 78.2 %copy-start.2 = (bf16[1792,128]{1,0:T(8,128)(2,1)}, bf16[1792,128]{1,0:T(8,128)(2,1)S(1)}, u32[]{:S(2)}) copy-start(bf16[1792,128]{1,0:T(8,128)(2,1)S(1)} %collective-permute-done.26.refs_7_) | copy-start | bytes 1376260
  235.8 92.6 %collective-permute-start.16 = (bf16[1792,128]{1,0:T(8,128)(2,1)}, bf16[1792,128]{1,0:T(8,128)(2,1)}, u32[]{:S(2)}, u32[]{:S(2)}) collective-permute-start(bf16[1792,128]{1,0:T(8,128)(2,1)} %bitcast.69), channel_id=1, source_target_pairs={{0,2},{1,3},{2,0},{3,1},{4,6},{5,7},{6,4},{7,5},{8,10},{9,11},{10,... | collective-permute-start | bytes 1376264 | tf_op jit(solution)/shard_map/ppermute | solution.py:280
  241.8 86.7 %collective-permute-start.17 = (bf16[1792,128]{1,0:T(8,128)(2,1)}, bf16[1792,128]{1,0:T(8,128)(2,1)}, u32[]{:S(2)}, u32[]{:S(2)}) collective-permute-start(bf16[1792,128]{1,0:T(8,128)(2,1)} %bitcast.68), channel_id=1, source_target_pairs={{0,3},{1,0},{2,1},{3,2},{4,7},{5,4},{6,5},{7,6},{8,11},{9,8},{10,9... | collective-permute-start | bytes 1376264 | tf_op jit(solution)/shard_map/ppermute | solution.py:280
  272.1 60.2 %collective-permute-start.10 = (bf16[1792,128]{1,0:T(8,128)(2,1)}, bf16[1792,128]{1,0:T(8,128)(2,1)}, u32[]{:S(2)}, u32[]{:S(2)}) collective-permute-start(bf16[1792,128]{1,0:T(8,128)(2,1)} %bitcast.67), channel_id=1, source_target_pairs={{0,2},{1,3},{2,0},{3,1},{4,6},{5,7},{6,4},{7,5},{8,10},{9,11},{10,... | collective-permute-start | bytes 1376264 | tf_op jit(solution)/shard_map/ppermute | solution.py:280
  272.2 60.2 %collective-permute-start.11 = (bf16[1792,128]{1,0:T(8,128)(2,1)}, bf16[1792,128]{1,0:T(8,128)(2,1)}, u32[]{:S(2)}, u32[]{:S(2)}) collective-permute-start(bf16[1792,128]{1,0:T(8,128)(2,1)} %bitcast.66), channel_id=1, source_target_pairs={{0,3},{1,0},{2,1},{3,2},{4,7},{5,4},{6,5},{7,6},{8,11},{9,8},{10,9... | collective-permute-start | bytes 1376264 | tf_op jit(solution)/shard_map/ppermute | solution.py:280
  272.2 60.1 %collective-permute-start.9 = (bf16[1792,128]{1,0:T(8,128)(2,1)}, bf16[1792,128]{1,0:T(8,128)(2,1)}, u32[]{:S(2)}, u32[]{:S(2)}) collective-permute-start(bf16[1792,128]{1,0:T(8,128)(2,1)} %bitcast.65), channel_id=1, source_target_pairs={{0,1},{1,2},{2,3},{3,0},{4,5},{5,6},{6,7},{7,4},{8,9},{9,10},{10,1... | collective-permute-start | bytes 1376264 | tf_op jit(solution)/shard_map/ppermute | solution.py:280
  (12 other events, 477.0 us)
where the time goes:
time: 401 us; the launch traced here: 400 us
  starting transfers between devices  138 us (34%)
  waiting for transfers between devices  101 us (25%)
  Pallas kernels  76.8 us (19%)
  blocking collectives  48.5 us (12%)
  other arithmetic  29.2 us (7%)
    ppermute x27, starting transfers between devices, send(): lax.ppermute(x, 'row', [(k, (k + shift) % ring) for k in range(ring)])  138 us
    ppermute x27, waiting for transfers between devices, send(): lax.ppermute(x, 'row', [(k, (k + shift) % ring) for k in range(ring)])  101 us
    psum x1, blocking collectives, body(): every_error = lax.psum(slots, ('expert', 'row'))  48.5 us
    pallas_call x4, Pallas kernels, row_mix(): pl.pallas_call(kernel, out_shape=[jax.ShapeDtypeStruct((blocks, high, LOW...  31.5 us
    pallas_call x2, Pallas kernels, quantize(): pl.pallas_call(kernel, grid=(rows // tile,), in_specs=in_specs, out_specs...  28.8 us
    convert_element_type x1, other arithmetic, mixer_table(): return jnp.where(common & 1 == 0, table, -table).astype(jnp.bfloat16)  20.4 us
    pallas_call x1, Pallas kernels, column_transform(): pl.pallas_call(kernel, grid=(rows // tile,), in_specs=[pl.BlockSpec(memor...  16.5 us
  transfers between devices with their start and end apart: 27, of which 8 were waited for; matrix products, arithmetic and copies ran while one was open for 7% of the time, Pallas kernels for 11%

commit v1 on v0

--- a/solution.py
+++ b/solution.py
@@ -14,6 +14,7 @@
 CHUNKS = 4
 AHEAD = 2
 OCTET = 8
+TILE2 = 448
 
 
 def butterfly(parts):
@@ -28,16 +29,21 @@
     return parts
 
 
-def column_transform(weights, left_bits, right_bits, place, ring, chunks):
-    rows, width = weights.shape
-    tile = 2 * HB
+def even_tile(rows, most):
+    return max(t for t in range(HB, most + 1, HB // 2) if rows % t == 0)
+
+
+def column_transform(weights, left_bits, right_bits, place, ring, chunks, first, rows, tile, before):
+    all_rows, width = weights.shape
+    skip = first // tile
     count = width // INNER
     piece = width // (chunks * ring)
     root = 1.0 / math.sqrt(width)
 
     def kernel(place_ref, w_ref, left_ref, right_ref, *rest):
+        rest = rest[0 if before is None else len(before) :]
         outs = rest[: chunks * ring]
-        table, stage, left_col, natural = rest[chunks * ring :]
+        table, stage, left_col = rest[chunks * ring :]
         mine = place_ref[0]
 
         @pl.when(pl.program_id(0) == 0)
@@ -53,7 +59,8 @@
         for part in range(tile // HB):
             cols = slice(part * HB, (part + 1) * HB)
             signs = (2 * left_ref[:, cols] - 1).astype(jnp.float32) * root
-            left_col[cols, :] = jnp.sum(jnp.where(eye, signs, 0.0), axis=1, keepdims=True)
+            column = jnp.sum(jnp.where(eye, signs, 0.0), axis=1, keepdims=True)
+            left_col[cols, :] = jnp.broadcast_to(column, (HB, INNER))
         right = (2 * right_ref[...] - 1).astype(jnp.float32).astype(jnp.bfloat16)
         signed = [
             w_ref[:, hi * INNER : (hi + 1) * INNER] * right[:, hi * INNER : (hi + 1) * INNER]
@@ -62,96 +69,113 @@
         turned = jnp.dot(jnp.concatenate(signed, axis=0), table[...], preferred_element_type=jnp.float32)
         stage[...] = turned.reshape(count, tile, INNER)
 
-        def one(group, _):
-            start = pl.multiple_of(group * LOW, LOW)
-            left = left_col[pl.ds(start, LOW), :]
-            parts = butterfly([stage[hi, pl.ds(start, LOW), :] for hi in range(count)])
-            for hi, part in enumerate(parts):
-                natural[pl.ds(start, LOW), hi * INNER : (hi + 1) * INNER] = (part * left).astype(jnp.bfloat16)
-            return 0
-
-        lax.fori_loop(0, tile // LOW, one, 0)
-        for chunk in range(chunks):
-            for shift in range(ring):
-                dest = lax.rem(mine + shift, ring)
-                start = pl.multiple_of((chunk * ring + dest) * piece, 128)
-                outs[chunk * ring + shift][...] = natural[:, pl.ds(start, piece)]
+        def finish(here):
+            def one(group, _):
+                held = pl.ds(pl.multiple_of(group * LOW, LOW), LOW)
+                left = left_col[held, :]
+                parts = butterfly([stage[hi, held, :] for hi in range(count)])
+                for hi, part in enumerate(parts):
+                    part = (part * left).astype(jnp.bfloat16)
+                    for begin in range(0, INNER, 128):
+                        index, offset = divmod(hi * INNER + begin, piece)
+                        chunk, dest = divmod(index, ring)
+                        out = outs[chunk * ring + (dest - here) % ring]
+                        out[held, offset : offset + 128] = part[:, begin : begin + 128]
+                return 0
+
+            lax.fori_loop(0, tile // LOW, one, 0, unroll=2)
+
+        for here in range(ring):
+            pl.when(mine == here)(lambda here=here: finish(here))
 
     pieces = chunks * ring
+    operands = [place, weights, left_bits, right_bits]
+    in_specs = [
+        pl.BlockSpec(memory_space=pltpu.SMEM),
+        pl.BlockSpec((tile, width), lambda r: (r + skip, 0)),
+        pl.BlockSpec((1, tile), lambda r: (0, r + skip)),
+        pl.BlockSpec((1, width), lambda r: (0, 0)),
+    ]
+    aliases = {}
+    if before is not None:
+        aliases = {len(operands) + k: ring + k for k in range(len(before))}
+        operands += list(before)
+        in_specs += [pl.BlockSpec(memory_space=pl.ANY)] * len(before)
     outs = pl.pallas_call(
         kernel,
         grid=(rows // tile,),
-        in_specs=[
-            pl.BlockSpec(memory_space=pltpu.SMEM),
-            pl.BlockSpec((tile, width), lambda r: (r, 0)),
-            pl.BlockSpec((1, tile), lambda r: (0, r)),
-            pl.BlockSpec((1, width), lambda r: (0, 0)),
-        ],
-        out_specs=[pl.BlockSpec((tile, piece), lambda r: (r, 0))] * pieces,
-        out_shape=[jax.ShapeDtypeStruct((rows, piece), jnp.bfloat16)] * pieces,
+        in_specs=in_specs,
+        out_specs=[pl.BlockSpec((tile, piece), lambda r: (r, 0))] * ring
+        + [pl.BlockSpec((tile, piece), lambda r: (r + skip, 0))] * (pieces - ring),
+        out_shape=[jax.ShapeDtypeStruct((rows, piece), jnp.bfloat16)] * ring
+        + [jax.ShapeDtypeStruct((all_rows, piece), jnp.bfloat16)] * (pieces - ring),
         scratch_shapes=[
             pltpu.VMEM((INNER, INNER), jnp.bfloat16),
             pltpu.VMEM((count, tile, INNER), jnp.float32),
-            pltpu.VMEM((tile, 1), jnp.float32),
-            pltpu.VMEM((tile, width), jnp.bfloat16),
+            pltpu.VMEM((tile, INNER), jnp.float32),
         ],
+        input_output_aliases=aliases,
         name="column_transform",
-    )(place, weights, left_bits, right_bits)
-    return [outs[c * ring : (c + 1) * ring] for c in range(chunks)]
-
-
-def row_mix(pieces, mixer, own_groups, before):
+    )(*operands)
+    return outs[:ring], outs[ring:]
+
+
+def row_mix(pieces, mixer, own_groups, before, splits):
     ring = len(pieces)
-    rows, width = pieces[0].shape
-    blocks = rows // HB
+    width = pieces[0][0].shape[1]
+    blocks = sum(splits)
     high = HB // LOW
     band = blocks * LOW
     root = 1.0 / math.sqrt(HB)
+    flat = [p.reshape(p.shape[0] // HB, high, LOW, width) for piece in pieces for p in piece]
 
     def kernel(*refs):
-        ins, m_ref, group_ref, before_ref = refs[:ring], refs[ring], refs[ring + 1], refs[ring + 2]
-        outs, peak_ref, stage = refs[ring + 3 : 2 * ring + 3], refs[2 * ring + 3], refs[2 * ring + 4]
+        ins = refs[: len(flat)]
+        m_ref, group_ref, before_ref = refs[len(flat) : len(flat) + 3]
+        outs, peak_ref, stage = refs[len(flat) + 3 : -2], refs[-2], refs[-1]
         for hi in range(high):
-            rhs = jnp.concatenate([r[:, hi].reshape(band, width) for r in ins], axis=0)
+            rhs = jnp.concatenate([r[:, hi].reshape(r.shape[0] * LOW, width) for r in ins], axis=0)
             stage[hi] = jnp.dot(m_ref[...], rhs, preferred_element_type=jnp.float32)
 
         peak = jnp.zeros((LOW, width), jnp.float32)
-        for shift in range(ring):
+        for index, out in enumerate(outs):
+            shift, split = divmod(index, len(splits))
+            base = shift * band + sum(splits[:split]) * LOW
 
             def one(a, peak):
-                start = pl.multiple_of(shift * band + a * LOW, LOW)
+                start = pl.multiple_of(base + a * LOW, LOW)
                 parts = butterfly([stage[hi, pl.ds(start, LOW), :] for hi in range(high)])
                 for hi, part in enumerate(parts):
                     part = part * root
                     peak = jnp.maximum(peak, jnp.abs(part))
-                    outs[shift][a, hi] = part.astype(jnp.bfloat16)
+                    out[a, hi] = part.astype(jnp.bfloat16)
                 return peak
 
-            peak = lax.fori_loop(0, blocks, one, peak)
+            peak = lax.fori_loop(0, splits[split], one, peak)
         column_peak = jnp.max(peak, axis=0, keepdims=True)
         ids = lax.broadcasted_iota(jnp.int32, (GROUPS, width), 0)
         held = jnp.max(jnp.where(group_ref[...] == ids, column_peak, 0.0), axis=1, keepdims=True)
         peak_ref[...] = jnp.maximum(before_ref[...], held)
 
-    shaped = [p.reshape(blocks, high, LOW, width) for p in pieces]
     result = pl.pallas_call(
         kernel,
-        out_shape=[jax.ShapeDtypeStruct((blocks, high, LOW, width), jnp.bfloat16)] * ring
+        out_shape=[jax.ShapeDtypeStruct((n, high, LOW, width), jnp.bfloat16) for n in splits] * ring
         + [jax.ShapeDtypeStruct((GROUPS, 128), jnp.float32)],
         scratch_shapes=[pltpu.VMEM((high, ring * band, width), jnp.float32)],
         name="row_mix",
-    )(*shaped, mixer, own_groups, before)
-    return [y.reshape(rows, width) for y in result[:ring]], result[ring]
-
-
-def quantize(part_index, pieces, scale_row, scale_octet, spread, numbers, before):
+    )(*flat, mixer, own_groups, before)
+    mixed = [y.reshape(y.shape[0] * HB, width) for y in result[:-1]]
+    return [mixed[s * len(splits) : (s + 1) * len(splits)] for s in range(ring)], result[-1]
+
+
+def quantize(part_index, pieces, scale_row, scale_octet, spread, numbers, before, first_row, rows, all_rows, tile):
     each = len(pieces)
     ring = len(pieces[0])
-    rows, piece = pieces[0][0].shape
+    piece = pieces[0][0].shape[1]
+    skip = first_row // tile
     width = each * ring * piece
     lanes = width // OCTET
     parts_in_all = scale_row.shape[1] // width
-    tile = 2 * HB
     flat = [p for chunk in pieces for p in chunk]
 
     def kernel(num_ref, *refs):
@@ -194,11 +218,11 @@
             shifted = jnp.where(low_half != jnp.floor(low_half), far_squares + 2.0 * smallest, far_squares)
             error = jnp.minimum(whole, shifted)
             error_ref[held, :] = error
-            position = lax.broadcasted_iota(jnp.int32, (LOW, lanes), 0) + (first + step * tile + group * LOW)
+            position = lax.broadcasted_iota(jnp.int32, (LOW, lanes), 0) + (first + first_row + step * tile + group * LOW)
             weight = (position.astype(jnp.float32) + 0.5) * share + (1.0 / 3.0)
             return carry + error * weight
 
-        part = lax.fori_loop(0, tile // LOW, one, jnp.zeros((LOW, lanes), jnp.float32))
+        part = lax.fori_loop(0, tile // LOW, one, jnp.zeros((LOW, lanes), jnp.float32), unroll=2)
 
         @pl.when(step == 0)
         def _():
@@ -207,7 +231,8 @@
         sum_ref[...] += part
 
     in_specs = [pl.BlockSpec(memory_space=pltpu.SMEM)]
-    in_specs += [pl.BlockSpec((tile, piece), lambda r: (r, 0))] * (each * ring)
+    for p in flat:
+        in_specs.append(pl.BlockSpec((tile, piece), lambda r, o=skip * (p.shape[0] == all_rows): (r + o, 0)))
     in_specs += [
         pl.BlockSpec((1, width), lambda r: (0, part_index)),
         pl.BlockSpec((OCTET, lanes), lambda r: (0, part_index)),
@@ -224,13 +249,13 @@
         grid=(rows // tile,),
         in_specs=in_specs,
         out_specs=[
-            pl.BlockSpec((tile, width), lambda r: (r, part_index)),
-            pl.BlockSpec((tile, lanes), lambda r: (r, part_index)),
+            pl.BlockSpec((tile, width), lambda r: (r + skip, part_index)),
+            pl.BlockSpec((tile, lanes), lambda r: (r + skip, part_index)),
             pl.BlockSpec((LOW, lanes), lambda r: (0, 0)),
         ],
         out_shape=[
-            jax.ShapeDtypeStruct((rows, parts_in_all * width), jnp.bfloat16),
-            jax.ShapeDtypeStruct((rows, parts_in_all * lanes), jnp.float32),
+            jax.ShapeDtypeStruct((all_rows, parts_in_all * width), jnp.bfloat16),
+            jax.ShapeDtypeStruct((all_rows, parts_in_all * lanes), jnp.float32),
             jax.ShapeDtypeStruct((LOW, lanes), jnp.float32),
         ],
         scratch_shapes=[pltpu.VMEM((tile, width), jnp.float32)],
@@ -279,25 +304,45 @@
     def send(x, shift):
         return lax.ppermute(x, "row", [(k, (k + shift) % ring) for k in range(ring)])
 
-    outgoing = column_transform(weights[0], left_bits, right_bits, place, ring, chunks)
+    splits = (blocks_here // 2, blocks_here - blocks_here // 2)
+    halves = [n * HB for n in splits]
+    step_rows = math.gcd(*halves)
+    column_args = (weights[0], left_bits, right_bits, place, ring, chunks)
+    early, whole = column_transform(*column_args, 0, halves[0], step_rows, None)
+    late, whole = column_transform(*column_args, halves[0], halves[1], step_rows, whole)
+    outgoing = [[[early[s], late[s]] for s in range(ring)]]
+    outgoing += [[[whole[c * ring + s]] for s in range(ring)] for c in range(chunks - 1)]
     mixer = mixer_table(mine, ring, blocks_here)
     spread = spread_table(mine, ring, piece, unit)
     own_groups = [
         lax.dynamic_slice_in_dim(groups, (chunk * ring + mine) * piece, piece, 1) for chunk in range(chunks)
     ]
     received, returned = [], []
-    peak = jnp.zeros((GROUPS, 128), jnp.float32)
     for chunk in range(chunks):
         leaving = outgoing[chunk][1:]
         if chunk >= AHEAD:
             leaving, received[chunk - AHEAD] = lax.optimization_barrier((leaving, received[chunk - AHEAD]))
-        received.append([send(leaving[s - 1], s) for s in range(1, ring)])
-    peaks = None
+        arrived = [[] for _ in range(1, ring)]
+        for part in range(len(leaving[0])):
+            for s in range(1, ring):
+                arrived[s - 1].append(send(leaving[s - 1][part], s))
+        received.append(arrived)
+    peak = jnp.zeros((GROUPS, 128), jnp.float32)
     for chunk in range(chunks):
-        mixed, peak = row_mix([outgoing[chunk][0]] + received[chunk], mixer, own_groups[chunk], peak)
-        if chunk == chunks - 1:
+        last = chunk == chunks - 1
+        mixed, peak = row_mix(
+            [outgoing[chunk][0]] + received[chunk],
+            mixer,
+            own_groups[chunk],
+            peak,
+            splits if last else (blocks_here,),
+        )
+        if last:
             peaks = [peak] + [send(peak, s) for s in range(1, ring)]
-        returned.append([mixed[0]] + [send(mixed[s], s) for s in range(1, ring)])
+        back = []
+        for part in range(len(mixed[0])):
+            back.append([mixed[0][part]] + [send(mixed[s][part], s) for s in range(1, ring)])
+        returned.append(back)
 
     group_peak = jnp.max(jnp.stack(peaks), axis=(0, 2))
     group_peak = jnp.maximum(group_peak, 1.0)
@@ -307,19 +352,34 @@
 
     numbers = jnp.stack([mine, mine * local_rows, jnp.int32(local_rows) * ring])
     before, total = None, 0.0
+    fine = even_tile(step_rows, TILE2)
     for part_index in range(width // unit):
         held = returned[part_index * each : (part_index + 1) * each]
-        scaled, errors, part = quantize(
-            part_index, held, scale_row[None, :], scale_octet, spread, numbers, before
-        )
-        before = (scaled, errors)
-        total = total + part
+        ranges = [(0, local_rows)]
+        if len(held[-1]) > 1:
+            ranges = [(0, halves[0]), (halves[0], halves[1])]
+        for part, (first_row, count) in enumerate(ranges):
+            scaled, errors, share = quantize(
+                part_index,
+                [chunk[part % len(chunk)] for chunk in held],
+                scale_row[None, :],
+                scale_octet,
+                spread,
+                numbers,
+                before,
+                first_row,
+                count,
+                local_rows,
+                fine,
+            )
+            before = (scaled, errors)
+            total = total + share
     partial_error = jnp.sum(total) / (local_rows * ring * width // OCTET)
-    expert_count = experts * lax.axis_size("expert")
-    expert = lax.axis_index("expert")
-    slots = jnp.where(jnp.arange(expert_count) == expert, partial_error, 0.0)
-    every_error = lax.psum(slots, ("expert", "row"))
-    expert_error = lax.dynamic_slice_in_dim(every_error, expert, 1)
+    expert_count = lax.axis_size("expert")
+    copies = jnp.broadcast_to(partial_error, (expert_count * ring, 1))
+    every_error = lax.all_to_all(copies, ("expert", "row"), 0, 0)
+    every_error = jnp.sum(every_error.reshape(expert_count, ring), axis=1)
+    expert_error = lax.dynamic_slice_in_dim(every_error, lax.axis_index("expert"), 1)
     total_error = jnp.sum(every_error) / expert_count
     return (scaled[None], errors[None], (group_peak / 2.0)[None], expert_error, total_error)
 

time: 401 us -> 357 us (0.89)
  blocking collectives: 48.5 us -> 0 us
  waiting for transfers between devices: 101 us -> 121 us
  starting transfers between devices: 138 us -> 122 us
    psum x1 -> x0, blocking collectives: 48.5 us -> none  [body(): every_error = lax.psum(slots, ('expert', 'row'))]
    ppermute x27 -> x33, starting transfers between devices: 138 us -> 115 us  [send(): lax.ppermute(x, 'row', [(k, (k + shift) % ring) for k in range(ring)])]
    ppermute x27 -> x33, waiting for transfers between devices: 101 us -> 114 us  [send(): lax.ppermute(x, 'row', [(k, (k + shift) % ring) for k in range(ring)])]
    all_to_all x0 -> x1, waiting for transfers between devices: none -> 7.19 us  [body(): every_error = lax.all_to_all(copies, ('expert', 'row'), 0, 0)]
    all_to_all x0 -> x1, starting transfers between devices: none -> 7.1 us  [body(): every_error = lax.all_to_all(copies, ('expert', 'row'), 0, 0)]
    pallas_call x5 -> x6, Pallas kernels: 48 us -> 44.3 us  [the longest x4 31.6 us: row_mix(): pl.pallas_call(kernel, out_shape=[jax.ShapeDtypeStruct((n, high, LOW, wid...]
    pallas_call x2 -> x3, Pallas kernels: 28.8 us -> 29.7 us  [quantize(): pl.pallas_call(kernel, grid=(rows // tile,), in_specs=in_specs, out_specs...]
  transfers between devices with their start and end apart: 27 -> 34, of which waited for: 8 -> 12; matrix products, arithmetic and copies ran while one was open for 7% -> 8% of each run, Pallas kernels for 11% -> 17%
where the time goes in v1:
time: 357 us
  starting transfers between devices  122 us (34%)
  waiting for transfers between devices  121 us (34%)
  Pallas kernels  74 us (21%)
  other arithmetic  29.4 us (8%)
  local copies, waits for them, and re-layouts  6.47 us (2%)
    ppermute x33, starting transfers between devices, send(): lax.ppermute(x, 'row', [(k, (k + shift) % ring) for k in range(ring)])  115 us
    ppermute x33, waiting for transfers between devices, send(): lax.ppermute(x, 'row', [(k, (k + shift) % ring) for k in range(ring)])  114 us
    pallas_call x4, Pallas kernels, row_mix(): pl.pallas_call(kernel, out_shape=[jax.ShapeDtypeStruct((n, high, LOW, wid...  31.6 us
    pallas_call x3, Pallas kernels, quantize(): pl.pallas_call(kernel, grid=(rows // tile,), in_specs=in_specs, out_specs...  29.7 us
    convert_element_type x1, other arithmetic, mixer_table(): return jnp.where(common & 1 == 0, table, -table).astype(jnp.bfloat16)  20.4 us
    pallas_call x2, Pallas kernels, column_transform(): pl.pallas_call(kernel, grid=(rows // tile,), in_specs=in_specs, out_specs...  12.7 us
    all_to_all x1, waiting for transfers between devices, body(): every_error = lax.all_to_all(copies, ('expert', 'row'), 0, 0)  7.19 us
  transfers between devices with their start and end apart: 34, of which 12 were waited for; matrix products, arithmetic and copies ran while one was open for 8% of the time, Pallas kernels for 17%

profile of v1, /device:TPU:0, one launch (start us, length us, event | category | flops | bytes accessed | tf_op | source)
XLA Modules:
  0.0 356.8 jit_solution(3208128015294213738)
XLA Ops:
  0.6 6.4 %column_transform.2 = (bf16[896,128]{1,0:T(8,128)(2,1)}, bf16[896,128]{1,0:T(8,128)(2,1)}, bf16[896,128]{1,0:T(8,128)(2,1)}, bf16[896,128]{1,0:T(8,128)(2,1)}, b...) custom-call(s32[1]{0:T(128)} %bitcast.place_ref, ...), custom_call_target="tpu_custom_call" | custom-call | tf_op jit(solution)/shard_map/column_transform/pallas_call | solution.py:104
  14.0 6.3 %column_transform.3 = (bf16[896,128]{1,0:T(8,128)(2,1)}, bf16[896,128]{1,0:T(8,128)(2,1)}, bf16[896,128]{1,0:T(8,128)(2,1)}, bf16[896,128]{1,0:T(8,128)(2,1)}, b...) custom-call(s32[1]{0:T(128)} %bitcast.place_ref, ...), custom_call_target="tpu_custom_call", output_to_operand_aliasing={{4}: (4, {}), {5}: (5, {}), {6}: (6, {}), {7}: (7, {}), {8}... | custom-call | tf_op jit(solution)/shard_map/column_transform/pallas_call | solution.py:104
  24.2 4.5 %collective-permute-done.2 = bf16[896,128]{1,0:T(8,128)(2,1)S(1)} collective-permute-done((bf16[896,128]{1,0:T(8,128)(2,1)}, bf16[896,128]{1,0:T(8,128)(2,1)S(1)}, u32[]{:S(2)}, u32[]{:S(2)}) %collective-permute-start.2) | collective-permute-done | bytes 229408 | tf_op jit(solution)/shard_map/ppermute | solution.py:305
  28.7 13.3 %collective-permute-start.9 = (bf16[1792,128]{1,0:T(8,128)(2,1)}, bf16[1792,128]{1,0:T(8,128)(2,1)S(1)}, u32[]{:S(2)}, u32[]{:S(2)}) collective-permute-start(bf16[1792,128]{1,0:T(8,128)(2,1)} %get-tuple-element.114), channel_id=1, source_target_pairs={{0,1},{1,2},{2,3},{3,0},{4,5},{5,6},{6,7},{7,4},{8,9},{9,10},{10,1... | collective-permute-start | bytes 1376264 | tf_op jit(solution)/shard_map/ppermute | solution.py:305
  42.1 3.8 %collective-permute-start.10 = (bf16[1792,128]{1,0:T(8,128)(2,1)}, bf16[1792,128]{1,0:T(8,128)(2,1)S(1)}, u32[]{:S(2)}, u32[]{:S(2)}) collective-permute-start(bf16[1792,128]{1,0:T(8,128)(2,1)} %get-tuple-element.115), channel_id=1, source_target_pairs={{0,2},{1,3},{2,0},{3,1},{4,6},{5,7},{6,4},{7,5},{8,10},{9,11},{10,... | collective-permute-start | bytes 1376264 | tf_op jit(solution)/shard_map/ppermute | solution.py:305
  46.5 20.7 %collective-permute-done.3 = bf16[896,128]{1,0:T(8,128)(2,1)S(1)} collective-permute-done((bf16[896,128]{1,0:T(8,128)(2,1)}, bf16[896,128]{1,0:T(8,128)(2,1)S(1)}, u32[]{:S(2)}, u32[]{:S(2)}) %collective-permute-start.3) | collective-permute-done | bytes 229408 | tf_op jit(solution)/shard_map/ppermute | solution.py:305
  67.9 4.9 %collective-permute-start.6 = (bf16[1792,128]{1,0:T(8,128)(2,1)}, bf16[1792,128]{1,0:T(8,128)(2,1)S(1)}, u32[]{:S(2)}, u32[]{:S(2)}) collective-permute-start(bf16[1792,128]{1,0:T(8,128)(2,1)} %get-tuple-element.107), channel_id=1, source_target_pairs={{0,1},{1,2},{2,3},{3,0},{4,5},{5,6},{6,7},{7,4},{8,9},{9,10},{10,1... | collective-permute-start | bytes 1376264 | tf_op jit(solution)/shard_map/ppermute | solution.py:305
  76.2 25.5 %collective-permute-done.10 = bf16[1792,128]{1,0:T(8,128)(2,1)S(1)} collective-permute-done((bf16[1792,128]{1,0:T(8,128)(2,1)}, bf16[1792,128]{1,0:T(8,128)(2,1)S(1)}, u32[]{:S(2)}, u32[]{:S(2)}) %collective-permute-start.10) | collective-permute-done | bytes 458784 | tf_op jit(solution)/shard_map/ppermute | solution.py:305
  102.4 9.8 %collective-permute-start.15 = (bf16[1792,128]{1,0:T(8,128)(2,1)}, bf16[1792,128]{1,0:T(8,128)(2,1)S(1)}, u32[]{:S(2)}, u32[]{:S(2)}) collective-permute-start(bf16[1792,128]{1,0:T(8,128)(2,1)} %get-tuple-element.135), channel_id=1, source_target_pairs={{0,1},{1,2},{2,3},{3,0},{4,5},{5,6},{6,7},{7,4},{8,9},{9,10},{10,1... | collective-permute-start | bytes 1376264 | tf_op jit(solution)/shard_map/ppermute | solution.py:305
  115.5 20.4 %fusion.37.refs_8_.refs_4_ = bf16[896,896]{1,0:T(8,128)(2,1)} fusion(s32[896]{0:T(1024)S(1)} %get-tuple-element.174, s32[896]{0:T(1024)S(1)} %get-tuple-element.175, s32[896]{0:T(1024)S(1)} %get-tuple-element.173, s32[896]{0:T(1024)S(1)} %get-tuple-element.180, s32[]{:T(128)} %axis_index.22, s32[896]{0:T(1024)S(1)} %get-tuple-element.176, ...), kind=kLoop, calls=%fused_computation.77 | loop fusion | flops 69042176 | bytes 1629828 | tf_op jit(solution)/shard_map/convert_element_type | solution.py:280
  137.0 8.0 %row_mix.4 = (bf16[14,8,16,128]{3,2,1,0:T(8,128)(2,1)}, bf16[14,8,16,128]{3,2,1,0:T(8,128)(2,1)}, bf16[14,8,16,128]{3,2,1,0:T(8,128)(2,1)}, bf16[14,8,16,128]{3,2,1,0:T(8,128)(2,1)}, f32[16,128]{1,0:T(8,128)}) custom-call(bf16[7,8,16,128]{3,2,1,0:T(8,128)(2,1)} %bitcast.69, bf16[7,8,16,128]{3,2,1,0:T(8,128)(2,1)} %bitcast.73, ...), custom_call_target="tpu_custom_call" | custom-call | tf_op jit(solution)/shard_map/row_mix/pallas_call | solution.py:160
  145.1 6.0 %collective-permute-start.27 = (bf16[1792,128]{1,0:T(8,128)(2,1)}, bf16[1792,128]{1,0:T(8,128)(2,1)S(1)}, u32[]{:S(2)}, u32[]{:S(2)}) collective-permute-start(bf16[1792,128]{1,0:T(8,128)(2,1)} %bitcast.93), channel_id=1, source_target_pairs={{0,1},{1,2},{2,3},{3,0},{4,5},{5,6},{6,7},{7,4},{8,9},{9,10},{10,1... | collective-permute-start | bytes 1376264 | tf_op jit(solution)/shard_map/ppermute | solution.py:305
  151.1 7.8 %row_mix.5 = (bf16[14,8,16,128]{3,2,1,0:T(8,128)(2,1)}, bf16[14,8,16,128]{3,2,1,0:T(8,128)(2,1)}, bf16[14,8,16,128]{3,2,1,0:T(8,128)(2,1)}, bf16[14,8,16,128]{3,2,1,0:T(8,128)(2,1)}, f32[16,128]{1,0:T(8,128)}) custom-call(bf16[14,8,16,128]{3,2,1,0:T(8,128)(2,1)} %bitcast.56, bf16[14,8,16,128]{3,2,1,0:T(8,128)(2,1)} %bitcast.64, ...), custom_call_target="tpu_custom_call" | custom-call | tf_op jit(solution)/shard_map/row_mix/pallas_call | solution.py:160
  158.9 3.9 %collective-permute-start.28 = (bf16[1792,128]{1,0:T(8,128)(2,1)}, bf16[1792,128]{1,0:T(8,128)(2,1)S(1)}, u32[]{:S(2)}, u32[]{:S(2)}) collective-permute-start(bf16[1792,128]{1,0:T(8,128)(2,1)} %bitcast.90), channel_id=1, source_target_pairs={{0,2},{1,3},{2,0},{3,1},{4,6},{5,7},{6,4},{7,5},{8,10},{9,11},{10,... | collective-permute-start | bytes 1376264 | tf_op jit(solution)/shard_map/ppermute | solution.py:305
  163.8 16.5 %collective-permute-done.16 = bf16[1792,128]{1,0:T(8,128)(2,1)S(1)} collective-permute-done((bf16[1792,128]{1,0:T(8,128)(2,1)}, bf16[1792,128]{1,0:T(8,128)(2,1)S(1)}, u32[]{:S(2)}, u32[]{:S(2)}) %collective-permute-start.16) | collective-permute-done | bytes 458784 | tf_op jit(solution)/shard_map/ppermute | solution.py:305
  181.2 9.8 %collective-permute-start.30 = (bf16[1792,128]{1,0:T(8,128)(2,1)}, bf16[1792,128]{1,0:T(8,128)(2,1)S(1)}, u32[]{:S(2)}, u32[]{:S(2)}) collective-permute-start(bf16[1792,128]{1,0:T(8,128)(2,1)} %bitcast.92), channel_id=1, source_target_pairs={{0,1},{1,2},{2,3},{3,0},{4,5},{5,6},{6,7},{7,4},{8,9},{9,10},{10,1... | collective-permute-start | bytes 1376264 | tf_op jit(solution)/shard_map/ppermute | solution.py:305
  194.3 7.9 %row_mix.6 = (bf16[14,8,16,128]{3,2,1,0:T(8,128)(2,1)}, bf16[14,8,16,128]{3,2,1,0:T(8,128)(2,1)}, bf16[14,8,16,128]{3,2,1,0:T(8,128)(2,1)}, bf16[14,8,16,128]{3,2,1,0:T(8,128)(2,1)}, f32[16,128]{1,0:T(8,128)}) custom-call(bf16[14,8,16,128]{3,2,1,0:T(8,128)(2,1)} %bitcast.57, bf16[14,8,16,128]{3,2,1,0:T(8,128)(2,1)} %bitcast.61, ...), custom_call_target="tpu_custom_call" | custom-call | tf_op jit(solution)/shard_map/row_mix/pallas_call | solution.py:160
  202.2 7.8 %row_mix.7 = (bf16[7,8,16,128]{3,2,1,0:T(8,128)(2,1)}, bf16[7,8,16,128]{3,2,1,0:T(8,128)(2,1)}, bf16[7,8,16,128]{3,2,1,0:T(8,128)(2,1)}, bf16[7,8,16,128]{3,2,1,...) custom-call(bf16[14,8,16,128]{3,2,1,0:T(8,128)(2,1)} %bitcast.58, ...), custom_call_target="tpu_custom_call" | custom-call | tf_op jit(solution)/shard_map/row_mix/pallas_call | solution.py:160
  210.1 9.6 %collective-permute-done.28.refs_2_ = bf16[1792,128]{1,0:T(8,128)(2,1)S(1)} collective-permute-done((bf16[1792,128]{1,0:T(8,128)(2,1)}, bf16[1792,128]{1,0:T(8,128)(2,1)S(1)}, u32[]{:S(2)}, u32[]{:S(2)}) %collective-permute-start.28) | collective-permute-done | bytes 458784 | tf_op jit(solution)/shard_map/ppermute | solution.py:305
  222.6 8.5 %collective-permute-start.12 = (bf16[1792,128]{1,0:T(8,128)(2,1)}, bf16[1792,128]{1,0:T(8,128)(2,1)S(1)}, u32[]{:S(2)}, u32[]{:S(2)}) collective-permute-start(bf16[1792,128]{1,0:T(8,128)(2,1)} %bitcast.88), channel_id=1, source_target_pairs={{0,1},{1,2},{2,3},{3,0},{4,5},{5,6},{6,7},{7,4},{8,9},{9,10},{10,1... | collective-permute-start | bytes 1376264 | tf_op jit(solution)/shard_map/ppermute | solution.py:305
  231.1 10.2 %collective-permute-start.22 = (f32[16,128]{1,0:T(8,128)}, f32[16,128]{1,0:T(8,128)S(1)}, u32[]{:S(2)}, u32[]{:S(2)}) collective-permute-start(f32[16,128]{1,0:T(8,128)} %get-tuple-element.143), channel_id=1, source_target_pairs={{0,2},{1,3},{2,0},{3,1},{4,6},{5,7},{6,4},{7,5},{8,10},{9,11},{10,... | collective-permute-start | bytes 24584 | tf_op jit(solution)/shard_map/ppermute | solution.py:305
  241.3 8.1 %collective-permute-done.31.refs_6_ = bf16[1792,128]{1,0:T(8,128)(2,1)S(1)} collective-permute-done((bf16[1792,128]{1,0:T(8,128)(2,1)}, bf16[1792,128]{1,0:T(8,128)(2,1)S(1)}, u32[]{:S(2)}, u32[]{:S(2)}) %collective-permute-start.31) | collective-permute-done | bytes 458784 | tf_op jit(solution)/shard_map/ppermute | solution.py:305
  250.1 4.4 %fusion.18.refs_10_ = bf16[1024,1024]{1,0:T(8,128)(2,1)} fusion(s32[1024]{0:T(1024)S(1)} %get-tuple-element.182, s32[1024]{0:T(1024)S(1)} %get-tuple-element.183, s32[]{:T(128)} %axis_index.22, s32[1024]{0:T(1024)S(1)} %get-tuple-element.181, s32[1024]{0:T(1024)S(1)} %get-tuple-element.184, pred[1024]{0:T(1024)(128)(4,1)S(1)} %get-tuple-element.185, ...), kind=kLoop, calls=%fused_computation.58 | loop fusion | flops 63963136 | bytes 2115588 | tf_op jit(solution)/shard_map/convert_element_type | solution.py:289
  254.5 15.0 %collective-permute-done.22 = f32[16,128]{1,0:T(8,128)S(1)} collective-permute-done((f32[16,128]{1,0:T(8,128)}, f32[16,128]{1,0:T(8,128)S(1)}, u32[]{:S(2)}, u32[]{:S(2)}) %collective-permute-start.22) | collective-permute-done | bytes 8224 | tf_op jit(solution)/shard_map/ppermute | solution.py:305
  277.0 3.7 %collective-permute-done.25.refs_6_ = bf16[896,128]{1,0:T(8,128)(2,1)} collective-permute-done((bf16[896,128]{1,0:T(8,128)(2,1)}, bf16[896,128]{1,0:T(8,128)(2,1)}, u32[]{:S(2)}, u32[]{:S(2)}) %collective-permute-start.25) | collective-permute-done | bytes 229408 | tf_op jit(solution)/shard_map/ppermute | solution.py:305
  282.9 10.5 %collective-permute-start.19 = (bf16[896,128]{1,0:T(8,128)(2,1)}, bf16[896,128]{1,0:T(8,128)(2,1)}, u32[]{:S(2)}, u32[]{:S(2)}) collective-permute-start(bf16[896,128]{1,0:T(8,128)(2,1)} %bitcast.95), channel_id=1, source_target_pairs={{0,2},{1,3},{2,0},{3,1},{4,6},{5,7},{6,4},{7,5},{8,10},{9,11},{10,... | collective-permute-start | bytes 688136 | tf_op jit(solution)/shard_map/ppermute | solution.py:305
  297.8 13.3 %quantize.3 = (bf16[1792,2048]{1,0:T(8,128)(2,1)}, f32[1792,256]{1,0:T(8,128)}, f32[16,128]{1,0:T(8,128)}) custom-call(s32[3]{0:T(128)} %pad_add_fusion.num_ref, bf16[1792,128]{1,0:T(8,128)(2,1)} %bitcast.59, bf16[1792,128]{1,0:T(8,128)(2,1)} %copy-done.3, bf16[1792,128]{1,0:T(8,128)(2,1)} %copy-done.4, bf16[1792,128]{1,0:T(8,128)(2,1)} %copy-done.5, ...), custom_call_target="tpu_custom_call" | custom-call | tf_op jit(solution)/shard_map/quantize/pallas_call | solution.py:247
  314.5 8.2 %quantize.4 = (bf16[1792,2048]{1,0:T(8,128)(2,1)}, f32[1792,256]{1,0:T(8,128)}, f32[16,128]{1,0:T(8,128)}) custom-call(s32[3]{0:T(128)} %pad_add_fusion.num_ref, bf16[1792,128]{1,0:T(8,128)(2,1)} %bitcast.54, bf16[1792,128]{1,0:T(8,128)(2,1)} %copy-done, bf16[1792,128]{1,0:T(8,128)(2,1)} %copy-done.1, ...), custom_call_target="tpu_custom_call", output_to_operand_aliasing={{0}: (12, {}), {1}: (13, {})} | custom-call | tf_op jit(solution)/shard_map/quantize/pallas_call | solution.py:247
  322.7 5.7 %collective-permute-done.19.refs_6_ = bf16[896,128]{1,0:T(8,128)(2,1)} collective-permute-done((bf16[896,128]{1,0:T(8,128)(2,1)}, bf16[896,128]{1,0:T(8,128)(2,1)}, u32[]{:S(2)}, u32[]{:S(2)}) %collective-permute-start.19) | collective-permute-done | bytes 229408 | tf_op jit(solution)/shard_map/ppermute | solution.py:305
  328.4 8.2 %quantize.5 = (bf16[1792,2048]{1,0:T(8,128)(2,1)}, f32[1792,256]{1,0:T(8,128)}, f32[16,128]{1,0:T(8,128)}) custom-call(s32[3]{0:T(128)} %pad_add_fusion.num_ref, bf16[1792,128]{1,0:T(8,128)(2,1)} %bitcast.55, bf16[1792,128]{1,0:T(8,128)(2,1)} %copy-done, bf16[1792,128]{1,0:T(8,128)(2,1)} %copy-done.1, ...), custom_call_target="tpu_custom_call", output_to_operand_aliasing={{0}: (12, {}), {1}: (13, {})} | custom-call | tf_op jit(solution)/shard_map/quantize/pallas_call | solution.py:247
  339.2 7.1 %all-to-all-start = ((f32[32,1,1]{2,1,0:T(1,128)}), f32[32,1,1]{2,1,0:T(1,128)S(1)}, u32[]{:S(2)}, u32[]{:S(2)}) async-start(f32[32,1,1]{2,1,0:T(1,128)} %broadcast_in_dim.38), calls=%async_computation | async-start | bytes 32768 | tf_op jit(solution)/shard_map/all_to_all | solution.py:380
  346.3 7.2 %all-to-all-done = f32[32,1,1]{2,1,0:T(1,128)S(1)} async-done(((f32[32,1,1]{2,1,0:T(1,128)}), f32[32,1,1]{2,1,0:T(1,128)S(1)}, u32[]{:S(2)}, u32[]{:S(2)}) %all-to-all-start) | async-done | bytes 160 | tf_op jit(solution)/shard_map/all_to_all | solution.py:380
  (129 shorter events, 50.4 us)
Async XLA Ops:
  7.0 14.3 %collective-permute-start = (bf16[896,128]{1,0:T(8,128)(2,1)}, bf16[896,128]{1,0:T(8,128)(2,1)S(1)}, u32[]{:S(2)}, u32[]{:S(2)}) collective-permute-start(bf16[896,128]{1,0:T(8,128)(2,1)} %get-tuple-element.101), channel_id=1, source_target_pairs={{0,1},{1,2},{2,3},{3,0},{4,5},{5,6},{6,7},{7,4},{8,9},{9,10},{10,1... | collective-permute-start | bytes 688136 | tf_op jit(solution)/shard_map/ppermute | solution.py:305
  10.0 18.7 %collective-permute-start.2 = (bf16[896,128]{1,0:T(8,128)(2,1)}, bf16[896,128]{1,0:T(8,128)(2,1)S(1)}, u32[]{:S(2)}, u32[]{:S(2)}) collective-permute-start(bf16[896,128]{1,0:T(8,128)(2,1)} %get-tuple-element.103), channel_id=1, source_target_pairs={{0,2},{1,3},{2,0},{3,1},{4,6},{5,7},{6,4},{7,5},{8,10},{9,11},{10,... | collective-permute-start | bytes 688136 | tf_op jit(solution)/shard_map/ppermute | solution.py:305
  12.6 29.5 %collective-permute-start.4 = (bf16[896,128]{1,0:T(8,128)(2,1)}, bf16[896,128]{1,0:T(8,128)(2,1)S(1)}, u32[]{:S(2)}, u32[]{:S(2)}) collective-permute-start(bf16[896,128]{1,0:T(8,128)(2,1)} %get-tuple-element.105), channel_id=1, source_target_pairs={{0,3},{1,0},{2,1},{3,2},{4,7},{5,4},{6,5},{7,6},{8,11},{9,8},{10,9... | collective-permute-start | bytes 688136 | tf_op jit(solution)/shard_map/ppermute | solution.py:305
  20.3 25.5 %collective-permute-start.1 = (bf16[896,128]{1,0:T(8,128)(2,1)}, bf16[896,128]{1,0:T(8,128)(2,1)S(1)}, u32[]{:S(2)}, u32[]{:S(2)}) collective-permute-start(bf16[896,128]{1,0:T(8,128)(2,1)} %get-tuple-element.102), channel_id=1, source_target_pairs={{0,1},{1,2},{2,3},{3,0},{4,5},{5,6},{6,7},{7,4},{8,9},{9,10},{10,1... | collective-permute-start | bytes 688136 | tf_op jit(solution)/shard_map/ppermute | solution.py:305
  21.0 46.3 %collective-permute-start.3 = (bf16[896,128]{1,0:T(8,128)(2,1)}, bf16[896,128]{1,0:T(8,128)(2,1)S(1)}, u32[]{:S(2)}, u32[]{:S(2)}) collective-permute-start(bf16[896,128]{1,0:T(8,128)(2,1)} %get-tuple-element.104), channel_id=1, source_target_pairs={{0,2},{1,3},{2,0},{3,1},{4,6},{5,7},{6,4},{7,5},{8,10},{9,11},{10,... | collective-permute-start | bytes 688136 | tf_op jit(solution)/shard_map/ppermute | solution.py:305
  21.3 45.9 %collective-permute-start.5 = (bf16[896,128]{1,0:T(8,128)(2,1)}, bf16[896,128]{1,0:T(8,128)(2,1)S(1)}, u32[]{:S(2)}, u32[]{:S(2)}) collective-permute-start(bf16[896,128]{1,0:T(8,128)(2,1)} %get-tuple-element.106), channel_id=1, source_target_pairs={{0,3},{1,0},{2,1},{3,2},{4,7},{5,4},{6,5},{7,6},{8,11},{9,8},{10,9... | collective-permute-start | bytes 688136 | tf_op jit(solution)/shard_map/ppermute | solution.py:305
  28.7 47.4 %collective-permute-start.9 = (bf16[1792,128]{1,0:T(8,128)(2,1)}, bf16[1792,128]{1,0:T(8,128)(2,1)S(1)}, u32[]{:S(2)}, u32[]{:S(2)}) collective-permute-start(bf16[1792,128]{1,0:T(8,128)(2,1)} %get-tuple-element.114), channel_id=1, source_target_pairs={{0,1},{1,2},{2,3},{3,0},{4,5},{5,6},{6,7},{7,4},{8,9},{9,10},{10,1... | collective-permute-start | bytes 1376264 | tf_op jit(solution)/shard_map/ppermute | solution.py:305
  42.1 59.6 %collective-permute-start.10 = (bf16[1792,128]{1,0:T(8,128)(2,1)}, bf16[1792,128]{1,0:T(8,128)(2,1)S(1)}, u32[]{:S(2)}, u32[]{:S(2)}) collective-permute-start(bf16[1792,128]{1,0:T(8,128)(2,1)} %get-tuple-element.115), channel_id=1, source_target_pairs={{0,2},{1,3},{2,0},{3,1},{4,6},{5,7},{6,4},{7,5},{8,10},{9,11},{10,... | collective-permute-start | bytes 1376264 | tf_op jit(solution)/shard_map/ppermute | solution.py:305
  45.9 55.8 %collective-permute-start.11 = (bf16[1792,128]{1,0:T(8,128)(2,1)}, bf16[1792,128]{1,0:T(8,128)(2,1)S(1)}, u32[]{:S(2)}, u32[]{:S(2)}) collective-permute-start(bf16[1792,128]{1,0:T(8,128)(2,1)} %get-tuple-element.116), channel_id=1, source_target_pairs={{0,3},{1,0},{2,1},{3,2},{4,7},{5,4},{6,5},{7,6},{8,11},{9,8},{10,9... | collective-permute-start | bytes 1376264 | tf_op jit(solution)/shard_map/ppermute | solution.py:305
  67.9 47.6 %collective-permute-start.6 = (bf16[1792,128]{1,0:T(8,128)(2,1)}, bf16[1792,128]{1,0:T(8,128)(2,1)S(1)}, u32[]{:S(2)}, u32[]{:S(2)}) collective-permute-start(bf16[1792,128]{1,0:T(8,128)(2,1)} %get-tuple-element.107), channel_id=1, source_target_pairs={{0,1},{1,2},{2,3},{3,0},{4,5},{5,6},{6,7},{7,4},{8,9},{9,10},{10,1... | collective-permute-start | bytes 1376264 | tf_op jit(solution)/shard_map/ppermute | solution.py:305
  72.8 72.3 %collective-permute-start.7 = (bf16[1792,128]{1,0:T(8,128)(2,1)}, bf16[1792,128]{1,0:T(8,128)(2,1)S(1)}, u32[]{:S(2)}, u32[]{:S(2)}) collective-permute-start(bf16[1792,128]{1,0:T(8,128)(2,1)} %get-tuple-element.108), channel_id=1, source_target_pairs={{0,2},{1,3},{2,0},{3,1},{4,6},{5,7},{6,4},{7,5},{8,10},{9,11},{10,... | collective-permute-start | bytes 1376264 | tf_op jit(solution)/shard_map/ppermute | solution.py:305
  76.1 82.8 %collective-permute-start.8 = (bf16[1792,128]{1,0:T(8,128)(2,1)}, bf16[1792,128]{1,0:T(8,128)(2,1)S(1)}, u32[]{:S(2)}, u32[]{:S(2)}) collective-permute-start(bf16[1792,128]{1,0:T(8,128)(2,1)} %get-tuple-element.109), channel_id=1, source_target_pairs={{0,3},{1,0},{2,1},{3,2},{4,7},{5,4},{6,5},{7,6},{8,11},{9,8},{10,9... | collective-permute-start | bytes 1376264 | tf_op jit(solution)/shard_map/ppermute | solution.py:305
  102.4 60.4 %collective-permute-start.15 = (bf16[1792,128]{1,0:T(8,128)(2,1)}, bf16[1792,128]{1,0:T(8,128)(2,1)S(1)}, u32[]{:S(2)}, u32[]{:S(2)}) collective-permute-start(bf16[1792,128]{1,0:T(8,128)(2,1)} %get-tuple-element.135), channel_id=1, source_target_pairs={{0,1},{1,2},{2,3},{3,0},{4,5},{5,6},{6,7},{7,4},{8,9},{9,10},{10,1... | collective-permute-start | bytes 1376264 | tf_op jit(solution)/shard_map/ppermute | solution.py:305
  112.2 68.2 %collective-permute-start.16 = (bf16[1792,128]{1,0:T(8,128)(2,1)}, bf16[1792,128]{1,0:T(8,128)(2,1)S(1)}, u32[]{:S(2)}, u32[]{:S(2)}) collective-permute-start(bf16[1792,128]{1,0:T(8,128)(2,1)} %get-tuple-element.136), channel_id=1, source_target_pairs={{0,2},{1,3},{2,0},{3,1},{4,6},{5,7},{6,4},{7,5},{8,10},{9,11},{10,... | collective-permute-start | bytes 1376264 | tf_op jit(solution)/shard_map/ppermute | solution.py:305
  115.5 75.5 %collective-permute-start.17 = (bf16[1792,128]{1,0:T(8,128)(2,1)}, bf16[1792,128]{1,0:T(8,128)(2,1)}, u32[]{:S(2)}, u32[]{:S(2)}) collective-permute-start(bf16[1792,128]{1,0:T(8,128)(2,1)} %get-tuple-element.137), channel_id=1, source_target_pairs={{0,3},{1,0},{2,1},{3,2},{4,7},{5,4},{6,5},{7,6},{8,11},{9,8},{10,9... | collective-permute-start | bytes 1376264 | tf_op jit(solution)/shard_map/ppermute | solution.py:305
  145.1 64.9 %collective-permute-start.27 = (bf16[1792,128]{1,0:T(8,128)(2,1)}, bf16[1792,128]{1,0:T(8,128)(2,1)S(1)}, u32[]{:S(2)}, u32[]{:S(2)}) collective-permute-start(bf16[1792,128]{1,0:T(8,128)(2,1)} %bitcast.93), channel_id=1, source_target_pairs={{0,1},{1,2},{2,3},{3,0},{4,5},{5,6},{6,7},{7,4},{8,9},{9,10},{10,1... | collective-permute-start | bytes 1376264 | tf_op jit(solution)/shard_map/ppermute | solution.py:305
  158.9 60.8 %collective-permute-start.28 = (bf16[1792,128]{1,0:T(8,128)(2,1)}, bf16[1792,128]{1,0:T(8,128)(2,1)S(1)}, u32[]{:S(2)}, u32[]{:S(2)}) collective-permute-start(bf16[1792,128]{1,0:T(8,128)(2,1)} %bitcast.90), channel_id=1, source_target_pairs={{0,2},{1,3},{2,0},{3,1},{4,6},{5,7},{6,4},{7,5},{8,10},{9,11},{10,... | collective-permute-start | bytes 1376264 | tf_op jit(solution)/shard_map/ppermute | solution.py:305
  162.8 59.7 %collective-permute-start.29 = (bf16[1792,128]{1,0:T(8,128)(2,1)}, bf16[1792,128]{1,0:T(8,128)(2,1)S(1)}, u32[]{:S(2)}, u32[]{:S(2)}) collective-permute-start(bf16[1792,128]{1,0:T(8,128)(2,1)} %bitcast.89), channel_id=1, source_target_pairs={{0,3},{1,0},{2,1},{3,2},{4,7},{5,4},{6,5},{7,6},{8,11},{9,8},{10,9... | collective-permute-start | bytes 1376264 | tf_op jit(solution)/shard_map/ppermute | solution.py:305
  181.2 49.9 %collective-permute-start.30 = (bf16[1792,128]{1,0:T(8,128)(2,1)}, bf16[1792,128]{1,0:T(8,128)(2,1)S(1)}, u32[]{:S(2)}, u32[]{:S(2)}) collective-permute-start(bf16[1792,128]{1,0:T(8,128)(2,1)} %bitcast.92), channel_id=1, source_target_pairs={{0,1},{1,2},{2,3},{3,0},{4,5},{5,6},{6,7},{7,4},{8,9},{9,10},{10,1... | collective-permute-start | bytes 1376264 | tf_op jit(solution)/shard_map/ppermute | solution.py:305
  191.0 58.4 %collective-permute-start.31 = (bf16[1792,128]{1,0:T(8,128)(2,1)}, bf16[1792,128]{1,0:T(8,128)(2,1)S(1)}, u32[]{:S(2)}, u32[]{:S(2)}) collective-permute-start(bf16[1792,128]{1,0:T(8,128)(2,1)} %bitcast.91), channel_id=1, source_target_pairs={{0,2},{1,3},{2,0},{3,1},{4,6},{5,7},{6,4},{7,5},{8,10},{9,11},{10,... | collective-permute-start | bytes 1376264 | tf_op jit(solution)/shard_map/ppermute | solution.py:305
  210.0 39.5 %collective-permute-start.23 = (f32[16,128]{1,0:T(8,128)}, f32[16,128]{1,0:T(8,128)S(1)}, u32[]{:S(2)}, u32[]{:S(2)}) collective-permute-start(f32[16,128]{1,0:T(8,128)} %get-tuple-element.143), channel_id=1, source_target_pairs={{0,3},{1,0},{2,1},{3,2},{4,7},{5,4},{6,5},{7,6},{8,11},{9,8},{10,9... | collective-permute-start | bytes 24584 | tf_op jit(solution)/shard_map/ppermute | solution.py:305
  219.7 51.6 %collective-permute-start.32 = (bf16[1792,128]{1,0:T(8,128)(2,1)}, bf16[1792,128]{1,0:T(8,128)(2,1)S(1)}, u32[]{:S(2)}, u32[]{:S(2)}) collective-permute-start(bf16[1792,128]{1,0:T(8,128)(2,1)} %bitcast.45), channel_id=1, source_target_pairs={{0,3},{1,0},{2,1},{3,2},{4,7},{5,4},{6,5},{7,6},{8,11},{9,8},{10,9... | collective-permute-start | bytes 1376264 | tf_op jit(solution)/shard_map/ppermute | solution.py:305
  222.6 70.9 %collective-permute-start.12 = (bf16[1792,128]{1,0:T(8,128)(2,1)}, bf16[1792,128]{1,0:T(8,128)(2,1)S(1)}, u32[]{:S(2)}, u32[]{:S(2)}) collective-permute-start(bf16[1792,128]{1,0:T(8,128)(2,1)} %bitcast.88), channel_id=1, source_target_pairs={{0,1},{1,2},{2,3},{3,0},{4,5},{5,6},{6,7},{7,4},{8,9},{9,10},{10,1... | collective-permute-start | bytes 1376264 | tf_op jit(solution)/shard_map/ppermute | solution.py:305
  231.1 38.4 %collective-permute-start.22 = (f32[16,128]{1,0:T(8,128)}, f32[16,128]{1,0:T(8,128)S(1)}, u32[]{:S(2)}, u32[]{:S(2)}) collective-permute-start(f32[16,128]{1,0:T(8,128)} %get-tuple-element.143), channel_id=1, source_target_pairs={{0,2},{1,3},{2,0},{3,1},{4,6},{5,7},{6,4},{7,5},{8,10},{9,11},{10,... | collective-permute-start | bytes 24584 | tf_op jit(solution)/shard_map/ppermute | solution.py:305
  249.4 20.1 %collective-permute-start.21 = (f32[16,128]{1,0:T(8,128)}, f32[16,128]{1,0:T(8,128)S(1)}, u32[]{:S(2)}, u32[]{:S(2)}) collective-permute-start(f32[16,128]{1,0:T(8,128)} %get-tuple-element.143), channel_id=1, source_target_pairs={{0,1},{1,2},{2,3},{3,0},{4,5},{5,6},{6,7},{7,4},{8,9},{9,10},{10,1... | collective-permute-start | bytes 24584 | tf_op jit(solution)/shard_map/ppermute | solution.py:305
  249.6 24.8 %collective-permute-start.24 = (bf16[896,128]{1,0:T(8,128)(2,1)}, bf16[896,128]{1,0:T(8,128)(2,1)S(1)}, u32[]{:S(2)}, u32[]{:S(2)}) collective-permute-start(bf16[896,128]{1,0:T(8,128)(2,1)} %bitcast.99), channel_id=1, source_target_pairs={{0,1},{1,2},{2,3},{3,0},{4,5},{5,6},{6,7},{7,4},{8,9},{9,10},{10,1... | collective-permute-start | bytes 688136 | tf_op jit(solution)/shard_map/ppermute | solution.py:305
  271.3 42.2 %collective-permute-start.13 = (bf16[1792,128]{1,0:T(8,128)(2,1)}, bf16[1792,128]{1,0:T(8,128)(2,1)S(1)}, u32[]{:S(2)}, u32[]{:S(2)}) collective-permute-start(bf16[1792,128]{1,0:T(8,128)(2,1)} %bitcast.87), channel_id=1, source_target_pairs={{0,2},{1,3},{2,0},{3,1},{4,6},{5,7},{6,4},{7,5},{8,10},{9,11},{10,... | collective-permute-start | bytes 1376264 | tf_op jit(solution)/shard_map/ppermute | solution.py:305
  274.3 39.2 %collective-permute-start.14 = (bf16[1792,128]{1,0:T(8,128)(2,1)}, bf16[1792,128]{1,0:T(8,128)(2,1)S(1)}, u32[]{:S(2)}, u32[]{:S(2)}) collective-permute-start(bf16[1792,128]{1,0:T(8,128)(2,1)} %bitcast.86), channel_id=1, source_target_pairs={{0,3},{1,0},{2,1},{3,2},{4,7},{5,4},{6,5},{7,6},{8,11},{9,8},{10,9... | collective-permute-start | bytes 1376264 | tf_op jit(solution)/shard_map/ppermute | solution.py:305
  280.7 41.9 %collective-permute-start.18 = (bf16[896,128]{1,0:T(8,128)(2,1)}, bf16[896,128]{1,0:T(8,128)(2,1)}, u32[]{:S(2)}, u32[]{:S(2)}) collective-permute-start(bf16[896,128]{1,0:T(8,128)(2,1)} %bitcast.96), channel_id=1, source_target_pairs={{0,1},{1,2},{2,3},{3,0},{4,5},{5,6},{6,7},{7,4},{8,9},{9,10},{10,1... | collective-permute-start | bytes 688136 | tf_op jit(solution)/shard_map/ppermute | solution.py:305
  282.9 45.4 %collective-permute-start.19 = (bf16[896,128]{1,0:T(8,128)(2,1)}, bf16[896,128]{1,0:T(8,128)(2,1)}, u32[]{:S(2)}, u32[]{:S(2)}) collective-permute-start(bf16[896,128]{1,0:T(8,128)(2,1)} %bitcast.95), channel_id=1, source_target_pairs={{0,2},{1,3},{2,0},{3,1},{4,6},{5,7},{6,4},{7,5},{8,10},{9,11},{10,... | collective-permute-start | bytes 688136 | tf_op jit(solution)/shard_map/ppermute | solution.py:305
  293.5 34.9 %collective-permute-start.20 = (bf16[896,128]{1,0:T(8,128)(2,1)}, bf16[896,128]{1,0:T(8,128)(2,1)}, u32[]{:S(2)}, u32[]{:S(2)}) collective-permute-start(bf16[896,128]{1,0:T(8,128)(2,1)} %bitcast.94), channel_id=1, source_target_pairs={{0,3},{1,0},{2,1},{3,2},{4,7},{5,4},{6,5},{7,6},{8,11},{9,8},{10,9... | collective-permute-start | bytes 688136 | tf_op jit(solution)/shard_map/ppermute | solution.py:305
  339.2 14.3 %all-to-all-start = ((f32[32,1,1]{2,1,0:T(1,128)}), f32[32,1,1]{2,1,0:T(1,128)S(1)}, u32[]{:S(2)}, u32[]{:S(2)}) async-start(f32[32,1,1]{2,1,0:T(1,128)} %broadcast_in_dim.38), calls=%async_computation | async-start | bytes 32768 | tf_op jit(solution)/shard_map/all_to_all | solution.py:380
  (30 other events, 953.1 us)

commit v2 on v1

--- a/solution.py
+++ b/solution.py
@@ -168,100 +168,172 @@
     return [mixed[s * len(splits) : (s + 1) * len(splits)] for s in range(ring)], result[-1]
 
 
-def quantize(part_index, pieces, scale_row, scale_octet, spread, numbers, before, first_row, rows, all_rows, tile):
-    each = len(pieces)
-    ring = len(pieces[0])
+def octet_error(values):
+    near_sum = low_sum = squares = far_squares = largest = smallest = None
+    for value in values:
+        near = jnp.floor(value + 0.5)
+        low = jnp.floor(value)
+        gap = jnp.abs(value - near)
+        far = 0.5 - gap
+        if near_sum is None:
+            near_sum, low_sum, squares, far_squares = near, low, gap * gap, far * far
+            largest = smallest = gap
+        else:
+            near_sum, low_sum = near_sum + near, low_sum + low
+            squares, far_squares = squares + gap * gap, far_squares + far * far
+            largest, smallest = jnp.maximum(largest, gap), jnp.minimum(smallest, gap)
+    near_half, low_half = near_sum * 0.5, low_sum * 0.5
+    whole = jnp.where(near_half != jnp.floor(near_half), squares + (1.0 - 2.0 * largest), squares)
+    shifted = jnp.where(low_half != jnp.floor(low_half), far_squares + 2.0 * smallest, far_squares)
+    return jnp.minimum(whole, shifted)
+
+
+def quantize(chunk, pieces, scale_row, scale_octet, spread, place, before, halves_error, first_row, rows, tile):
+    ring = len(pieces)
+    piece = pieces[0].shape[1]
+    all_rows, all_width = before[2]
+    width = ring * piece
+    fold = OCTET * 128 // width
+    lanes = width // OCTET
+    skip = first_row // tile
+    band = tile // fold
+    closing = chunk % fold == fold - 1
+
+    def kernel(place_ref, *refs):
+        ins = refs[:ring]
+        row_ref, oct_ref, spread_ref = refs[ring : ring + 3]
+        half_ref = refs[ring + 3] if halves_error is not None else None
+        scaled_ref, error_ref, stage = refs[-3:]
+        mine = place_ref[0]
+        bands = [r[f * band : (f + 1) * band, :] for f in range(fold) for r in ins]
+        stage[...] = jnp.dot(
+            jnp.concatenate(bands, axis=1), spread_ref[...], preferred_element_type=jnp.float32
+        )
+        starts = [pl.multiple_of(lax.rem(mine - s + ring, ring) * piece, 128) for s in range(ring)]
+
+        def one(group, _):
+            start = pl.multiple_of(group * LOW, LOW)
+            for f in range(fold):
+                held = pl.ds(f * band + start, LOW)
+                for s in range(ring):
+                    cols = pl.ds(starts[s], piece)
+                    scaled = ins[s][held, :].astype(jnp.float32) * row_ref[:, cols]
+                    scaled_ref[held, cols] = scaled.astype(jnp.bfloat16)
+            held = pl.ds(start, LOW)
+            error = octet_error(stage[held, i * 128 : (i + 1) * 128] * oct_ref[i : i + 1, :] for i in range(OCTET))
+            if fold == 1 or not closing:
+                error_ref[held, :] = error
+            else:
+                other = half_ref[held, :]
+                left = lax.broadcasted_iota(jnp.int32, (LOW, 128), 1) < lanes
+                error_ref[held, :] = jnp.where(left, other, pltpu.roll(error, lanes, 1))
+                error_ref[pl.ds(band + start, LOW), :] = jnp.where(left, pltpu.roll(other, lanes, 1), error)
+            return 0
+
+        lax.fori_loop(0, band // LOW, one, 0, unroll=2)
+
+    in_specs = [pl.BlockSpec(memory_space=pltpu.SMEM)]
+    for p in pieces:
+        in_specs.append(pl.BlockSpec((tile, piece), lambda r, o=skip * (p.shape[0] == all_rows): (r + o, 0)))
+    in_specs += [
+        pl.BlockSpec((1, width), lambda r: (0, chunk)),
+        pl.BlockSpec((OCTET, 128), lambda r: (chunk, 0)),
+        pl.BlockSpec((OCTET * 128, OCTET * 128), lambda r: (0, 0)),
+    ]
+    operands = [place, *pieces, scale_row, scale_octet, spread]
+    if halves_error is not None:
+        in_specs.append(pl.BlockSpec((band, 128), lambda r: (r + skip, 0)))
+        operands.append(halves_error)
+    aliases = {}
+    if before[0] is not None:
+        aliases[len(operands)] = 0
+        in_specs.append(pl.BlockSpec(memory_space=pl.ANY))
+        operands.append(before[0])
+    if closing:
+        error_spec = pl.BlockSpec((tile, 128), lambda r: (r + skip, chunk // fold))
+        error_shape = (all_rows, all_width // OCTET)
+        if before[1] is not None:
+            aliases[len(operands)] = 1
+            in_specs.append(pl.BlockSpec(memory_space=pl.ANY))
+            operands.append(before[1])
+    else:
+        error_spec = pl.BlockSpec((band, 128), lambda r: (r + skip, 0))
+        error_shape = (all_rows // fold, 128)
+    scaled, errors = pl.pallas_call(
+        kernel,
+        grid=(rows // tile,),
+        in_specs=in_specs,
+        out_specs=[pl.BlockSpec((tile, width), lambda r: (r + skip, chunk)), error_spec],
+        out_shape=[
+            jax.ShapeDtypeStruct((all_rows, all_width), jnp.bfloat16),
+            jax.ShapeDtypeStruct(error_shape, jnp.float32),
+        ],
+        scratch_shapes=[pltpu.VMEM((band, OCTET * 128), jnp.float32)],
+        input_output_aliases=aliases,
+        name="quantize",
+    )(*operands)
+    if closing:
+        return (scaled, errors, before[2]), None
+    return (scaled, before[1], before[2]), errors
+
+
+def lattice_sum(pieces, scale_own, spread_own, place, first_row, rows, tile, all_rows):
+    ring = len(pieces)
     piece = pieces[0][0].shape[1]
+    own = len(pieces[0]) * piece
+    fold = OCTET * 128 // own
     skip = first_row // tile
-    width = each * ring * piece
-    lanes = width // OCTET
-    parts_in_all = scale_row.shape[1] // width
-    flat = [p for chunk in pieces for p in chunk]
-
-    def kernel(num_ref, *refs):
-        ins = refs[: each * ring]
-        row_ref, oct_ref, spread_ref = refs[each * ring : each * ring + 3]
-        scaled_ref, error_ref, sum_ref, stage = refs[-4:]
-        mine, first, total = num_ref[0], num_ref[1], num_ref[2]
+    share = 4.0 / (3.0 * all_rows * ring)
+    flat = [p for owner in pieces for p in owner]
+
+    def kernel(place_ref, *refs):
+        ins, oct_ref, spread_ref, sum_ref, stage = refs[: len(flat)], *refs[len(flat) :]
+        mine = place_ref[0]
         step = pl.program_id(0)
-        stage[...] = jnp.dot(
-            jnp.concatenate([r[...] for r in ins], axis=1), spread_ref[...], preferred_element_type=jnp.float32
-        )
-        starts = []
-        for index in range(each * ring):
-            owner = lax.rem(mine - index % ring + ring, ring)
-            starts.append(pl.multiple_of((index // ring * ring + owner) * piece, 128))
-        share = 4.0 / (3.0 * total.astype(jnp.float32))
-
-        def one(group, carry):
-            held = pl.ds(pl.multiple_of(group * LOW, LOW), LOW)
-            for index in range(each * ring):
-                cols = pl.ds(starts[index], piece)
-                scaled = ins[index][held, :].astype(jnp.float32) * row_ref[:, cols]
-                scaled_ref[held, cols] = scaled.astype(jnp.bfloat16)
-            near_sum = low_sum = squares = far_squares = largest = smallest = None
-            for i in range(OCTET):
-                value = stage[held, i * lanes : (i + 1) * lanes] * oct_ref[i : i + 1, :]
-                near = jnp.floor(value + 0.5)
-                low = jnp.floor(value)
-                gap = jnp.abs(value - near)
-                far = 0.5 - gap
-                if i == 0:
-                    near_sum, low_sum, squares, far_squares = near, low, gap * gap, far * far
-                    largest = smallest = gap
-                else:
-                    near_sum, low_sum = near_sum + near, low_sum + low
-                    squares, far_squares = squares + gap * gap, far_squares + far * far
-                    largest, smallest = jnp.maximum(largest, gap), jnp.minimum(smallest, gap)
-            near_half, low_half = near_sum * 0.5, low_sum * 0.5
-            whole = jnp.where(near_half != jnp.floor(near_half), squares + (1.0 - 2.0 * largest), squares)
-            shifted = jnp.where(low_half != jnp.floor(low_half), far_squares + 2.0 * smallest, far_squares)
-            error = jnp.minimum(whole, shifted)
-            error_ref[held, :] = error
-            position = lax.broadcasted_iota(jnp.int32, (LOW, lanes), 0) + (first + first_row + step * tile + group * LOW)
-            weight = (position.astype(jnp.float32) + 0.5) * share + (1.0 / 3.0)
-            return carry + error * weight
-
-        part = lax.fori_loop(0, tile // LOW, one, jnp.zeros((LOW, lanes), jnp.float32), unroll=2)
 
         @pl.when(step == 0)
         def _():
             sum_ref[...] = jnp.zeros_like(sum_ref)
 
-        sum_ref[...] += part
+        lane = lax.broadcasted_iota(jnp.int32, (LOW, 128), 1)
+        inside = lax.broadcasted_iota(jnp.int32, (LOW, 128), 0)
+        each = len(flat) // ring * fold
+        for group in range(ring // fold):
+            stage[...] = jnp.dot(
+                jnp.concatenate([r[...] for r in ins[group * each : (group + 1) * each]], axis=1),
+                spread_ref[...],
+                preferred_element_type=jnp.float32,
+            )
+            owner = mine + (group * fold + lane // (128 // fold))
+            owner = jnp.where(owner >= ring, owner - ring, owner)
+            position = owner * all_rows + inside + (first_row + step * tile)
+
+            def one(index, carry):
+                held = pl.ds(pl.multiple_of(index * LOW, LOW), LOW)
+                error = octet_error(
+                    stage[held, i * 128 : (i + 1) * 128] * oct_ref[i : i + 1, :] for i in range(OCTET)
+                )
+                weight = ((position + index * LOW).astype(jnp.float32) + 0.5) * share + (1.0 / 3.0)
+                return carry + error * weight
+
+            sum_ref[...] += lax.fori_loop(0, tile // LOW, one, jnp.zeros((LOW, 128), jnp.float32), unroll=2)
 
     in_specs = [pl.BlockSpec(memory_space=pltpu.SMEM)]
     for p in flat:
         in_specs.append(pl.BlockSpec((tile, piece), lambda r, o=skip * (p.shape[0] == all_rows): (r + o, 0)))
     in_specs += [
-        pl.BlockSpec((1, width), lambda r: (0, part_index)),
-        pl.BlockSpec((OCTET, lanes), lambda r: (0, part_index)),
-        pl.BlockSpec((width, width), lambda r: (0, 0)),
+        pl.BlockSpec((OCTET, 128), lambda r: (0, 0)),
+        pl.BlockSpec((OCTET * 128, OCTET * 128), lambda r: (0, 0)),
     ]
-    operands = [numbers, *flat, scale_row, scale_octet, spread]
-    aliases = {}
-    if before is not None:
-        aliases = {len(operands): 0, len(operands) + 1: 1}
-        in_specs += [pl.BlockSpec(memory_space=pl.ANY)] * 2
-        operands += list(before)
     return pl.pallas_call(
         kernel,
         grid=(rows // tile,),
         in_specs=in_specs,
-        out_specs=[
-            pl.BlockSpec((tile, width), lambda r: (r + skip, part_index)),
-            pl.BlockSpec((tile, lanes), lambda r: (r + skip, part_index)),
-            pl.BlockSpec((LOW, lanes), lambda r: (0, 0)),
-        ],
-        out_shape=[
-            jax.ShapeDtypeStruct((all_rows, parts_in_all * width), jnp.bfloat16),
-            jax.ShapeDtypeStruct((all_rows, parts_in_all * lanes), jnp.float32),
-            jax.ShapeDtypeStruct((LOW, lanes), jnp.float32),
-        ],
-        scratch_shapes=[pltpu.VMEM((tile, width), jnp.float32)],
-        input_output_aliases=aliases,
-        name="quantize",
-    )(*operands)
+        out_specs=pl.BlockSpec((LOW, 128), lambda r: (0, 0)),
+        out_shape=jax.ShapeDtypeStruct((LOW, 128), jnp.float32),
+        scratch_shapes=[pltpu.VMEM((tile, OCTET * 128), jnp.float32)],
+        name="lattice_sum",
+    )(place, *flat, scale_own, spread_own)
 
 
 def mixer_table(mine, ring, blocks):
@@ -280,13 +352,19 @@
     return jnp.where((common & 1) == 0, table, -table).astype(jnp.bfloat16)
 
 
-def spread_table(mine, ring, piece, width):
-    row = lax.broadcasted_iota(jnp.int32, (width, width), 0)
-    col = lax.broadcasted_iota(jnp.int32, (width, width), 1)
-    index = row // piece
-    natural = (index // ring * ring + (mine - index % ring + ring) % ring) * piece + row % piece
-    target = (natural % OCTET) * (width // OCTET) + natural // OCTET
+def spread_table(natural, fold):
+    side = OCTET * 128
+    width = side // fold
+    row = lax.broadcasted_iota(jnp.int32, (side, side), 0)
+    col = lax.broadcasted_iota(jnp.int32, (side, side), 1)
+    column = natural(row % width)
+    target = (column % OCTET) * 128 + (row // width) * (width // OCTET) + column // OCTET
     return (target == col).astype(jnp.bfloat16)
+
+
+def octet_rows(scales):
+    turned = jnp.swapaxes(scales.reshape(scales.shape[:-1] + (-1, OCTET)), -1, -2)
+    return jnp.concatenate([turned] * (128 // turned.shape[-1]), axis=-1)
 
 
 def body(weights, left_bits, right_bits, groups):
@@ -297,27 +375,33 @@
     blocks_here = local_rows // HB
     chunks = chunk_count(width, ring)
     piece = width // (chunks * ring)
-    unit = OCTET * 128
-    each = unit // (ring * piece)
     place = mine.reshape(1)
 
     def send(x, shift):
         return lax.ppermute(x, "row", [(k, (k + shift) % ring) for k in range(ring)])
 
+    column_args = (weights[0], left_bits, right_bits, place, ring, chunks)
+    start_rows = max(blocks_here * 2 // 7, 1) * HB
+    early, whole = column_transform(*column_args, 0, start_rows, start_rows, None)
+    left_rows = local_rows - start_rows
+    late, whole = column_transform(
+        *column_args, start_rows, left_rows, math.gcd(start_rows, left_rows), whole
+    )
     splits = (blocks_here // 2, blocks_here - blocks_here // 2)
     halves = [n * HB for n in splits]
     step_rows = math.gcd(*halves)
-    column_args = (weights[0], left_bits, right_bits, place, ring, chunks)
-    early, whole = column_transform(*column_args, 0, halves[0], step_rows, None)
-    late, whole = column_transform(*column_args, halves[0], halves[1], step_rows, whole)
     outgoing = [[[early[s], late[s]] for s in range(ring)]]
     outgoing += [[[whole[c * ring + s]] for s in range(ring)] for c in range(chunks - 1)]
     mixer = mixer_table(mine, ring, blocks_here)
-    spread = spread_table(mine, ring, piece, unit)
+    band_columns = ring * piece
+    spread = spread_table(
+        lambda at: (mine - at // piece + ring) % ring * piece + at % piece, OCTET * 128 // band_columns
+    )
+    spread_own = spread_table(lambda at: at, OCTET * 128 // (chunks * piece))
     own_groups = [
         lax.dynamic_slice_in_dim(groups, (chunk * ring + mine) * piece, piece, 1) for chunk in range(chunks)
     ]
-    received, returned = [], []
+    received, returned, kept = [], [], []
     for chunk in range(chunks):
         leaving = outgoing[chunk][1:]
         if chunk >= AHEAD:
@@ -339,6 +423,7 @@
         )
         if last:
             peaks = [peak] + [send(peak, s) for s in range(1, ring)]
+        kept.append(mixed)
         back = []
         for part in range(len(mixed[0])):
             back.append([mixed[0][part]] + [send(mixed[s][part], s) for s in range(1, ring)])
@@ -348,39 +433,46 @@
     group_peak = jnp.maximum(group_peak, 1.0)
     in_group = groups == jnp.arange(GROUPS, dtype=jnp.int32)[:, None]
     scale_row = jnp.sum(jnp.where(in_group, (2.0 / group_peak)[:, None], 0.0), axis=0)
-    scale_octet = scale_row.reshape(width // OCTET, OCTET).T
-
-    numbers = jnp.stack([mine, mine * local_rows, jnp.int32(local_rows) * ring])
-    before, total = None, 0.0
+    scale_octet = octet_rows(scale_row.reshape(chunks, band_columns)).reshape(chunks * OCTET, 128)
+    own_scale = lax.dynamic_slice_in_dim(scale_row.reshape(chunks, ring, piece), mine, 1, 1)
+    scale_own = octet_rows(own_scale.reshape(chunks * piece))
+
     fine = even_tile(step_rows, TILE2)
-    for part_index in range(width // unit):
-        held = returned[part_index * each : (part_index + 1) * each]
-        ranges = [(0, local_rows)]
-        if len(held[-1]) > 1:
-            ranges = [(0, halves[0]), (halves[0], halves[1])]
-        for part, (first_row, count) in enumerate(ranges):
-            scaled, errors, share = quantize(
-                part_index,
-                [chunk[part % len(chunk)] for chunk in held],
-                scale_row[None, :],
-                scale_octet,
-                spread,
-                numbers,
-                before,
-                first_row,
-                count,
-                local_rows,
-                fine,
-            )
-            before = (scaled, errors)
-            total = total + share
-    partial_error = jnp.sum(total) / (local_rows * ring * width // OCTET)
+    ranges = [(0, halves[0]), (halves[0], halves[1])]
+    shares = []
+    for part, (first_row, count) in enumerate(ranges):
+        own_pieces = [[k[s][part % len(k[s])] for k in kept] for s in range(ring)]
+        shares.append(
+            lattice_sum(own_pieces, scale_own, spread_own, place, first_row, count, fine, local_rows)
+        )
+    partial_error = jnp.sum(sum(shares)) / (local_rows * ring * width // OCTET)
     expert_count = lax.axis_size("expert")
     copies = jnp.broadcast_to(partial_error, (expert_count * ring, 1))
     every_error = lax.all_to_all(copies, ("expert", "row"), 0, 0)
     every_error = jnp.sum(every_error.reshape(expert_count, ring), axis=1)
     expert_error = lax.dynamic_slice_in_dim(every_error, lax.axis_index("expert"), 1)
     total_error = jnp.sum(every_error) / expert_count
+
+    before, half_error = (None, None, (local_rows, width)), None
+    for chunk in range(chunks):
+        back = returned[chunk]
+        spans = [(0, local_rows)] if len(back) == 1 else ranges
+        given = half_error
+        for part, (first_row, count) in enumerate(spans):
+            before, half_error = quantize(
+                chunk,
+                back[part],
+                scale_row[None, :],
+                scale_octet,
+                spread,
+                place,
+                before,
+                given,
+                first_row,
+                count,
+                fine,
+            )
+    scaled, errors, _ = before
     return (scaled[None], errors[None], (group_peak / 2.0)[None], expert_error, total_error)
 
 

time: 357 us -> 379 us (1.062)
  Pallas kernels: 74 us -> 107 us
  waiting for transfers between devices: 121 us -> 104 us
  starting transfers between devices: 122 us -> 126 us
    pallas_call x0 -> x2, Pallas kernels: none -> 23.7 us  [lattice_sum(): pl.pallas_call(kernel, grid=(rows // tile,), in_specs=in_specs, out_specs...]
    ppermute x33, waiting for transfers between devices: 114 us -> 102 us  [send(): lax.ppermute(x, 'row', [(k, (k + shift) % ring) for k in range(ring)])]
    pallas_call x3 -> x5, Pallas kernels: 29.7 us -> 38.5 us  [quantize(): pl.pallas_call(kernel, grid=(rows // tile,), in_specs=in_specs, out_specs...]
    ppermute x33, starting transfers between devices: 115 us -> 121 us  [send(): lax.ppermute(x, 'row', [(k, (k + shift) % ring) for k in range(ring)])]
    all_to_all x1, waiting for transfers between devices: 7.19 us -> 2.54 us  [body(): every_error = lax.all_to_all(copies, ('expert', 'row'), 0, 0)]
  transfers between devices with their start and end apart: 34 -> 34, of which waited for: 12 -> 9; matrix products, arithmetic and copies ran while one was open for 8% -> 9% of each run, Pallas kernels for 17% -> 21%
where the time goes in v2:
time: 379 us
  starting transfers between devices  126 us (33%)
  Pallas kernels  107 us (28%)
  waiting for transfers between devices  104 us (27%)
  other arithmetic  30.5 us (8%)
  local copies, waits for them, and re-layouts  8.05 us (2%)
    ppermute x33, starting transfers between devices, send(): lax.ppermute(x, 'row', [(k, (k + shift) % ring) for k in range(ring)])  121 us
    ppermute x33, waiting for transfers between devices, send(): lax.ppermute(x, 'row', [(k, (k + shift) % ring) for k in range(ring)])  102 us
    pallas_call x5, Pallas kernels, quantize(): pl.pallas_call(kernel, grid=(rows // tile,), in_specs=in_specs, out_specs...  38.5 us
    pallas_call x4, Pallas kernels, row_mix(): pl.pallas_call(kernel, out_shape=[jax.ShapeDtypeStruct((n, high, LOW, wid...  31.8 us
    pallas_call x2, Pallas kernels, lattice_sum(): pl.pallas_call(kernel, grid=(rows // tile,), in_specs=in_specs, out_specs...  23.7 us
    convert_element_type x1, other arithmetic, mixer_table(): return jnp.where(common & 1 == 0, table, -table).astype(jnp.bfloat16)  20.4 us
    pallas_call x2, Pallas kernels, column_transform(): pl.pallas_call(kernel, grid=(rows // tile,), in_specs=in_specs, out_specs...  12.6 us
  transfers between devices with their start and end apart: 34, of which 9 were waited for; matrix products, arithmetic and copies ran while one was open for 9% of the time, Pallas kernels for 21%

profile of v2, /device:TPU:0, one launch (start us, length us, event | category | flops | bytes accessed | tf_op | source)
XLA Modules:
  0.0 378.8 jit_solution(5788645332213988808)
XLA Ops:
  0.6 4.4 %column_transform.2 = (bf16[512,128]{1,0:T(8,128)(2,1)}, bf16[512,128]{1,0:T(8,128)(2,1)}, bf16[512,128]{1,0:T(8,128)(2,1)}, bf16[512,128]{1,0:T(8,128)(2,1)}, b...) custom-call(s32[1]{0:T(128)} %bitcast.place_ref, ...), custom_call_target="tpu_custom_call" | custom-call | tf_op jit(solution)/shard_map/column_transform/pallas_call | solution.py:104
  5.1 8.2 %column_transform.3 = (bf16[1280,128]{1,0:T(8,128)(2,1)}, bf16[1280,128]{1,0:T(8,128)(2,1)}, bf16[1280,128]{1,0:T(8,128)(2,1)}, bf16[1280,128]{1,0:T(8,128)(2,1)...) custom-call(s32[1]{0:T(128)} %bitcast.place_ref, ...), custom_call_target="tpu_custom_call", output_to_operand_aliasing={{4}: (4, {}), {5}: (5, {}), {6}: (6, {}), {7}: (7, {}), {8}... | custom-call | tf_op jit(solution)/shard_map/column_transform/pallas_call | solution.py:104
  21.3 22.9 %collective-permute-done.6 = bf16[512,128]{1,0:T(8,128)(2,1)S(1)} collective-permute-done((bf16[512,128]{1,0:T(8,128)(2,1)S(1)}, bf16[512,128]{1,0:T(8,128)(2,1)S(1)}, u32[]{:S(2)}, u32[]{:S(2)}) %collective-permute-start.6) | collective-permute-done | bytes 131104 | tf_op jit(solution)/shard_map/ppermute | solution.py:381
  44.1 11.7 %collective-permute-done.8 = bf16[512,128]{1,0:T(8,128)(2,1)S(1)} collective-permute-done((bf16[512,128]{1,0:T(8,128)(2,1)S(1)}, bf16[512,128]{1,0:T(8,128)(2,1)S(1)}, u32[]{:S(2)}, u32[]{:S(2)}) %collective-permute-start.8) | collective-permute-done | bytes 131104 | tf_op jit(solution)/shard_map/ppermute | solution.py:381
  59.3 4.9 %collective-permute-start.1 = (bf16[1792,128]{1,0:T(8,128)(2,1)}, bf16[1792,128]{1,0:T(8,128)(2,1)S(1)}, u32[]{:S(2)}, u32[]{:S(2)}) collective-permute-start(bf16[1792,128]{1,0:T(8,128)(2,1)} %get-tuple-element.103), channel_id=1, source_target_pairs={{0,2},{1,3},{2,0},{3,1},{4,6},{5,7},{6,4},{7,5},{8,10},{9,11},{10,... | collective-permute-start | bytes 1376264 | tf_op jit(solution)/shard_map/ppermute | solution.py:381
  67.2 5.8 %collective-permute-done = bf16[1792,128]{1,0:T(8,128)(2,1)S(1)} collective-permute-done((bf16[1792,128]{1,0:T(8,128)(2,1)}, bf16[1792,128]{1,0:T(8,128)(2,1)S(1)}, u32[]{:S(2)}, u32[]{:S(2)}) %collective-permute-start) | collective-permute-done | bytes 458784 | tf_op jit(solution)/shard_map/ppermute | solution.py:381
  72.9 3.4 collective-permute-start.14
  76.4 16.3 %collective-permute-done.1 = bf16[1792,128]{1,0:T(8,128)(2,1)S(1)} collective-permute-done((bf16[1792,128]{1,0:T(8,128)(2,1)}, bf16[1792,128]{1,0:T(8,128)(2,1)S(1)}, u32[]{:S(2)}, u32[]{:S(2)}) %collective-permute-start.1) | collective-permute-done | bytes 458784 | tf_op jit(solution)/shard_map/ppermute | solution.py:381
  92.7 30.1 %collective-permute-start.3 = (bf16[1792,128]{1,0:T(8,128)(2,1)}, bf16[1792,128]{1,0:T(8,128)(2,1)}, u32[]{:S(2)}, u32[]{:S(2)}) collective-permute-start(bf16[1792,128]{1,0:T(8,128)(2,1)} %get-tuple-element.105), channel_id=1, source_target_pairs={{0,1},{1,2},{2,3},{3,0},{4,5},{5,6},{6,7},{7,4},{8,9},{9,10},{10,1... | collective-permute-start | bytes 1376264 | tf_op jit(solution)/shard_map/ppermute | solution.py:381
  125.1 20.4 %fusion.42.refs_8_.refs_4_ = bf16[896,896]{1,0:T(8,128)(2,1)} fusion(s32[896]{0:T(1024)S(1)} %get-tuple-element.178, s32[896]{0:T(1024)S(1)} %get-tuple-element.179, s32[896]{0:T(1024)S(1)} %get-tuple-element.177, s32[896]{0:T(1024)S(1)} %get-tuple-element.184, s32[]{:T(128)} %axis_index.22, s32[896]{0:T(1024)S(1)} %get-tuple-element.180, ...), kind=kLoop, calls=%fused_computation.87 | loop fusion | flops 69042176 | bytes 1629828 | tf_op jit(solution)/shard_map/convert_element_type | solution.py:352
  147.3 7.9 %row_mix.4 = (bf16[14,8,16,128]{3,2,1,0:T(8,128)(2,1)}, bf16[14,8,16,128]{3,2,1,0:T(8,128)(2,1)}, bf16[14,8,16,128]{3,2,1,0:T(8,128)(2,1)}, bf16[14,8,16,128]{3,2,1,0:T(8,128)(2,1)}, f32[16,128]{1,0:T(8,128)}) custom-call(bf16[4,8,16,128]{3,2,1,0:T(8,128)(2,1)} %bitcast.127, bf16[10,8,16,128]{3,2,1,0:T(8,128)(2,1)} %bitcast.113, ...), custom_call_target="tpu_custom_call" | custom-call | tf_op jit(solution)/shard_map/row_mix/pallas_call | solution.py:160
  155.2 7.9 %row_mix.5 = (bf16[14,8,16,128]{3,2,1,0:T(8,128)(2,1)}, bf16[14,8,16,128]{3,2,1,0:T(8,128)(2,1)}, bf16[14,8,16,128]{3,2,1,0:T(8,128)(2,1)}, bf16[14,8,16,128]{3,2,1,0:T(8,128)(2,1)}, f32[16,128]{1,0:T(8,128)}) custom-call(bf16[14,8,16,128]{3,2,1,0:T(8,128)(2,1)} %bitcast.93, bf16[14,8,16,128]{3,2,1,0:T(8,128)(2,1)} %bitcast.101, ...), custom_call_target="tpu_custom_call" | custom-call | tf_op jit(solution)/shard_map/row_mix/pallas_call | solution.py:160
  164.1 8.0 %row_mix.6 = (bf16[14,8,16,128]{3,2,1,0:T(8,128)(2,1)}, bf16[14,8,16,128]{3,2,1,0:T(8,128)(2,1)}, bf16[14,8,16,128]{3,2,1,0:T(8,128)(2,1)}, bf16[14,8,16,128]{3,2,1,0:T(8,128)(2,1)}, f32[16,128]{1,0:T(8,128)}) custom-call(bf16[14,8,16,128]{3,2,1,0:T(8,128)(2,1)} %bitcast.94, bf16[14,8,16,128]{3,2,1,0:T(8,128)(2,1)} %bitcast.103, ...), custom_call_target="tpu_custom_call" | custom-call | tf_op jit(solution)/shard_map/row_mix/pallas_call | solution.py:160
  172.2 8.0 %row_mix.7 = (bf16[7,8,16,128]{3,2,1,0:T(8,128)(2,1)}, bf16[7,8,16,128]{3,2,1,0:T(8,128)(2,1)}, bf16[7,8,16,128]{3,2,1,0:T(8,128)(2,1)}, bf16[7,8,16,128]{3,2,1,...) custom-call(bf16[14,8,16,128]{3,2,1,0:T(8,128)(2,1)} %bitcast.95, ...), custom_call_target="tpu_custom_call" | custom-call | tf_op jit(solution)/shard_map/row_mix/pallas_call | solution.py:160
  180.2 7.5 %collective-permute-start.20 = (f32[16,128]{1,0:T(8,128)}, f32[16,128]{1,0:T(8,128)S(1)}, u32[]{:S(2)}, u32[]{:S(2)}) collective-permute-start(f32[16,128]{1,0:T(8,128)} %get-tuple-element.140), channel_id=1, source_target_pairs={{0,3},{1,0},{2,1},{3,2},{4,7},{5,4},{6,5},{7,6},{8,11},{9,8},{10,9... | collective-permute-start | bytes 24584 | tf_op jit(solution)/shard_map/ppermute | solution.py:381
  196.3 5.5 %fusion.22 = (bf16[1024,1024]{1,0:T(8,128)(2,1)}, bf16[1024,1024]{1,0:T(8,128)(2,1)}) fusion(s32[1024]{0:T(1024)S(1)} %get-tuple-element.185, s32[1024]{0:T(1024)S(1)} %get-tuple-element.188, s32[1024]{0:T(1024)S(1)} %get-tuple-element.186, s32[1024]{0:T(1024)S(1)} %get-tuple-element.187, pred[1024]{0:T(1024)(128)(4,1)S(1)} %get-tuple-element.189, ...), kind=kLoop, calls=%fused_computation.67 | loop fusion | flops 83886080 | bytes 4212740 | tf_op jit(solution)/shard_map/convert_element_type | solution.py:362
  202.2 3.3 collective-permute-done.27.refs_1_
  208.1 17.1 %collective-permute-done.28.refs_2_ = bf16[1792,128]{1,0:T(8,128)(2,1)} collective-permute-done((bf16[1792,128]{1,0:T(8,128)(2,1)S(1)}, bf16[1792,128]{1,0:T(8,128)(2,1)}, u32[]{:S(2)}, u32[]{:S(2)}) %collective-permute-start.28) | collective-permute-done | bytes 458784 | tf_op jit(solution)/shard_map/ppermute | solution.py:381
  225.2 25.3 %collective-permute-start.21 = (bf16[1792,128]{1,0:T(8,128)(2,1)}, bf16[1792,128]{1,0:T(8,128)(2,1)S(1)}, u32[]{:S(2)}, u32[]{:S(2)}) collective-permute-start(bf16[1792,128]{1,0:T(8,128)(2,1)} %bitcast.90), channel_id=1, source_target_pairs={{0,1},{1,2},{2,3},{3,0},{4,5},{5,6},{6,7},{7,4},{8,9},{9,10},{10,1... | collective-permute-start | bytes 1376264 | tf_op jit(solution)/shard_map/ppermute | solution.py:381
  250.5 4.0 %collective-permute-start.22 = (bf16[1792,128]{1,0:T(8,128)(2,1)S(1)}, bf16[1792,128]{1,0:T(8,128)(2,1)S(1)}, u32[]{:S(2)}, u32[]{:S(2)}) collective-permute-start(bf16[1792,128]{1,0:T(8,128)(2,1)S(1)} %bitcast.80), channel_id=1, source_target_pairs={{0,2},{1,3},{2,0},{3,1},{4,6},{5,7},{6,4},{7,5},{8,10},{9,11},{10,... | collective-permute-start | bytes 1376264 | tf_op jit(solution)/shard_map/ppermute | solution.py:381
  254.5 3.1 collective-permute-start.23
  258.1 24.0 %collective-permute-done.25.refs_2_ = bf16[1792,128]{1,0:T(8,128)(2,1)} collective-permute-done((bf16[1792,128]{1,0:T(8,128)(2,1)}, bf16[1792,128]{1,0:T(8,128)(2,1)}, u32[]{:S(2)}, u32[]{:S(2)}) %collective-permute-start.25) | collective-permute-done | bytes 458784 | tf_op jit(solution)/shard_map/ppermute | solution.py:381
  282.1 9.3 %collective-permute-start.30 = (bf16[896,128]{1,0:T(8,128)(2,1)}, bf16[896,128]{1,0:T(8,128)(2,1)}, u32[]{:S(2)}, u32[]{:S(2)}) collective-permute-start(bf16[896,128]{1,0:T(8,128)(2,1)} %bitcast.43.refs_7_), channel_id=1, source_target_pairs={{0,1},{1,2},{2,3},{3,0},{4,5},{5,6},{6,7},{7,4},{8,9},{9,10},{10,1... | collective-permute-start | bytes 688136 | tf_op jit(solution)/shard_map/ppermute | solution.py:381
  292.4 11.8 %lattice_sum.2 = f32[16,128]{1,0:T(8,128)} custom-call(s32[1]{0:T(128)} %bitcast.place_ref, bf16[1792,128]{1,0:T(8,128)(2,1)} %bitcast.60, bf16[1792,128]{1,0:T(8,128)(2,1)} %bitcast.63, bf16[1792,128]{1,0:T(8,128)(2,1)} %bitcast.57, bf16[896,128]{1,0:T(8,128)(2,1)} %bitcast.98, bf16[1792,128]{1,0:T(8,128)(2,1)} %bitcast.69, bf16[1792,128]{1,0:T(8,128)(2,1)} %bitcast.84, ...), custom_call_target="tpu_custom_call" | custom-call | tf_op jit(solution)/shard_map/lattice_sum/pallas_call | solution.py:328
  304.2 11.9 %lattice_sum.3 = f32[16,128]{1,0:T(8,128)} custom-call(s32[1]{0:T(128)} %bitcast.place_ref, bf16[1792,128]{1,0:T(8,128)(2,1)} %bitcast.61, bf16[1792,128]{1,0:T(8,128)(2,1)} %bitcast.64, bf16[1792,128]{1,0:T(8,128)(2,1)} %bitcast.58, bf16[896,128]{1,0:T(8,128)(2,1)} %bitcast.96, bf16[1792,128]{1,0:T(8,128)(2,1)} %bitcast.70, bf16[1792,128]{1,0:T(8,128)(2,1)} %bitcast.85, ...), custom_call_target="tpu_custom_call" | custom-call | tf_op jit(solution)/shard_map/lattice_sum/pallas_call | solution.py:328
  316.2 3.4 collective-permute-start.16
  326.7 5.4 %all-to-all-start = ((f32[32,1,1]{2,1,0:T(1,128)}), f32[32,1,1]{2,1,0:T(1,128)S(1)}, u32[]{:S(2)}, u32[]{:S(2)}) async-start(f32[32,1,1]{2,1,0:T(1,128)} %broadcast_in_dim.40), calls=%async_computation | async-start | bytes 32768 | tf_op jit(solution)/shard_map/all_to_all | solution.py:451
  332.9 7.9 %quantize.5 = (bf16[1792,2048]{1,0:T(8,128)(2,1)}, f32[896,128]{1,0:T(8,128)}) custom-call(s32[1]{0:T(128)} %bitcast.place_ref, bf16[1792,128]{1,0:T(8,128)(2,1)} %bitcast.62, bf16[1792,128]{1,0:T(8,128)(2,1)} %collective-permute-done.27.refs_1_, bf16[1792,128]{1,0:T(8,128)(2,1)} %collective-permute-done.28.refs_2_, ...), custom_call_target="tpu_custom_call" | custom-call | tf_op jit(solution)/shard_map/quantize/pallas_call | solution.py:262
  340.8 9.9 %quantize.6 = (bf16[1792,2048]{1,0:T(8,128)(2,1)}, f32[1792,256]{1,0:T(8,128)}) custom-call(s32[1]{0:T(128)} %bitcast.place_ref, bf16[1792,128]{1,0:T(8,128)(2,1)} %bitcast.65, bf16[1792,128]{1,0:T(8,128)(2,1)} %collective-permute-done.24.refs_1_, bf16[1792,128]{1,0:T(8,128)(2,1)} %collective-permute-done.25.refs_2_, ...), custom_call_target="tpu_custom_call", output_to_operand_aliasing={{0}: (9, {})} | custom-call | tf_op jit(solution)/shard_map/quantize/pallas_call | solution.py:262
  355.5 7.9 %quantize.7 = (bf16[1792,2048]{1,0:T(8,128)(2,1)}, f32[896,128]{1,0:T(8,128)}) custom-call(s32[1]{0:T(128)} %bitcast.place_ref, bf16[1792,128]{1,0:T(8,128)(2,1)} %bitcast.59, bf16[1792,128]{1,0:T(8,128)(2,1)} %copy-done.11, bf16[1792,128]{1,0:T(8,128)(2,1)} %copy-done.12, bf16[1792,128]{1,0:T(8,128)(2,1)} %copy-done.14, ...), custom_call_target="tpu_custom_call", output_to_operand_aliasing={{0}: (8, {})} | custom-call | tf_op jit(solution)/shard_map/quantize/pallas_call | solution.py:262
  364.2 6.4 %quantize.8 = (bf16[1792,2048]{1,0:T(8,128)(2,1)}, f32[1792,256]{1,0:T(8,128)}) custom-call(s32[1]{0:T(128)} %bitcast.place_ref, bf16[896,128]{1,0:T(8,128)(2,1)} %bitcast.99, bf16[896,128]{1,0:T(8,128)(2,1)} %collective-permute-done.30.refs_1_, bf16[896,128]{1,0:T(8,128)(2,1)} %copy-done.24, ...), custom_call_target="tpu_custom_call", output_to_operand_aliasing={{0}: (9, {}), {1}: (10, {})} | custom-call | tf_op jit(solution)/shard_map/quantize/pallas_call | solution.py:262
  371.3 6.4 %quantize.9 = (bf16[1792,2048]{1,0:T(8,128)(2,1)}, f32[1792,256]{1,0:T(8,128)}) custom-call(s32[1]{0:T(128)} %bitcast.place_ref, bf16[896,128]{1,0:T(8,128)(2,1)} %bitcast.97, bf16[896,128]{1,0:T(8,128)(2,1)} %copy-done.22, bf16[896,128]{1,0:T(8,128)(2,1)} %copy-done.23, ...), custom_call_target="tpu_custom_call", output_to_operand_aliasing={{0}: (9, {}), {1}: (10, {})} | custom-call | tf_op jit(solution)/shard_map/quantize/pallas_call | solution.py:262
  (151 shorter events, 45.5 us)
Async XLA Ops:
  13.3 50.9 %collective-permute-start.7 = (bf16[1280,128]{1,0:T(8,128)(2,1)}, bf16[1280,128]{1,0:T(8,128)(2,1)S(1)}, u32[]{:S(2)}, u32[]{:S(2)}) collective-permute-start(bf16[1280,128]{1,0:T(8,128)(2,1)} %get-tuple-element.113), channel_id=1, source_target_pairs={{0,1},{1,2},{2,3},{3,0},{4,5},{5,6},{6,7},{7,4},{8,9},{9,10},{10,1... | collective-permute-start | bytes 983048 | tf_op jit(solution)/shard_map/ppermute | solution.py:381
  16.3 47.9 %collective-permute-start.9 = (bf16[1280,128]{1,0:T(8,128)(2,1)}, bf16[1280,128]{1,0:T(8,128)(2,1)S(1)}, u32[]{:S(2)}, u32[]{:S(2)}) collective-permute-start(bf16[1280,128]{1,0:T(8,128)(2,1)} %get-tuple-element.115), channel_id=1, source_target_pairs={{0,2},{1,3},{2,0},{3,1},{4,6},{5,7},{6,4},{7,5},{8,10},{9,11},{10,... | collective-permute-start | bytes 983048 | tf_op jit(solution)/shard_map/ppermute | solution.py:381
  18.9 45.3 %collective-permute-start.11 = (bf16[1280,128]{1,0:T(8,128)(2,1)}, bf16[1280,128]{1,0:T(8,128)(2,1)S(1)}, u32[]{:S(2)}, u32[]{:S(2)}) collective-permute-start(bf16[1280,128]{1,0:T(8,128)(2,1)} %get-tuple-element.117), channel_id=1, source_target_pairs={{0,3},{1,0},{2,1},{3,2},{4,7},{5,4},{6,5},{7,6},{8,11},{9,8},{10,9... | collective-permute-start | bytes 983048 | tf_op jit(solution)/shard_map/ppermute | solution.py:381
  20.2 23.9 %collective-permute-start.6 = (bf16[512,128]{1,0:T(8,128)(2,1)S(1)}, bf16[512,128]{1,0:T(8,128)(2,1)S(1)}, u32[]{:S(2)}, u32[]{:S(2)}) collective-permute-start(bf16[512,128]{1,0:T(8,128)(2,1)S(1)} %copy-done.34), channel_id=1, source_target_pairs={{0,1},{1,2},{2,3},{3,0},{4,5},{5,6},{6,7},{7,4},{8,9},{9,10},{10,1... | collective-permute-start | bytes 393224 | tf_op jit(solution)/shard_map/ppermute | solution.py:381
  20.9 35.0 %collective-permute-start.8 = (bf16[512,128]{1,0:T(8,128)(2,1)S(1)}, bf16[512,128]{1,0:T(8,128)(2,1)S(1)}, u32[]{:S(2)}, u32[]{:S(2)}) collective-permute-start(bf16[512,128]{1,0:T(8,128)(2,1)S(1)} %copy-done.33), channel_id=1, source_target_pairs={{0,2},{1,3},{2,0},{3,1},{4,6},{5,7},{6,4},{7,5},{8,10},{9,11},{10,... | collective-permute-start | bytes 393224 | tf_op jit(solution)/shard_map/ppermute | solution.py:381
  44.1 14.5 %collective-permute-start.10 = (bf16[512,128]{1,0:T(8,128)(2,1)S(1)}, bf16[512,128]{1,0:T(8,128)(2,1)S(1)}, u32[]{:S(2)}, u32[]{:S(2)}) collective-permute-start(bf16[512,128]{1,0:T(8,128)(2,1)S(1)} %copy-done.32), channel_id=1, source_target_pairs={{0,3},{1,0},{2,1},{3,2},{4,7},{5,4},{6,5},{7,6},{8,11},{9,8},{10,9... | collective-permute-start | bytes 393224 | tf_op jit(solution)/shard_map/ppermute | solution.py:381
  56.5 16.4 %collective-permute-start = (bf16[1792,128]{1,0:T(8,128)(2,1)}, bf16[1792,128]{1,0:T(8,128)(2,1)S(1)}, u32[]{:S(2)}, u32[]{:S(2)}) collective-permute-start(bf16[1792,128]{1,0:T(8,128)(2,1)} %get-tuple-element.102), channel_id=1, source_target_pairs={{0,1},{1,2},{2,3},{3,0},{4,5},{5,6},{6,7},{7,4},{8,9},{9,10},{10,1... | collective-permute-start | bytes 1376264 | tf_op jit(solution)/shard_map/ppermute | solution.py:381
  59.3 33.4 %collective-permute-start.1 = (bf16[1792,128]{1,0:T(8,128)(2,1)}, bf16[1792,128]{1,0:T(8,128)(2,1)S(1)}, u32[]{:S(2)}, u32[]{:S(2)}) collective-permute-start(bf16[1792,128]{1,0:T(8,128)(2,1)} %get-tuple-element.103), channel_id=1, source_target_pairs={{0,2},{1,3},{2,0},{3,1},{4,6},{5,7},{6,4},{7,5},{8,10},{9,11},{10,... | collective-permute-start | bytes 1376264 | tf_op jit(solution)/shard_map/ppermute | solution.py:381
  64.2 28.5 %collective-permute-start.2 = (bf16[1792,128]{1,0:T(8,128)(2,1)}, bf16[1792,128]{1,0:T(8,128)(2,1)S(1)}, u32[]{:S(2)}, u32[]{:S(2)}) collective-permute-start(bf16[1792,128]{1,0:T(8,128)(2,1)} %get-tuple-element.104), channel_id=1, source_target_pairs={{0,3},{1,0},{2,1},{3,2},{4,7},{5,4},{6,5},{7,6},{8,11},{9,8},{10,9... | collective-permute-start | bytes 1376264 | tf_op jit(solution)/shard_map/ppermute | solution.py:381
  65.0 57.7 %collective-permute-start.12 = (bf16[1792,128]{1,0:T(8,128)(2,1)}, bf16[1792,128]{1,0:T(8,128)(2,1)S(1)}, u32[]{:S(2)}, u32[]{:S(2)}) collective-permute-start(bf16[1792,128]{1,0:T(8,128)(2,1)} %get-tuple-element.118), channel_id=1, source_target_pairs={{0,1},{1,2},{2,3},{3,0},{4,5},{5,6},{6,7},{7,4},{8,9},{9,10},{10,1... | collective-permute-start | bytes 1376264 | tf_op jit(solution)/shard_map/ppermute | solution.py:381
  67.0 96.1 %collective-permute-start.13 = (bf16[1792,128]{1,0:T(8,128)(2,1)}, bf16[1792,128]{1,0:T(8,128)(2,1)S(1)}, u32[]{:S(2)}, u32[]{:S(2)}) collective-permute-start(bf16[1792,128]{1,0:T(8,128)(2,1)} %get-tuple-element.119), channel_id=1, source_target_pairs={{0,2},{1,3},{2,0},{3,1},{4,6},{5,7},{6,4},{7,5},{8,10},{9,11},{10,... | collective-permute-start | bytes 1376264 | tf_op jit(solution)/shard_map/ppermute | solution.py:381
  72.9 90.2 %collective-permute-start.14 = (bf16[1792,128]{1,0:T(8,128)(2,1)}, bf16[1792,128]{1,0:T(8,128)(2,1)S(1)}, u32[]{:S(2)}, u32[]{:S(2)}) collective-permute-start(bf16[1792,128]{1,0:T(8,128)(2,1)} %get-tuple-element.120), channel_id=1, source_target_pairs={{0,3},{1,0},{2,1},{3,2},{4,7},{5,4},{6,5},{7,6},{8,11},{9,8},{10,9... | collective-permute-start | bytes 1376264 | tf_op jit(solution)/shard_map/ppermute | solution.py:381
  92.7 79.5 %collective-permute-start.3 = (bf16[1792,128]{1,0:T(8,128)(2,1)}, bf16[1792,128]{1,0:T(8,128)(2,1)}, u32[]{:S(2)}, u32[]{:S(2)}) collective-permute-start(bf16[1792,128]{1,0:T(8,128)(2,1)} %get-tuple-element.105), channel_id=1, source_target_pairs={{0,1},{1,2},{2,3},{3,0},{4,5},{5,6},{6,7},{7,4},{8,9},{9,10},{10,1... | collective-permute-start | bytes 1376264 | tf_op jit(solution)/shard_map/ppermute | solution.py:381
  122.7 49.5 %collective-permute-start.4 = (bf16[1792,128]{1,0:T(8,128)(2,1)}, bf16[1792,128]{1,0:T(8,128)(2,1)}, u32[]{:S(2)}, u32[]{:S(2)}) collective-permute-start(bf16[1792,128]{1,0:T(8,128)(2,1)} %get-tuple-element.106), channel_id=1, source_target_pairs={{0,2},{1,3},{2,0},{3,1},{4,6},{5,7},{6,4},{7,5},{8,10},{9,11},{10,... | collective-permute-start | bytes 1376264 | tf_op jit(solution)/shard_map/ppermute | solution.py:381
  122.7 49.5 %collective-permute-start.5 = (bf16[1792,128]{1,0:T(8,128)(2,1)}, bf16[1792,128]{1,0:T(8,128)(2,1)}, u32[]{:S(2)}, u32[]{:S(2)}) collective-permute-start(bf16[1792,128]{1,0:T(8,128)(2,1)} %get-tuple-element.107), channel_id=1, source_target_pairs={{0,3},{1,0},{2,1},{3,2},{4,7},{5,4},{6,5},{7,6},{8,11},{9,8},{10,9... | collective-permute-start | bytes 1376264 | tf_op jit(solution)/shard_map/ppermute | solution.py:381
  180.2 13.9 %collective-permute-start.20 = (f32[16,128]{1,0:T(8,128)}, f32[16,128]{1,0:T(8,128)S(1)}, u32[]{:S(2)}, u32[]{:S(2)}) collective-permute-start(f32[16,128]{1,0:T(8,128)} %get-tuple-element.140), channel_id=1, source_target_pairs={{0,3},{1,0},{2,1},{3,2},{4,7},{5,4},{6,5},{7,6},{8,11},{9,8},{10,9... | collective-permute-start | bytes 24584 | tf_op jit(solution)/shard_map/ppermute | solution.py:381
  189.7 15.8 %collective-permute-start.27 = (bf16[1792,128]{1,0:T(8,128)(2,1)S(1)}, bf16[1792,128]{1,0:T(8,128)(2,1)}, u32[]{:S(2)}, u32[]{:S(2)}) collective-permute-start(bf16[1792,128]{1,0:T(8,128)(2,1)S(1)} %bitcast.71), channel_id=1, source_target_pairs={{0,1},{1,2},{2,3},{3,0},{4,5},{5,6},{6,7},{7,4},{8,9},{9,10},{10,1... | collective-permute-start | bytes 1376264 | tf_op jit(solution)/shard_map/ppermute | solution.py:381
  191.3 33.9 %collective-permute-start.28 = (bf16[1792,128]{1,0:T(8,128)(2,1)S(1)}, bf16[1792,128]{1,0:T(8,128)(2,1)}, u32[]{:S(2)}, u32[]{:S(2)}) collective-permute-start(bf16[1792,128]{1,0:T(8,128)(2,1)S(1)} %bitcast.74), channel_id=1, source_target_pairs={{0,2},{1,3},{2,0},{3,1},{4,6},{5,7},{6,4},{7,5},{8,10},{9,11},{10,... | collective-permute-start | bytes 1376264 | tf_op jit(solution)/shard_map/ppermute | solution.py:381
  194.2 56.3 %collective-permute-start.29 = (bf16[1792,128]{1,0:T(8,128)(2,1)S(1)}, bf16[1792,128]{1,0:T(8,128)(2,1)}, u32[]{:S(2)}, u32[]{:S(2)}) collective-permute-start(bf16[1792,128]{1,0:T(8,128)(2,1)S(1)} %bitcast.77), channel_id=1, source_target_pairs={{0,3},{1,0},{2,1},{3,2},{4,7},{5,4},{6,5},{7,6},{8,11},{9,8},{10,9... | collective-permute-start | bytes 1376264 | tf_op jit(solution)/shard_map/ppermute | solution.py:381
  194.2 60.2 %collective-permute-start.24 = (bf16[1792,128]{1,0:T(8,128)(2,1)S(1)}, bf16[1792,128]{1,0:T(8,128)(2,1)}, u32[]{:S(2)}, u32[]{:S(2)}) collective-permute-start(bf16[1792,128]{1,0:T(8,128)(2,1)S(1)} %bitcast.86), channel_id=1, source_target_pairs={{0,1},{1,2},{2,3},{3,0},{4,5},{5,6},{6,7},{7,4},{8,9},{9,10},{10,1... | collective-permute-start | bytes 1376264 | tf_op jit(solution)/shard_map/ppermute | solution.py:381
  196.2 85.9 %collective-permute-start.25 = (bf16[1792,128]{1,0:T(8,128)(2,1)}, bf16[1792,128]{1,0:T(8,128)(2,1)}, u32[]{:S(2)}, u32[]{:S(2)}) collective-permute-start(bf16[1792,128]{1,0:T(8,128)(2,1)} %bitcast.87), channel_id=1, source_target_pairs={{0,2},{1,3},{2,0},{3,1},{4,6},{5,7},{6,4},{7,5},{8,10},{9,11},{10,... | collective-permute-start | bytes 1376264 | tf_op jit(solution)/shard_map/ppermute | solution.py:381
  205.5 110.6 %collective-permute-start.26 = (bf16[1792,128]{1,0:T(8,128)(2,1)S(1)}, bf16[1792,128]{1,0:T(8,128)(2,1)S(1)}, u32[]{:S(2)}, u32[]{:S(2)}) collective-permute-start(bf16[1792,128]{1,0:T(8,128)(2,1)S(1)} %bitcast.83), channel_id=1, source_target_pairs={{0,3},{1,0},{2,1},{3,2},{4,7},{5,4},{6,5},{7,6},{8,11},{9,8},{10,9... | collective-permute-start | bytes 1376264 | tf_op jit(solution)/shard_map/ppermute | solution.py:381
  225.2 94.4 %collective-permute-start.21 = (bf16[1792,128]{1,0:T(8,128)(2,1)}, bf16[1792,128]{1,0:T(8,128)(2,1)S(1)}, u32[]{:S(2)}, u32[]{:S(2)}) collective-permute-start(bf16[1792,128]{1,0:T(8,128)(2,1)} %bitcast.90), channel_id=1, source_target_pairs={{0,1},{1,2},{2,3},{3,0},{4,5},{5,6},{6,7},{7,4},{8,9},{9,10},{10,1... | collective-permute-start | bytes 1376264 | tf_op jit(solution)/shard_map/ppermute | solution.py:381
  250.5 72.0 %collective-permute-start.22 = (bf16[1792,128]{1,0:T(8,128)(2,1)S(1)}, bf16[1792,128]{1,0:T(8,128)(2,1)S(1)}, u32[]{:S(2)}, u32[]{:S(2)}) collective-permute-start(bf16[1792,128]{1,0:T(8,128)(2,1)S(1)} %bitcast.80), channel_id=1, source_target_pairs={{0,2},{1,3},{2,0},{3,1},{4,6},{5,7},{6,4},{7,5},{8,10},{9,11},{10,... | collective-permute-start | bytes 1376264 | tf_op jit(solution)/shard_map/ppermute | solution.py:381
  254.5 68.0 %collective-permute-start.23 = (bf16[1792,128]{1,0:T(8,128)(2,1)S(1)}, bf16[1792,128]{1,0:T(8,128)(2,1)S(1)}, u32[]{:S(2)}, u32[]{:S(2)}) collective-permute-start(bf16[1792,128]{1,0:T(8,128)(2,1)S(1)} %bitcast.68), channel_id=1, source_target_pairs={{0,3},{1,0},{2,1},{3,2},{4,7},{5,4},{6,5},{7,6},{8,11},{9,8},{10,9... | collective-permute-start | bytes 1376264 | tf_op jit(solution)/shard_map/ppermute | solution.py:381
  282.1 34.0 %collective-permute-start.30 = (bf16[896,128]{1,0:T(8,128)(2,1)}, bf16[896,128]{1,0:T(8,128)(2,1)}, u32[]{:S(2)}, u32[]{:S(2)}) collective-permute-start(bf16[896,128]{1,0:T(8,128)(2,1)} %bitcast.43.refs_7_), channel_id=1, source_target_pairs={{0,1},{1,2},{2,3},{3,0},{4,5},{5,6},{6,7},{7,4},{8,9},{9,10},{10,1... | collective-permute-start | bytes 688136 | tf_op jit(solution)/shard_map/ppermute | solution.py:381
  316.1 54.4 %collective-permute-start.15 = (bf16[896,128]{1,0:T(8,128)(2,1)}, bf16[896,128]{1,0:T(8,128)(2,1)S(1)}, u32[]{:S(2)}, u32[]{:S(2)}) collective-permute-start(bf16[896,128]{1,0:T(8,128)(2,1)} %bitcast.122), channel_id=1, source_target_pairs={{0,1},{1,2},{2,3},{3,0},{4,5},{5,6},{6,7},{7,4},{8,9},{9,10},{10,1... | collective-permute-start | bytes 688136 | tf_op jit(solution)/shard_map/ppermute | solution.py:381
  316.2 54.4 %collective-permute-start.16 = (bf16[896,128]{1,0:T(8,128)(2,1)}, bf16[896,128]{1,0:T(8,128)(2,1)S(1)}, u32[]{:S(2)}, u32[]{:S(2)}) collective-permute-start(bf16[896,128]{1,0:T(8,128)(2,1)} %bitcast.120), channel_id=1, source_target_pairs={{0,2},{1,3},{2,0},{3,1},{4,6},{5,7},{6,4},{7,5},{8,10},{9,11},{10,... | collective-permute-start | bytes 688136 | tf_op jit(solution)/shard_map/ppermute | solution.py:381
  319.6 51.0 %collective-permute-start.17 = (bf16[896,128]{1,0:T(8,128)(2,1)S(1)}, bf16[896,128]{1,0:T(8,128)(2,1)}, u32[]{:S(2)}, u32[]{:S(2)}) collective-permute-start(bf16[896,128]{1,0:T(8,128)(2,1)S(1)} %bitcast.118), channel_id=1, source_target_pairs={{0,3},{1,0},{2,1},{3,2},{4,7},{5,4},{6,5},{7,6},{8,11},{9,8},{10,9... | collective-permute-start | bytes 688136 | tf_op jit(solution)/shard_map/ppermute | solution.py:381
  322.5 40.9 %collective-permute-start.31 = (bf16[896,128]{1,0:T(8,128)(2,1)}, bf16[896,128]{1,0:T(8,128)(2,1)S(1)}, u32[]{:S(2)}, u32[]{:S(2)}) collective-permute-start(bf16[896,128]{1,0:T(8,128)(2,1)} %bitcast.126), channel_id=1, source_target_pairs={{0,2},{1,3},{2,0},{3,1},{4,6},{5,7},{6,4},{7,5},{8,10},{9,11},{10,... | collective-permute-start | bytes 688136 | tf_op jit(solution)/shard_map/ppermute | solution.py:381
  322.5 40.9 %collective-permute-start.32 = (bf16[896,128]{1,0:T(8,128)(2,1)}, bf16[896,128]{1,0:T(8,128)(2,1)S(1)}, u32[]{:S(2)}, u32[]{:S(2)}) collective-permute-start(bf16[896,128]{1,0:T(8,128)(2,1)} %bitcast.124), channel_id=1, source_target_pairs={{0,3},{1,0},{2,1},{3,2},{4,7},{5,4},{6,5},{7,6},{8,11},{9,8},{10,9... | collective-permute-start | bytes 688136 | tf_op jit(solution)/shard_map/ppermute | solution.py:381
  326.7 26.6 %all-to-all-start = ((f32[32,1,1]{2,1,0:T(1,128)}), f32[32,1,1]{2,1,0:T(1,128)S(1)}, u32[]{:S(2)}, u32[]{:S(2)}) async-start(f32[32,1,1]{2,1,0:T(1,128)} %broadcast_in_dim.40), calls=%async_computation | async-start | bytes 32768 | tf_op jit(solution)/shard_map/all_to_all | solution.py:451
  (37 other events, 1235.9 us)

commit v3 on v2

--- a/solution.py
+++ b/solution.py
@@ -230,7 +230,7 @@
                 error_ref[pl.ds(band + start, LOW), :] = jnp.where(left, pltpu.roll(other, lanes, 1), error)
             return 0
 
-        lax.fori_loop(0, band // LOW, one, 0, unroll=2)
+        lax.fori_loop(0, band // LOW, one, 0, unroll=True)
 
     in_specs = [pl.BlockSpec(memory_space=pltpu.SMEM)]
     for p in pieces:
@@ -381,16 +381,17 @@
         return lax.ppermute(x, "row", [(k, (k + shift) % ring) for k in range(ring)])
 
     column_args = (weights[0], left_bits, right_bits, place, ring, chunks)
-    start_rows = max(blocks_here * 2 // 7, 1) * HB
-    early, whole = column_transform(*column_args, 0, start_rows, start_rows, None)
-    left_rows = local_rows - start_rows
-    late, whole = column_transform(
-        *column_args, start_rows, left_rows, math.gcd(start_rows, left_rows), whole
-    )
+    small, middle = blocks_here // 7, blocks_here * 2 // 7
+    thirds = (small, middle, blocks_here - small - middle)
+    early, whole, first_row = [], None, 0
+    for count in thirds:
+        count *= HB
+        piece_rows, whole = column_transform(*column_args, first_row, count, math.gcd(first_row, count) or count, whole)
+        early.append(piece_rows)
+        first_row += count
     splits = (blocks_here // 2, blocks_here - blocks_here // 2)
-    halves = [n * HB for n in splits]
-    step_rows = math.gcd(*halves)
-    outgoing = [[[early[s], late[s]] for s in range(ring)]]
+    step_rows = math.gcd(*(n * HB for n in splits))
+    outgoing = [[[rows[s] for rows in early] for s in range(ring)]]
     outgoing += [[[whole[c * ring + s]] for s in range(ring)] for c in range(chunks - 1)]
     mixer = mixer_table(mine, ring, blocks_here)
     band_columns = ring * piece
@@ -408,7 +409,7 @@
             leaving, received[chunk - AHEAD] = lax.optimization_barrier((leaving, received[chunk - AHEAD]))
         arrived = [[] for _ in range(1, ring)]
         for part in range(len(leaving[0])):
-            for s in range(1, ring):
+            for s in sorted(range(1, ring), key=lambda s: abs(s - ring // 2)):
                 arrived[s - 1].append(send(leaving[s - 1][part], s))
         received.append(arrived)
     peak = jnp.zeros((GROUPS, 128), jnp.float32)
@@ -438,7 +439,7 @@
     scale_own = octet_rows(own_scale.reshape(chunks * piece))
 
     fine = even_tile(step_rows, TILE2)
-    ranges = [(0, halves[0]), (halves[0], halves[1])]
+    ranges = [(sum(splits[:k]) * HB, n * HB) for k, n in enumerate(splits)]
     shares = []
     for part, (first_row, count) in enumerate(ranges):
         own_pieces = [[k[s][part % len(k[s])] for k in kept] for s in range(ring)]

time: 379 us -> 378 us (level)
  starting transfers between devices: 126 us -> 138 us
  waiting for transfers between devices: 104 us -> 96 us
  Pallas kernels: 107 us -> 102 us
    ppermute x33 -> x36, starting transfers between devices: 121 us -> 133 us  [send(): lax.ppermute(x, 'row', [(k, (k + shift) % ring) for k in range(ring)])]
    ppermute x33 -> x36, waiting for transfers between devices: 102 us -> 89.4 us  [send(): lax.ppermute(x, 'row', [(k, (k + shift) % ring) for k in range(ring)])]
    pallas_call x5, Pallas kernels: 38.5 us -> 32.6 us  [quantize(): pl.pallas_call(kernel, grid=(rows // tile,), in_specs=in_specs, out_specs...]
    all_to_all x1, waiting for transfers between devices: 2.54 us -> 6.59 us  [body(): every_error = lax.all_to_all(copies, ('expert', 'row'), 0, 0)]
    pallas_call x2 -> x3, Pallas kernels: 12.6 us -> 13.8 us  [column_transform(): pl.pallas_call(kernel, grid=(rows // tile,), in_specs=in_specs, out_specs...]
  transfers between devices with their start and end apart: 34 -> 37, of which waited for: 9 -> 8; matrix products, arithmetic and copies ran while one was open for 9% -> 9% of each run, Pallas kernels for 21% -> 23%
where the time goes in v3:
time: 378 us; the launch traced here: 377 us
  starting transfers between devices  138 us (37%)
  Pallas kernels  102 us (27%)
  waiting for transfers between devices  96 us (25%)
  other arithmetic  30.4 us (8%)
  local copies, waits for them, and re-layouts  7.25 us (2%)
    ppermute x36, starting transfers between devices, send(): lax.ppermute(x, 'row', [(k, (k + shift) % ring) for k in range(ring)])  133 us
    ppermute x36, waiting for transfers between devices, send(): lax.ppermute(x, 'row', [(k, (k + shift) % ring) for k in range(ring)])  89.4 us
    pallas_call x5, Pallas kernels, quantize(): pl.pallas_call(kernel, grid=(rows // tile,), in_specs=in_specs, out_specs...  32.6 us
    pallas_call x4, Pallas kernels, row_mix(): pl.pallas_call(kernel, out_shape=[jax.ShapeDtypeStruct((n, high, LOW, wid...  31.9 us
    pallas_call x2, Pallas kernels, lattice_sum(): pl.pallas_call(kernel, grid=(rows // tile,), in_specs=in_specs, out_specs...  23.7 us
    convert_element_type x1, other arithmetic, mixer_table(): return jnp.where(common & 1 == 0, table, -table).astype(jnp.bfloat16)  20.4 us
    pallas_call x3, Pallas kernels, column_transform(): pl.pallas_call(kernel, grid=(rows // tile,), in_specs=in_specs, out_specs...  13.8 us
  transfers between devices with their start and end apart: 37, of which 8 were waited for; matrix products, arithmetic and copies ran while one was open for 9% of the time, Pallas kernels for 23%

profile of v3, /device:TPU:0, one launch (start us, length us, event | category | flops | bytes accessed | tf_op | source)
XLA Modules:
  0.0 377.5 jit_solution(10137355847238486825)
XLA Ops:
  9.4 4.1 %column_transform.4 = (bf16[512,128]{1,0:T(8,128)(2,1)}, bf16[512,128]{1,0:T(8,128)(2,1)}, bf16[512,128]{1,0:T(8,128)(2,1)}, bf16[512,128]{1,0:T(8,128)(2,1)}, b...) custom-call(s32[1]{0:T(128)} %bitcast.place_ref, ...), custom_call_target="tpu_custom_call", output_to_operand_aliasing={{4}: (4, {}), {5}: (5, {}), {6}: (6, {}), {7}: (7, {}), {8}... | custom-call | tf_op jit(solution)/shard_map/column_transform/pallas_call | solution.py:104
  13.5 6.7 %column_transform.5 = (bf16[1024,128]{1,0:T(8,128)(2,1)}, bf16[1024,128]{1,0:T(8,128)(2,1)}, bf16[1024,128]{1,0:T(8,128)(2,1)}, bf16[1024,128]{1,0:T(8,128)(2,1)...) custom-call(s32[1]{0:T(128)} %bitcast.place_ref, ...), custom_call_target="tpu_custom_call", output_to_operand_aliasing={{4}: (4, {}), {5}: (5, {}), {6}: (6, {}), {7}: (7, {}), {8}... | custom-call | tf_op jit(solution)/shard_map/column_transform/pallas_call | solution.py:104
  21.0 3.5 collective-permute-start.11
  26.6 15.8 %collective-permute-done.12 = bf16[256,128]{1,0:T(8,128)(2,1)S(1)} collective-permute-done((bf16[256,128]{1,0:T(8,128)(2,1)S(1)}, bf16[256,128]{1,0:T(8,128)(2,1)S(1)}, u32[]{:S(2)}, u32[]{:S(2)}) %collective-permute-start.12) | collective-permute-done | bytes 65568 | tf_op jit(solution)/shard_map/ppermute | solution.py:381
  43.0 5.2 %collective-permute-start.10 = (bf16[512,128]{1,0:T(8,128)(2,1)S(1)}, bf16[512,128]{1,0:T(8,128)(2,1)S(1)}, u32[]{:S(2)}, u32[]{:S(2)}) collective-permute-start(bf16[512,128]{1,0:T(8,128)(2,1)S(1)} %copy-done.36), channel_id=1, source_target_pairs={{0,2},{1,3},{2,0},{3,1},{4,6},{5,7},{6,4},{7,5},{8,10},{9,11},{10,... | collective-permute-start | bytes 393224 | tf_op jit(solution)/shard_map/ppermute | solution.py:381
  54.5 3.6 collective-permute-start
  63.9 8.8 %collective-permute-done = bf16[1792,128]{1,0:T(8,128)(2,1)S(1)} collective-permute-done((bf16[1792,128]{1,0:T(8,128)(2,1)}, bf16[1792,128]{1,0:T(8,128)(2,1)S(1)}, u32[]{:S(2)}, u32[]{:S(2)}) %collective-permute-start) | collective-permute-done | bytes 458784 | tf_op jit(solution)/shard_map/ppermute | solution.py:381
  75.9 16.6 %collective-permute-done.1 = bf16[1792,128]{1,0:T(8,128)(2,1)S(1)} collective-permute-done((bf16[1792,128]{1,0:T(8,128)(2,1)}, bf16[1792,128]{1,0:T(8,128)(2,1)S(1)}, u32[]{:S(2)}, u32[]{:S(2)}) %collective-permute-start.1) | collective-permute-done | bytes 458784 | tf_op jit(solution)/shard_map/ppermute | solution.py:381
  92.4 30.1 %collective-permute-start.3 = (bf16[1792,128]{1,0:T(8,128)(2,1)}, bf16[1792,128]{1,0:T(8,128)(2,1)}, u32[]{:S(2)}, u32[]{:S(2)}) collective-permute-start(bf16[1792,128]{1,0:T(8,128)(2,1)} %get-tuple-element.136), channel_id=1, source_target_pairs={{0,1},{1,2},{2,3},{3,0},{4,5},{5,6},{6,7},{7,4},{8,9},{9,10},{10,1... | collective-permute-start | bytes 1376264 | tf_op jit(solution)/shard_map/ppermute | solution.py:381
  124.9 20.4 %fusion.42.refs_12_.refs_4_ = bf16[896,896]{1,0:T(8,128)(2,1)} fusion(s32[896]{0:T(1024)S(1)} %get-tuple-element.216, s32[896]{0:T(1024)S(1)} %get-tuple-element.217, s32[896]{0:T(1024)S(1)} %get-tuple-element.215, s32[896]{0:T(1024)S(1)} %get-tuple-element.222, s32[]{:T(128)} %axis_index.22, s32[896]{0:T(1024)S(1)} %get-tuple-element.218, ...), kind=kLoop, calls=%fused_computation.87 | loop fusion | flops 69042176 | bytes 1629828 | tf_op jit(solution)/shard_map/convert_element_type | solution.py:352
  147.1 7.9 %row_mix.4 = (bf16[14,8,16,128]{3,2,1,0:T(8,128)(2,1)}, bf16[14,8,16,128]{3,2,1,0:T(8,128)(2,1)}, bf16[14,8,16,128]{3,2,1,0:T(8,128)(2,1)}, bf16[14,8,16,128]{3,2,1,0:T(8,128)(2,1)}, f32[16,128]{1,0:T(8,128)}) custom-call(bf16[2,8,16,128]{3,2,1,0:T(8,128)(2,1)} %bitcast.136, bf16[4,8,16,128]{3,2,1,0:T(8,128)(2,1)} %bitcast.132, ...), custom_call_target="tpu_custom_call" | custom-call | tf_op jit(solution)/shard_map/row_mix/pallas_call | solution.py:160
  155.1 7.9 %row_mix.5 = (bf16[14,8,16,128]{3,2,1,0:T(8,128)(2,1)}, bf16[14,8,16,128]{3,2,1,0:T(8,128)(2,1)}, bf16[14,8,16,128]{3,2,1,0:T(8,128)(2,1)}, bf16[14,8,16,128]{3,2,1,0:T(8,128)(2,1)}, f32[16,128]{1,0:T(8,128)}) custom-call(bf16[14,8,16,128]{3,2,1,0:T(8,128)(2,1)} %bitcast.71, bf16[14,8,16,128]{3,2,1,0:T(8,128)(2,1)} %bitcast.106, ...), custom_call_target="tpu_custom_call" | custom-call | tf_op jit(solution)/shard_map/row_mix/pallas_call | solution.py:160
  164.0 8.1 %row_mix.6 = (bf16[14,8,16,128]{3,2,1,0:T(8,128)(2,1)}, bf16[14,8,16,128]{3,2,1,0:T(8,128)(2,1)}, bf16[14,8,16,128]{3,2,1,0:T(8,128)(2,1)}, bf16[14,8,16,128]{3,2,1,0:T(8,128)(2,1)}, f32[16,128]{1,0:T(8,128)}) custom-call(bf16[14,8,16,128]{3,2,1,0:T(8,128)(2,1)} %bitcast.72, bf16[14,8,16,128]{3,2,1,0:T(8,128)(2,1)} %bitcast.108, ...), custom_call_target="tpu_custom_call" | custom-call | tf_op jit(solution)/shard_map/row_mix/pallas_call | solution.py:160
  172.1 8.0 %row_mix.7 = (bf16[7,8,16,128]{3,2,1,0:T(8,128)(2,1)}, bf16[7,8,16,128]{3,2,1,0:T(8,128)(2,1)}, bf16[7,8,16,128]{3,2,1,0:T(8,128)(2,1)}, bf16[7,8,16,128]{3,2,1,...) custom-call(bf16[14,8,16,128]{3,2,1,0:T(8,128)(2,1)} %bitcast.73, ...), custom_call_target="tpu_custom_call" | custom-call | tf_op jit(solution)/shard_map/row_mix/pallas_call | solution.py:160
  180.1 7.5 %collective-permute-start.23 = (f32[16,128]{1,0:T(8,128)}, f32[16,128]{1,0:T(8,128)S(1)}, u32[]{:S(2)}, u32[]{:S(2)}) collective-permute-start(f32[16,128]{1,0:T(8,128)} %get-tuple-element.178), channel_id=1, source_target_pairs={{0,3},{1,0},{2,1},{3,2},{4,7},{5,4},{6,5},{7,6},{8,11},{9,8},{10,9... | collective-permute-start | bytes 24584 | tf_op jit(solution)/shard_map/ppermute | solution.py:381
  191.2 3.5 collective-permute-start.31
  196.8 5.4 %fusion.22 = (bf16[1024,1024]{1,0:T(8,128)(2,1)}, bf16[1024,1024]{1,0:T(8,128)(2,1)}) fusion(s32[1024]{0:T(1024)S(1)} %get-tuple-element.223, s32[1024]{0:T(1024)S(1)} %get-tuple-element.226, s32[1024]{0:T(1024)S(1)} %get-tuple-element.224, s32[1024]{0:T(1024)S(1)} %get-tuple-element.225, pred[1024]{0:T(1024)(128)(4,1)S(1)} %get-tuple-element.227, ...), kind=kLoop, calls=%fused_computation.67 | loop fusion | flops 83886080 | bytes 4212740 | tf_op jit(solution)/shard_map/convert_element_type | solution.py:362
  208.3 17.4 %collective-permute-done.31.refs_2_ = bf16[1792,128]{1,0:T(8,128)(2,1)} collective-permute-done((bf16[1792,128]{1,0:T(8,128)(2,1)S(1)}, bf16[1792,128]{1,0:T(8,128)(2,1)}, u32[]{:S(2)}, u32[]{:S(2)}) %collective-permute-start.31) | collective-permute-done | bytes 458784 | tf_op jit(solution)/shard_map/ppermute | solution.py:381
  225.7 25.9 %collective-permute-start.24 = (bf16[1792,128]{1,0:T(8,128)(2,1)}, bf16[1792,128]{1,0:T(8,128)(2,1)S(1)}, u32[]{:S(2)}, u32[]{:S(2)}) collective-permute-start(bf16[1792,128]{1,0:T(8,128)(2,1)} %bitcast.98), channel_id=1, source_target_pairs={{0,1},{1,2},{2,3},{3,0},{4,5},{5,6},{6,7},{7,4},{8,9},{9,10},{10,1... | collective-permute-start | bytes 1376264 | tf_op jit(solution)/shard_map/ppermute | solution.py:381
  251.6 4.0 %collective-permute-start.25 = (bf16[1792,128]{1,0:T(8,128)(2,1)S(1)}, bf16[1792,128]{1,0:T(8,128)(2,1)S(1)}, u32[]{:S(2)}, u32[]{:S(2)}) collective-permute-start(bf16[1792,128]{1,0:T(8,128)(2,1)S(1)} %bitcast.88), channel_id=1, source_target_pairs={{0,2},{1,3},{2,0},{3,1},{4,6},{5,7},{6,4},{7,5},{8,10},{9,11},{10,... | collective-permute-start | bytes 1376264 | tf_op jit(solution)/shard_map/ppermute | solution.py:381
  258.7 24.5 %collective-permute-done.28.refs_2_ = bf16[1792,128]{1,0:T(8,128)(2,1)} collective-permute-done((bf16[1792,128]{1,0:T(8,128)(2,1)}, bf16[1792,128]{1,0:T(8,128)(2,1)}, u32[]{:S(2)}, u32[]{:S(2)}) %collective-permute-start.28) | collective-permute-done | bytes 458784 | tf_op jit(solution)/shard_map/ppermute | solution.py:381
  283.2 8.7 %collective-permute-start.33 = (bf16[896,128]{1,0:T(8,128)(2,1)}, bf16[896,128]{1,0:T(8,128)(2,1)}, u32[]{:S(2)}, u32[]{:S(2)}) collective-permute-start(bf16[896,128]{1,0:T(8,128)(2,1)} %bitcast.47.refs_7_), channel_id=1, source_target_pairs={{0,1},{1,2},{2,3},{3,0},{4,5},{5,6},{6,7},{7,4},{8,9},{9,10},{10,1... | collective-permute-start | bytes 688136 | tf_op jit(solution)/shard_map/ppermute | solution.py:381
  292.9 11.8 %lattice_sum.2 = f32[16,128]{1,0:T(8,128)} custom-call(s32[1]{0:T(128)} %bitcast.place_ref, bf16[1792,128]{1,0:T(8,128)(2,1)} %bitcast.62, bf16[1792,128]{1,0:T(8,128)(2,1)} %bitcast.68, bf16[1792,128]{1,0:T(8,128)(2,1)} %bitcast.65, bf16[896,128]{1,0:T(8,128)(2,1)} %bitcast.103, bf16[1792,128]{1,0:T(8,128)(2,1)} %bitcast.74, bf16[1792,128]{1,0:T(8,128)(2,1)} %bitcast.92, ...), custom_call_target="tpu_custom_call" | custom-call | tf_op jit(solution)/shard_map/lattice_sum/pallas_call | solution.py:328
  304.7 11.9 %lattice_sum.3 = f32[16,128]{1,0:T(8,128)} custom-call(s32[1]{0:T(128)} %bitcast.place_ref, bf16[1792,128]{1,0:T(8,128)(2,1)} %bitcast.63, bf16[1792,128]{1,0:T(8,128)(2,1)} %bitcast.69, bf16[1792,128]{1,0:T(8,128)(2,1)} %bitcast.66, bf16[896,128]{1,0:T(8,128)(2,1)} %bitcast.101, bf16[1792,128]{1,0:T(8,128)(2,1)} %bitcast.75, bf16[1792,128]{1,0:T(8,128)(2,1)} %bitcast.93, ...), custom_call_target="tpu_custom_call" | custom-call | tf_op jit(solution)/shard_map/lattice_sum/pallas_call | solution.py:328
  316.7 3.4 collective-permute-start.19
  327.2 5.4 %all-to-all-start = ((f32[32,1,1]{2,1,0:T(1,128)}), f32[32,1,1]{2,1,0:T(1,128)S(1)}, u32[]{:S(2)}, u32[]{:S(2)}) async-start(f32[32,1,1]{2,1,0:T(1,128)} %broadcast_in_dim.40), calls=%async_computation | async-start | bytes 32768 | tf_op jit(solution)/shard_map/all_to_all | solution.py:452
  333.4 7.3 %quantize.5 = (bf16[1792,2048]{1,0:T(8,128)(2,1)}, f32[896,128]{1,0:T(8,128)}) custom-call(s32[1]{0:T(128)} %bitcast.place_ref, bf16[1792,128]{1,0:T(8,128)(2,1)} %bitcast.64, bf16[1792,128]{1,0:T(8,128)(2,1)} %collective-permute-done.30.refs_1_, bf16[1792,128]{1,0:T(8,128)(2,1)} %collective-permute-done.31.refs_2_, ...), custom_call_target="tpu_custom_call" | custom-call | tf_op jit(solution)/shard_map/quantize/pallas_call | solution.py:262
  340.7 7.7 %quantize.6 = (bf16[1792,2048]{1,0:T(8,128)(2,1)}, f32[1792,256]{1,0:T(8,128)}) custom-call(s32[1]{0:T(128)} %bitcast.place_ref, bf16[1792,128]{1,0:T(8,128)(2,1)} %bitcast.70, bf16[1792,128]{1,0:T(8,128)(2,1)} %collective-permute-done.27.refs_1_, bf16[1792,128]{1,0:T(8,128)(2,1)} %collective-permute-done.28.refs_2_, ...), custom_call_target="tpu_custom_call", output_to_operand_aliasing={{0}: (9, {})} | custom-call | tf_op jit(solution)/shard_map/quantize/pallas_call | solution.py:262
  348.4 6.6 %all-to-all-done = f32[32,1,1]{2,1,0:T(1,128)S(1)} async-done(((f32[32,1,1]{2,1,0:T(1,128)}), f32[32,1,1]{2,1,0:T(1,128)S(1)}, u32[]{:S(2)}, u32[]{:S(2)}) %all-to-all-start) | async-done | bytes 160 | tf_op jit(solution)/shard_map/all_to_all | solution.py:452
  357.2 7.3 %quantize.7 = (bf16[1792,2048]{1,0:T(8,128)(2,1)}, f32[896,128]{1,0:T(8,128)}) custom-call(s32[1]{0:T(128)} %bitcast.place_ref, bf16[1792,128]{1,0:T(8,128)(2,1)} %bitcast.67, bf16[1792,128]{1,0:T(8,128)(2,1)} %copy-done.11, bf16[1792,128]{1,0:T(8,128)(2,1)} %copy-done.13, bf16[1792,128]{1,0:T(8,128)(2,1)} %copy-done.15, ...), custom_call_target="tpu_custom_call", output_to_operand_aliasing={{0}: (8, {})} | custom-call | tf_op jit(solution)/shard_map/quantize/pallas_call | solution.py:262
  365.3 5.1 %quantize.8 = (bf16[1792,2048]{1,0:T(8,128)(2,1)}, f32[1792,256]{1,0:T(8,128)}) custom-call(s32[1]{0:T(128)} %bitcast.place_ref, bf16[896,128]{1,0:T(8,128)(2,1)} %bitcast.104, bf16[896,128]{1,0:T(8,128)(2,1)} %collective-permute-done.33.refs_1_, bf16[896,128]{1,0:T(8,128)(2,1)} %copy-done.24, ...), custom_call_target="tpu_custom_call", output_to_operand_aliasing={{0}: (9, {}), {1}: (10, {})} | custom-call | tf_op jit(solution)/shard_map/quantize/pallas_call | solution.py:262
  371.2 5.2 %quantize.9 = (bf16[1792,2048]{1,0:T(8,128)(2,1)}, f32[1792,256]{1,0:T(8,128)}) custom-call(s32[1]{0:T(128)} %bitcast.place_ref, bf16[896,128]{1,0:T(8,128)(2,1)} %bitcast.102, bf16[896,128]{1,0:T(8,128)(2,1)} %copy-done.22, bf16[896,128]{1,0:T(8,128)(2,1)} %copy-done.23, ...), custom_call_target="tpu_custom_call", output_to_operand_aliasing={{0}: (9, {}), {1}: (10, {})} | custom-call | tf_op jit(solution)/shard_map/quantize/pallas_call | solution.py:262
  (164 shorter events, 58.8 us)
Async XLA Ops:
  3.7 20.8 %collective-permute-start.6 = (bf16[256,128]{1,0:T(8,128)(2,1)}, bf16[256,128]{1,0:T(8,128)(2,1)S(1)}, u32[]{:S(2)}, u32[]{:S(2)}) collective-permute-start(bf16[256,128]{1,0:T(8,128)(2,1)} %get-tuple-element.143), channel_id=1, source_target_pairs={{0,1},{1,2},{2,3},{3,0},{4,5},{5,6},{6,7},{7,4},{8,9},{9,10},{10,1... | collective-permute-start | bytes 196616 | tf_op jit(solution)/shard_map/ppermute | solution.py:381
  6.8 18.8 %collective-permute-start.9 = (bf16[256,128]{1,0:T(8,128)(2,1)}, bf16[256,128]{1,0:T(8,128)(2,1)S(1)}, u32[]{:S(2)}, u32[]{:S(2)}) collective-permute-start(bf16[256,128]{1,0:T(8,128)(2,1)} %get-tuple-element.146), channel_id=1, source_target_pairs={{0,2},{1,3},{2,0},{3,1},{4,6},{5,7},{6,4},{7,5},{8,10},{9,11},{10,... | collective-permute-start | bytes 196616 | tf_op jit(solution)/shard_map/ppermute | solution.py:381
  13.4 34.8 %collective-permute-start.7 = (bf16[512,128]{1,0:T(8,128)(2,1)}, bf16[512,128]{1,0:T(8,128)(2,1)S(1)}, u32[]{:S(2)}, u32[]{:S(2)}) collective-permute-start(bf16[512,128]{1,0:T(8,128)(2,1)} %get-tuple-element.144), channel_id=1, source_target_pairs={{0,1},{1,2},{2,3},{3,0},{4,5},{5,6},{6,7},{7,4},{8,9},{9,10},{10,1... | collective-permute-start | bytes 393224 | tf_op jit(solution)/shard_map/ppermute | solution.py:381
  20.2 41.4 %collective-permute-start.8 = (bf16[1024,128]{1,0:T(8,128)(2,1)}, bf16[1024,128]{1,0:T(8,128)(2,1)S(1)}, u32[]{:S(2)}, u32[]{:S(2)}) collective-permute-start(bf16[1024,128]{1,0:T(8,128)(2,1)} %get-tuple-element.145), channel_id=1, source_target_pairs={{0,1},{1,2},{2,3},{3,0},{4,5},{5,6},{6,7},{7,4},{8,9},{9,10},{10,1... | collective-permute-start | bytes 786440 | tf_op jit(solution)/shard_map/ppermute | solution.py:381
  21.0 40.6 %collective-permute-start.11 = (bf16[1024,128]{1,0:T(8,128)(2,1)}, bf16[1024,128]{1,0:T(8,128)(2,1)S(1)}, u32[]{:S(2)}, u32[]{:S(2)}) collective-permute-start(bf16[1024,128]{1,0:T(8,128)(2,1)} %get-tuple-element.148), channel_id=1, source_target_pairs={{0,2},{1,3},{2,0},{3,1},{4,6},{5,7},{6,4},{7,5},{8,10},{9,11},{10,... | collective-permute-start | bytes 786440 | tf_op jit(solution)/shard_map/ppermute | solution.py:381
  25.1 36.5 %collective-permute-start.14 = (bf16[1024,128]{1,0:T(8,128)(2,1)}, bf16[1024,128]{1,0:T(8,128)(2,1)S(1)}, u32[]{:S(2)}, u32[]{:S(2)}) collective-permute-start(bf16[1024,128]{1,0:T(8,128)(2,1)} %get-tuple-element.151), channel_id=1, source_target_pairs={{0,3},{1,0},{2,1},{3,2},{4,7},{5,4},{6,5},{7,6},{8,11},{9,8},{10,9... | collective-permute-start | bytes 786440 | tf_op jit(solution)/shard_map/ppermute | solution.py:381
  25.5 16.9 %collective-permute-start.12 = (bf16[256,128]{1,0:T(8,128)(2,1)S(1)}, bf16[256,128]{1,0:T(8,128)(2,1)S(1)}, u32[]{:S(2)}, u32[]{:S(2)}) collective-permute-start(bf16[256,128]{1,0:T(8,128)(2,1)S(1)} %copy-done.37), channel_id=1, source_target_pairs={{0,3},{1,0},{2,1},{3,2},{4,7},{5,4},{6,5},{7,6},{8,11},{9,8},{10,9... | collective-permute-start | bytes 196616 | tf_op jit(solution)/shard_map/ppermute | solution.py:381
  54.5 18.2 %collective-permute-start = (bf16[1792,128]{1,0:T(8,128)(2,1)}, bf16[1792,128]{1,0:T(8,128)(2,1)S(1)}, u32[]{:S(2)}, u32[]{:S(2)}) collective-permute-start(bf16[1792,128]{1,0:T(8,128)(2,1)} %get-tuple-element.133), channel_id=1, source_target_pairs={{0,1},{1,2},{2,3},{3,0},{4,5},{5,6},{6,7},{7,4},{8,9},{9,10},{10,1... | collective-permute-start | bytes 1376264 | tf_op jit(solution)/shard_map/ppermute | solution.py:381
  58.1 34.3 %collective-permute-start.1 = (bf16[1792,128]{1,0:T(8,128)(2,1)}, bf16[1792,128]{1,0:T(8,128)(2,1)S(1)}, u32[]{:S(2)}, u32[]{:S(2)}) collective-permute-start(bf16[1792,128]{1,0:T(8,128)(2,1)} %get-tuple-element.134), channel_id=1, source_target_pairs={{0,2},{1,3},{2,0},{3,1},{4,6},{5,7},{6,4},{7,5},{8,10},{9,11},{10,... | collective-permute-start | bytes 1376264 | tf_op jit(solution)/shard_map/ppermute | solution.py:381
  61.6 30.9 %collective-permute-start.2 = (bf16[1792,128]{1,0:T(8,128)(2,1)}, bf16[1792,128]{1,0:T(8,128)(2,1)S(1)}, u32[]{:S(2)}, u32[]{:S(2)}) collective-permute-start(bf16[1792,128]{1,0:T(8,128)(2,1)} %get-tuple-element.135), channel_id=1, source_target_pairs={{0,3},{1,0},{2,1},{3,2},{4,7},{5,4},{6,5},{7,6},{8,11},{9,8},{10,9... | collective-permute-start | bytes 1376264 | tf_op jit(solution)/shard_map/ppermute | solution.py:381
  61.6 60.9 %collective-permute-start.15 = (bf16[1792,128]{1,0:T(8,128)(2,1)}, bf16[1792,128]{1,0:T(8,128)(2,1)S(1)}, u32[]{:S(2)}, u32[]{:S(2)}) collective-permute-start(bf16[1792,128]{1,0:T(8,128)(2,1)} %get-tuple-element.152), channel_id=1, source_target_pairs={{0,1},{1,2},{2,3},{3,0},{4,5},{5,6},{6,7},{7,4},{8,9},{9,10},{10,1... | collective-permute-start | bytes 1376264 | tf_op jit(solution)/shard_map/ppermute | solution.py:381
  63.8 99.3 %collective-permute-start.16 = (bf16[1792,128]{1,0:T(8,128)(2,1)}, bf16[1792,128]{1,0:T(8,128)(2,1)S(1)}, u32[]{:S(2)}, u32[]{:S(2)}) collective-permute-start(bf16[1792,128]{1,0:T(8,128)(2,1)} %get-tuple-element.153), channel_id=1, source_target_pairs={{0,2},{1,3},{2,0},{3,1},{4,6},{5,7},{6,4},{7,5},{8,10},{9,11},{10,... | collective-permute-start | bytes 1376264 | tf_op jit(solution)/shard_map/ppermute | solution.py:381
  72.7 90.3 %collective-permute-start.17 = (bf16[1792,128]{1,0:T(8,128)(2,1)}, bf16[1792,128]{1,0:T(8,128)(2,1)S(1)}, u32[]{:S(2)}, u32[]{:S(2)}) collective-permute-start(bf16[1792,128]{1,0:T(8,128)(2,1)} %get-tuple-element.154), channel_id=1, source_target_pairs={{0,3},{1,0},{2,1},{3,2},{4,7},{5,4},{6,5},{7,6},{8,11},{9,8},{10,9... | collective-permute-start | bytes 1376264 | tf_op jit(solution)/shard_map/ppermute | solution.py:381
  92.4 79.6 %collective-permute-start.3 = (bf16[1792,128]{1,0:T(8,128)(2,1)}, bf16[1792,128]{1,0:T(8,128)(2,1)}, u32[]{:S(2)}, u32[]{:S(2)}) collective-permute-start(bf16[1792,128]{1,0:T(8,128)(2,1)} %get-tuple-element.136), channel_id=1, source_target_pairs={{0,1},{1,2},{2,3},{3,0},{4,5},{5,6},{6,7},{7,4},{8,9},{9,10},{10,1... | collective-permute-start | bytes 1376264 | tf_op jit(solution)/shard_map/ppermute | solution.py:381
  122.5 49.6 %collective-permute-start.4 = (bf16[1792,128]{1,0:T(8,128)(2,1)}, bf16[1792,128]{1,0:T(8,128)(2,1)}, u32[]{:S(2)}, u32[]{:S(2)}) collective-permute-start(bf16[1792,128]{1,0:T(8,128)(2,1)} %get-tuple-element.137), channel_id=1, source_target_pairs={{0,2},{1,3},{2,0},{3,1},{4,6},{5,7},{6,4},{7,5},{8,10},{9,11},{10,... | collective-permute-start | bytes 1376264 | tf_op jit(solution)/shard_map/ppermute | solution.py:381
  122.5 49.6 %collective-permute-start.5 = (bf16[1792,128]{1,0:T(8,128)(2,1)}, bf16[1792,128]{1,0:T(8,128)(2,1)}, u32[]{:S(2)}, u32[]{:S(2)}) collective-permute-start(bf16[1792,128]{1,0:T(8,128)(2,1)} %get-tuple-element.138), channel_id=1, source_target_pairs={{0,3},{1,0},{2,1},{3,2},{4,7},{5,4},{6,5},{7,6},{8,11},{9,8},{10,9... | collective-permute-start | bytes 1376264 | tf_op jit(solution)/shard_map/ppermute | solution.py:381
  190.2 15.8 %collective-permute-start.30 = (bf16[1792,128]{1,0:T(8,128)(2,1)S(1)}, bf16[1792,128]{1,0:T(8,128)(2,1)}, u32[]{:S(2)}, u32[]{:S(2)}) collective-permute-start(bf16[1792,128]{1,0:T(8,128)(2,1)S(1)} %bitcast.76), channel_id=1, source_target_pairs={{0,1},{1,2},{2,3},{3,0},{4,5},{5,6},{6,7},{7,4},{8,9},{9,10},{10,1... | collective-permute-start | bytes 1376264 | tf_op jit(solution)/shard_map/ppermute | solution.py:381
  191.2 34.5 %collective-permute-start.31 = (bf16[1792,128]{1,0:T(8,128)(2,1)S(1)}, bf16[1792,128]{1,0:T(8,128)(2,1)}, u32[]{:S(2)}, u32[]{:S(2)}) collective-permute-start(bf16[1792,128]{1,0:T(8,128)(2,1)S(1)} %bitcast.79), channel_id=1, source_target_pairs={{0,2},{1,3},{2,0},{3,1},{4,6},{5,7},{6,4},{7,5},{8,10},{9,11},{10,... | collective-permute-start | bytes 1376264 | tf_op jit(solution)/shard_map/ppermute | solution.py:381
  194.6 56.9 %collective-permute-start.32 = (bf16[1792,128]{1,0:T(8,128)(2,1)S(1)}, bf16[1792,128]{1,0:T(8,128)(2,1)}, u32[]{:S(2)}, u32[]{:S(2)}) collective-permute-start(bf16[1792,128]{1,0:T(8,128)(2,1)S(1)} %bitcast.82), channel_id=1, source_target_pairs={{0,3},{1,0},{2,1},{3,2},{4,7},{5,4},{6,5},{7,6},{8,11},{9,8},{10,9... | collective-permute-start | bytes 1376264 | tf_op jit(solution)/shard_map/ppermute | solution.py:381
  194.7 60.8 %collective-permute-start.27 = (bf16[1792,128]{1,0:T(8,128)(2,1)S(1)}, bf16[1792,128]{1,0:T(8,128)(2,1)}, u32[]{:S(2)}, u32[]{:S(2)}) collective-permute-start(bf16[1792,128]{1,0:T(8,128)(2,1)S(1)} %bitcast.94), channel_id=1, source_target_pairs={{0,1},{1,2},{2,3},{3,0},{4,5},{5,6},{6,7},{7,4},{8,9},{9,10},{10,1... | collective-permute-start | bytes 1376264 | tf_op jit(solution)/shard_map/ppermute | solution.py:381
  196.7 86.5 %collective-permute-start.28 = (bf16[1792,128]{1,0:T(8,128)(2,1)}, bf16[1792,128]{1,0:T(8,128)(2,1)}, u32[]{:S(2)}, u32[]{:S(2)}) collective-permute-start(bf16[1792,128]{1,0:T(8,128)(2,1)} %bitcast.95), channel_id=1, source_target_pairs={{0,2},{1,3},{2,0},{3,1},{4,6},{5,7},{6,4},{7,5},{8,10},{9,11},{10,... | collective-permute-start | bytes 1376264 | tf_op jit(solution)/shard_map/ppermute | solution.py:381
  206.0 110.6 %collective-permute-start.29 = (bf16[1792,128]{1,0:T(8,128)(2,1)S(1)}, bf16[1792,128]{1,0:T(8,128)(2,1)S(1)}, u32[]{:S(2)}, u32[]{:S(2)}) collective-permute-start(bf16[1792,128]{1,0:T(8,128)(2,1)S(1)} %bitcast.91), channel_id=1, source_target_pairs={{0,3},{1,0},{2,1},{3,2},{4,7},{5,4},{6,5},{7,6},{8,11},{9,8},{10,9... | collective-permute-start | bytes 1376264 | tf_op jit(solution)/shard_map/ppermute | solution.py:381
  225.7 94.4 %collective-permute-start.24 = (bf16[1792,128]{1,0:T(8,128)(2,1)}, bf16[1792,128]{1,0:T(8,128)(2,1)S(1)}, u32[]{:S(2)}, u32[]{:S(2)}) collective-permute-start(bf16[1792,128]{1,0:T(8,128)(2,1)} %bitcast.98), channel_id=1, source_target_pairs={{0,1},{1,2},{2,3},{3,0},{4,5},{5,6},{6,7},{7,4},{8,9},{9,10},{10,1... | collective-permute-start | bytes 1376264 | tf_op jit(solution)/shard_map/ppermute | solution.py:381
  251.6 71.4 %collective-permute-start.25 = (bf16[1792,128]{1,0:T(8,128)(2,1)S(1)}, bf16[1792,128]{1,0:T(8,128)(2,1)S(1)}, u32[]{:S(2)}, u32[]{:S(2)}) collective-permute-start(bf16[1792,128]{1,0:T(8,128)(2,1)S(1)} %bitcast.88), channel_id=1, source_target_pairs={{0,2},{1,3},{2,0},{3,1},{4,6},{5,7},{6,4},{7,5},{8,10},{9,11},{10,... | collective-permute-start | bytes 1376264 | tf_op jit(solution)/shard_map/ppermute | solution.py:381
  255.6 67.4 %collective-permute-start.26 = (bf16[1792,128]{1,0:T(8,128)(2,1)S(1)}, bf16[1792,128]{1,0:T(8,128)(2,1)S(1)}, u32[]{:S(2)}, u32[]{:S(2)}) collective-permute-start(bf16[1792,128]{1,0:T(8,128)(2,1)S(1)} %bitcast.85), channel_id=1, source_target_pairs={{0,3},{1,0},{2,1},{3,2},{4,7},{5,4},{6,5},{7,6},{8,11},{9,8},{10,9... | collective-permute-start | bytes 1376264 | tf_op jit(solution)/shard_map/ppermute | solution.py:381
  283.2 33.5 %collective-permute-start.33 = (bf16[896,128]{1,0:T(8,128)(2,1)}, bf16[896,128]{1,0:T(8,128)(2,1)}, u32[]{:S(2)}, u32[]{:S(2)}) collective-permute-start(bf16[896,128]{1,0:T(8,128)(2,1)} %bitcast.47.refs_7_), channel_id=1, source_target_pairs={{0,1},{1,2},{2,3},{3,0},{4,5},{5,6},{6,7},{7,4},{8,9},{9,10},{10,1... | collective-permute-start | bytes 688136 | tf_op jit(solution)/shard_map/ppermute | solution.py:381
  316.6 53.8 %collective-permute-start.18 = (bf16[896,128]{1,0:T(8,128)(2,1)}, bf16[896,128]{1,0:T(8,128)(2,1)S(1)}, u32[]{:S(2)}, u32[]{:S(2)}) collective-permute-start(bf16[896,128]{1,0:T(8,128)(2,1)} %bitcast.127), channel_id=1, source_target_pairs={{0,1},{1,2},{2,3},{3,0},{4,5},{5,6},{6,7},{7,4},{8,9},{9,10},{10,1... | collective-permute-start | bytes 688136 | tf_op jit(solution)/shard_map/ppermute | solution.py:381
  316.7 53.8 %collective-permute-start.19 = (bf16[896,128]{1,0:T(8,128)(2,1)}, bf16[896,128]{1,0:T(8,128)(2,1)S(1)}, u32[]{:S(2)}, u32[]{:S(2)}) collective-permute-start(bf16[896,128]{1,0:T(8,128)(2,1)} %bitcast.125), channel_id=1, source_target_pairs={{0,2},{1,3},{2,0},{3,1},{4,6},{5,7},{6,4},{7,5},{8,10},{9,11},{10,... | collective-permute-start | bytes 688136 | tf_op jit(solution)/shard_map/ppermute | solution.py:381
  320.1 50.4 %collective-permute-start.20 = (bf16[896,128]{1,0:T(8,128)(2,1)S(1)}, bf16[896,128]{1,0:T(8,128)(2,1)}, u32[]{:S(2)}, u32[]{:S(2)}) collective-permute-start(bf16[896,128]{1,0:T(8,128)(2,1)S(1)} %bitcast.123), channel_id=1, source_target_pairs={{0,3},{1,0},{2,1},{3,2},{4,7},{5,4},{6,5},{7,6},{8,11},{9,8},{10,9... | collective-permute-start | bytes 688136 | tf_op jit(solution)/shard_map/ppermute | solution.py:381
  323.0 41.5 %collective-permute-start.34 = (bf16[896,128]{1,0:T(8,128)(2,1)}, bf16[896,128]{1,0:T(8,128)(2,1)S(1)}, u32[]{:S(2)}, u32[]{:S(2)}) collective-permute-start(bf16[896,128]{1,0:T(8,128)(2,1)} %bitcast.131), channel_id=1, source_target_pairs={{0,2},{1,3},{2,0},{3,1},{4,6},{5,7},{6,4},{7,5},{8,10},{9,11},{10,... | collective-permute-start | bytes 688136 | tf_op jit(solution)/shard_map/ppermute | solution.py:381
  323.0 41.5 %collective-permute-start.35 = (bf16[896,128]{1,0:T(8,128)(2,1)}, bf16[896,128]{1,0:T(8,128)(2,1)S(1)}, u32[]{:S(2)}, u32[]{:S(2)}) collective-permute-start(bf16[896,128]{1,0:T(8,128)(2,1)} %bitcast.129), channel_id=1, source_target_pairs={{0,3},{1,0},{2,1},{3,2},{4,7},{5,4},{6,5},{7,6},{8,11},{9,8},{10,9... | collective-permute-start | bytes 688136 | tf_op jit(solution)/shard_map/ppermute | solution.py:381
  327.2 27.8 %all-to-all-start = ((f32[32,1,1]{2,1,0:T(1,128)}), f32[32,1,1]{2,1,0:T(1,128)S(1)}, u32[]{:S(2)}, u32[]{:S(2)}) async-start(f32[32,1,1]{2,1,0:T(1,128)} %broadcast_in_dim.40), calls=%async_computation | async-start | bytes 32768 | tf_op jit(solution)/shard_map/all_to_all | solution.py:452
  (43 other events, 1308.1 us)

commit v4 on v3

--- a/solution.py
+++ b/solution.py
@@ -12,9 +12,9 @@
 INNER = 256
 LOW = 16
 CHUNKS = 4
-AHEAD = 2
+AHEAD = 3
 OCTET = 8
-TILE2 = 448
+TILE2 = 256
 
 
 def butterfly(parts):
@@ -389,7 +389,7 @@
         piece_rows, whole = column_transform(*column_args, first_row, count, math.gcd(first_row, count) or count, whole)
         early.append(piece_rows)
         first_row += count
-    splits = (blocks_here // 2, blocks_here - blocks_here // 2)
+    splits = thirds[::-1]
     step_rows = math.gcd(*(n * HB for n in splits))
     outgoing = [[[rows[s] for rows in early] for s in range(ring)]]
     outgoing += [[[whole[c * ring + s]] for s in range(ring)] for c in range(chunks - 1)]

time: 378 us -> 384 us (1.016)
  starting transfers between devices: 138 us -> 105 us
  waiting for transfers between devices: 96 us -> 124 us
  Pallas kernels: 102 us -> 112 us
    ppermute x36 -> x39, waiting for transfers between devices: 89.4 us -> 124 us  [send(): lax.ppermute(x, 'row', [(k, (k + shift) % ring) for k in range(ring)])]
    ppermute x36 -> x39, starting transfers between devices: 133 us -> 102 us  [send(): lax.ppermute(x, 'row', [(k, (k + shift) % ring) for k in range(ring)])]
    pallas_call x5 -> x6, Pallas kernels: 32.6 us -> 39.3 us  [quantize(): pl.pallas_call(kernel, grid=(rows // tile,), in_specs=in_specs, out_specs...]
    all_to_all x1, waiting for transfers between devices: 6.59 us -> 0.01 us  [body(): every_error = lax.all_to_all(copies, ('expert', 'row'), 0, 0)]
    pallas_call x2 -> x3, Pallas kernels: 23.7 us -> 27 us  [lattice_sum(): pl.pallas_call(kernel, grid=(rows // tile,), in_specs=in_specs, out_specs...]
  transfers between devices with their start and end apart: 37 -> 40, of which waited for: 8 -> 8; matrix products, arithmetic and copies ran while one was open for 9% -> 9% of each run, Pallas kernels for 23% -> 23%
where the time goes in v4:
time: 384 us; the launch traced here: 383 us
  waiting for transfers between devices  124 us (32%)
  Pallas kernels  112 us (29%)
  starting transfers between devices  105 us (27%)
  other arithmetic  30.5 us (8%)
  local copies, waits for them, and re-layouts  7.81 us (2%)
    ppermute x39, waiting for transfers between devices, send(): lax.ppermute(x, 'row', [(k, (k + shift) % ring) for k in range(ring)])  124 us
    ppermute x39, starting transfers between devices, send(): lax.ppermute(x, 'row', [(k, (k + shift) % ring) for k in range(ring)])  102 us
    pallas_call x6, Pallas kernels, quantize(): pl.pallas_call(kernel, grid=(rows // tile,), in_specs=in_specs, out_specs...  39.3 us
    pallas_call x4, Pallas kernels, row_mix(): pl.pallas_call(kernel, out_shape=[jax.ShapeDtypeStruct((n, high, LOW, wid...  31.9 us
    pallas_call x3, Pallas kernels, lattice_sum(): pl.pallas_call(kernel, grid=(rows // tile,), in_specs=in_specs, out_specs...  27 us
    convert_element_type x1, other arithmetic, mixer_table(): return jnp.where(common & 1 == 0, table, -table).astype(jnp.bfloat16)  20.4 us
    pallas_call x3, Pallas kernels, column_transform(): pl.pallas_call(kernel, grid=(rows // tile,), in_specs=in_specs, out_specs...  13.9 us
  transfers between devices with their start and end apart: 40, of which 8 were waited for; matrix products, arithmetic and copies ran while one was open for 9% of the time, Pallas kernels for 23%

profile of v4, /device:TPU:0, one launch (start us, length us, event | category | flops | bytes accessed | tf_op | source)
XLA Modules:
  0.0 382.6 jit_solution(1523385427366135973)
XLA Ops:
  3.7 4.1 %column_transform.4 = (bf16[512,128]{1,0:T(8,128)(2,1)}, bf16[512,128]{1,0:T(8,128)(2,1)}, bf16[512,128]{1,0:T(8,128)(2,1)}, bf16[512,128]{1,0:T(8,128)(2,1)}, b...) custom-call(s32[1]{0:T(128)} %bitcast.place_ref, ...), custom_call_target="tpu_custom_call", output_to_operand_aliasing={{4}: (4, {}), {5}: (5, {}), {6}: (6, {}), {7}: (7, {}), {8}... | custom-call | tf_op jit(solution)/shard_map/column_transform/pallas_call | solution.py:104
  7.8 6.7 %column_transform.5 = (bf16[1024,128]{1,0:T(8,128)(2,1)}, bf16[1024,128]{1,0:T(8,128)(2,1)}, bf16[1024,128]{1,0:T(8,128)(2,1)}, bf16[1024,128]{1,0:T(8,128)(2,1)...) custom-call(s32[1]{0:T(128)} %bitcast.place_ref, ...), custom_call_target="tpu_custom_call", output_to_operand_aliasing={{4}: (4, {}), {5}: (5, {}), {6}: (6, {}), {7}: (7, {}), {8}... | custom-call | tf_op jit(solution)/shard_map/column_transform/pallas_call | solution.py:104
  23.7 4.8 %collective-permute-done = bf16[256,128]{1,0:T(8,128)(2,1)S(1)} collective-permute-done((bf16[256,128]{1,0:T(8,128)(2,1)S(1)}, bf16[256,128]{1,0:T(8,128)(2,1)S(1)}, u32[]{:S(2)}, u32[]{:S(2)}) %collective-permute-start) | collective-permute-done | bytes 65568 | tf_op jit(solution)/shard_map/ppermute | solution.py:381
  31.1 5.0 %collective-permute-done.3 = bf16[256,128]{1,0:T(8,128)(2,1)S(1)} collective-permute-done((bf16[256,128]{1,0:T(8,128)(2,1)S(1)}, bf16[256,128]{1,0:T(8,128)(2,1)S(1)}, u32[]{:S(2)}, u32[]{:S(2)}) %collective-permute-start.3) | collective-permute-done | bytes 65568 | tf_op jit(solution)/shard_map/ppermute | solution.py:381
  36.1 4.3 %collective-permute-done.6 = bf16[256,128]{1,0:T(8,128)(2,1)S(1)} collective-permute-done((bf16[256,128]{1,0:T(8,128)(2,1)S(1)}, bf16[256,128]{1,0:T(8,128)(2,1)S(1)}, u32[]{:S(2)}, u32[]{:S(2)}) %collective-permute-start.6) | collective-permute-done | bytes 65568 | tf_op jit(solution)/shard_map/ppermute | solution.py:381
  50.9 35.0 %collective-permute-done.5 = bf16[1024,128]{1,0:T(8,128)(2,1)S(1)} collective-permute-done((bf16[1024,128]{1,0:T(8,128)(2,1)}, bf16[1024,128]{1,0:T(8,128)(2,1)S(1)}, u32[]{:S(2)}, u32[]{:S(2)}) %collective-permute-start.5) | collective-permute-done | bytes 262176 | tf_op jit(solution)/shard_map/ppermute | solution.py:381
  85.9 14.0 %collective-permute-done.8 = bf16[1024,128]{1,0:T(8,128)(2,1)S(1)} collective-permute-done((bf16[1024,128]{1,0:T(8,128)(2,1)}, bf16[1024,128]{1,0:T(8,128)(2,1)S(1)}, u32[]{:S(2)}, u32[]{:S(2)}) %collective-permute-start.8) | collective-permute-done | bytes 262176 | tf_op jit(solution)/shard_map/ppermute | solution.py:381
  99.9 10.1 %collective-permute-start.13 = (bf16[1792,128]{1,0:T(8,128)(2,1)}, bf16[1792,128]{1,0:T(8,128)(2,1)S(1)}, u32[]{:S(2)}, u32[]{:S(2)}) collective-permute-start(bf16[1792,128]{1,0:T(8,128)(2,1)} %get-tuple-element.147), channel_id=1, source_target_pairs={{0,2},{1,3},{2,0},{3,1},{4,6},{5,7},{6,4},{7,5},{8,10},{9,11},{10,... | collective-permute-start | bytes 1376264 | tf_op jit(solution)/shard_map/ppermute | solution.py:381
  110.0 3.3 collective-permute-start.14
  113.9 17.3 %collective-permute-start.11 = (bf16[1792,128]{1,0:T(8,128)(2,1)}, bf16[1792,128]{1,0:T(8,128)(2,1)}, u32[]{:S(2)}, u32[]{:S(2)}) collective-permute-start(bf16[1792,128]{1,0:T(8,128)(2,1)} %get-tuple-element.144), channel_id=1, source_target_pairs={{0,3},{1,0},{2,1},{3,2},{4,7},{5,4},{6,5},{7,6},{8,11},{9,8},{10,9... | collective-permute-start | bytes 1376264 | tf_op jit(solution)/shard_map/ppermute | solution.py:381
  131.2 20.4 %fusion.42.refs_12_.refs_4_ = bf16[896,896]{1,0:T(8,128)(2,1)} fusion(s32[896]{0:T(1024)S(1)} %get-tuple-element.216, s32[896]{0:T(1024)S(1)} %get-tuple-element.217, s32[896]{0:T(1024)S(1)} %get-tuple-element.215, s32[896]{0:T(1024)S(1)} %get-tuple-element.222, s32[]{:T(128)} %axis_index.22, s32[896]{0:T(1024)S(1)} %get-tuple-element.218, ...), kind=kLoop, calls=%fused_computation.87 | loop fusion | flops 69042176 | bytes 1629828 | tf_op jit(solution)/shard_map/convert_element_type | solution.py:352
  153.5 8.0 %row_mix.4 = (bf16[14,8,16,128]{3,2,1,0:T(8,128)(2,1)}, bf16[14,8,16,128]{3,2,1,0:T(8,128)(2,1)}, bf16[14,8,16,128]{3,2,1,0:T(8,128)(2,1)}, bf16[14,8,16,128]{3,2,1,0:T(8,128)(2,1)}, f32[16,128]{1,0:T(8,128)}) custom-call(bf16[2,8,16,128]{3,2,1,0:T(8,128)(2,1)} %bitcast.163, bf16[4,8,16,128]{3,2,1,0:T(8,128)(2,1)} %bitcast.153, ...), custom_call_target="tpu_custom_call" | custom-call | tf_op jit(solution)/shard_map/row_mix/pallas_call | solution.py:160
  161.5 7.8 %row_mix.5 = (bf16[14,8,16,128]{3,2,1,0:T(8,128)(2,1)}, bf16[14,8,16,128]{3,2,1,0:T(8,128)(2,1)}, bf16[14,8,16,128]{3,2,1,0:T(8,128)(2,1)}, bf16[14,8,16,128]{3,2,1,0:T(8,128)(2,1)}, f32[16,128]{1,0:T(8,128)}) custom-call(bf16[14,8,16,128]{3,2,1,0:T(8,128)(2,1)} %bitcast.114, bf16[14,8,16,128]{3,2,1,0:T(8,128)(2,1)} %bitcast.130, ...), custom_call_target="tpu_custom_call" | custom-call | tf_op jit(solution)/shard_map/row_mix/pallas_call | solution.py:160
  170.3 8.1 %row_mix.6 = (bf16[14,8,16,128]{3,2,1,0:T(8,128)(2,1)}, bf16[14,8,16,128]{3,2,1,0:T(8,128)(2,1)}, bf16[14,8,16,128]{3,2,1,0:T(8,128)(2,1)}, bf16[14,8,16,128]{3,2,1,0:T(8,128)(2,1)}, f32[16,128]{1,0:T(8,128)}) custom-call(bf16[14,8,16,128]{3,2,1,0:T(8,128)(2,1)} %bitcast.115, bf16[14,8,16,128]{3,2,1,0:T(8,128)(2,1)} %bitcast.129, ...), custom_call_target="tpu_custom_call" | custom-call | tf_op jit(solution)/shard_map/row_mix/pallas_call | solution.py:160
  178.4 8.0 %row_mix.7 = (bf16[8,8,16,128]{3,2,1,0:T(8,128)(2,1)}, bf16[4,8,16,128]{3,2,1,0:T(8,128)(2,1)}, bf16[2,8,16,128]{3,2,1,0:T(8,128)(2,1)}, bf16[8,8,16,128]{3,2,1,...) custom-call(bf16[14,8,16,128]{3,2,1,0:T(8,128)(2,1)} %bitcast.116, ...), custom_call_target="tpu_custom_call" | custom-call | tf_op jit(solution)/shard_map/row_mix/pallas_call | solution.py:160
  186.4 3.7 collective-permute-start.23
  196.1 17.0 %collective-permute-done.22 = f32[16,128]{1,0:T(8,128)S(1)} collective-permute-done((f32[16,128]{1,0:T(8,128)}, f32[16,128]{1,0:T(8,128)S(1)}, u32[]{:S(2)}, u32[]{:S(2)}) %collective-permute-start.22) | collective-permute-done | bytes 8224 | tf_op jit(solution)/shard_map/ppermute | solution.py:381
  213.0 5.4 %fusion.22 = (bf16[1024,1024]{1,0:T(8,128)(2,1)}, bf16[1024,1024]{1,0:T(8,128)(2,1)}) fusion(s32[1024]{0:T(1024)S(1)} %get-tuple-element.223, s32[1024]{0:T(1024)S(1)} %get-tuple-element.226, s32[1024]{0:T(1024)S(1)} %get-tuple-element.224, s32[1024]{0:T(1024)S(1)} %get-tuple-element.225, pred[1024]{0:T(1024)(128)(4,1)S(1)} %get-tuple-element.227, ...), kind=kLoop, calls=%fused_computation.67 | loop fusion | flops 83886080 | bytes 4212740 | tf_op jit(solution)/shard_map/convert_element_type | solution.py:362
  218.8 15.1 %collective-permute-done.21 = f32[16,128]{1,0:T(8,128)S(1)} collective-permute-done((f32[16,128]{1,0:T(8,128)}, f32[16,128]{1,0:T(8,128)S(1)}, u32[]{:S(2)}, u32[]{:S(2)}) %collective-permute-start.21) | collective-permute-done | bytes 8224 | tf_op jit(solution)/shard_map/ppermute | solution.py:381
  233.9 11.5 %collective-permute-start.25 = (bf16[1792,128]{1,0:T(8,128)(2,1)}, bf16[1792,128]{1,0:T(8,128)(2,1)}, u32[]{:S(2)}, u32[]{:S(2)}) collective-permute-start(bf16[1792,128]{1,0:T(8,128)(2,1)} %bitcast.106), channel_id=1, source_target_pairs={{0,2},{1,3},{2,0},{3,1},{4,6},{5,7},{6,4},{7,5},{8,10},{9,11},{10,... | collective-permute-start | bytes 1376264 | tf_op jit(solution)/shard_map/ppermute | solution.py:381
  248.1 28.5 %collective-permute-done.33.refs_1_ = bf16[512,128]{1,0:T(8,128)(2,1)S(1)} collective-permute-done((bf16[512,128]{1,0:T(8,128)(2,1)}, bf16[512,128]{1,0:T(8,128)(2,1)S(1)}, u32[]{:S(2)}, u32[]{:S(2)}) %collective-permute-start.33) | collective-permute-done | bytes 131104 | tf_op jit(solution)/shard_map/ppermute | solution.py:381
  277.3 10.9 %collective-permute-start.28 = (bf16[1792,128]{1,0:T(8,128)(2,1)S(1)}, bf16[1792,128]{1,0:T(8,128)(2,1)S(1)}, u32[]{:S(2)}, u32[]{:S(2)}) collective-permute-start(bf16[1792,128]{1,0:T(8,128)(2,1)S(1)} %bitcast.85), channel_id=1, source_target_pairs={{0,2},{1,3},{2,0},{3,1},{4,6},{5,7},{6,4},{7,5},{8,10},{9,11},{10,... | collective-permute-start | bytes 1376264 | tf_op jit(solution)/shard_map/ppermute | solution.py:381
  290.6 4.8 %collective-permute-start.38 = (bf16[1024,128]{1,0:T(8,128)(2,1)S(1)}, bf16[1024,128]{1,0:T(8,128)(2,1)S(1)}, u32[]{:S(2)}, u32[]{:S(2)}) collective-permute-start(bf16[1024,128]{1,0:T(8,128)(2,1)S(1)} %bitcast.138), channel_id=1, source_target_pairs={{0,3},{1,0},{2,1},{3,2},{4,7},{5,4},{6,5},{7,6},{8,11},{9,8},{10,9... | collective-permute-start | bytes 786440 | tf_op jit(solution)/shard_map/ppermute | solution.py:381
  296.2 13.6 %lattice_sum.3 = f32[16,128]{1,0:T(8,128)} custom-call(s32[1]{0:T(128)} %bitcast.place_ref, bf16[1792,128]{1,0:T(8,128)(2,1)} %bitcast.74, bf16[1792,128]{1,0:T(8,128)(2,1)} %bitcast.66, bf16[1792,128]{1,0:T(8,128)(2,1)} %bitcast.70, bf16[1024,128]{1,0:T(8,128)(2,1)} %bitcast.117, bf16[1792,128]{1,0:T(8,128)(2,1)} %bitcast.86, bf16[1792,128]{1,0:T(8,128)(2,1)} %bitcast.98, ...), custom_call_target="tpu_custom_call" | custom-call | tf_op jit(solution)/shard_map/lattice_sum/pallas_call | solution.py:328
  309.8 8.1 %lattice_sum.4 = f32[16,128]{1,0:T(8,128)} custom-call(s32[1]{0:T(128)} %bitcast.place_ref, bf16[1792,128]{1,0:T(8,128)(2,1)} %bitcast.75, bf16[1792,128]{1,0:T(8,128)(2,1)} %bitcast.67, bf16[1792,128]{1,0:T(8,128)(2,1)} %bitcast.71, bf16[512,128]{1,0:T(8,128)(2,1)} %bitcast.126, bf16[1792,128]{1,0:T(8,128)(2,1)} %bitcast.87, bf16[1792,128]{1,0:T(8,128)(2,1)} %bitcast.99, ...), custom_call_target="tpu_custom_call" | custom-call | tf_op jit(solution)/shard_map/lattice_sum/pallas_call | solution.py:328
  317.9 5.4 %lattice_sum.5 = f32[16,128]{1,0:T(8,128)} custom-call(s32[1]{0:T(128)} %bitcast.place_ref, bf16[1792,128]{1,0:T(8,128)(2,1)} %bitcast.76, bf16[1792,128]{1,0:T(8,128)(2,1)} %bitcast.68, bf16[1792,128]{1,0:T(8,128)(2,1)} %bitcast.72, bf16[256,128]{1,0:T(8,128)(2,1)} %bitcast.135, bf16[1792,128]{1,0:T(8,128)(2,1)} %bitcast.88, bf16[1792,128]{1,0:T(8,128)(2,1)} %bitcast.100, ...), custom_call_target="tpu_custom_call" | custom-call | tf_op jit(solution)/shard_map/lattice_sum/pallas_call | solution.py:328
  333.7 8.5 %quantize.6 = (bf16[1792,2048]{1,0:T(8,128)(2,1)}, f32[896,128]{1,0:T(8,128)}) custom-call(s32[1]{0:T(128)} %bitcast.place_ref, bf16[1792,128]{1,0:T(8,128)(2,1)} %bitcast.77, bf16[1792,128]{1,0:T(8,128)(2,1)} %collective-permute-done.30.refs_1_, bf16[1792,128]{1,0:T(8,128)(2,1)} %collective-permute-done.31.refs_2_, ...), custom_call_target="tpu_custom_call" | custom-call | tf_op jit(solution)/shard_map/quantize/pallas_call | solution.py:262
  343.9 3.2 collective-permute-start.20
  349.2 9.1 %quantize.7 = (bf16[1792,2048]{1,0:T(8,128)(2,1)}, f32[1792,256]{1,0:T(8,128)}) custom-call(s32[1]{0:T(128)} %bitcast.place_ref, bf16[1792,128]{1,0:T(8,128)(2,1)} %bitcast.69, bf16[1792,128]{1,0:T(8,128)(2,1)} %copy-done.11, bf16[1792,128]{1,0:T(8,128)(2,1)} %copy-done.14, ...), custom_call_target="tpu_custom_call", output_to_operand_aliasing={{0}: (9, {})} | custom-call | tf_op jit(solution)/shard_map/quantize/pallas_call | solution.py:262
  358.4 8.5 %quantize.8 = (bf16[1792,2048]{1,0:T(8,128)(2,1)}, f32[896,128]{1,0:T(8,128)}) custom-call(s32[1]{0:T(128)} %bitcast.place_ref, bf16[1792,128]{1,0:T(8,128)(2,1)} %bitcast.73, bf16[1792,128]{1,0:T(8,128)(2,1)} %collective-permute-done.24.refs_1_, bf16[1792,128]{1,0:T(8,128)(2,1)} %collective-permute-done.25.refs_2_, ...), custom_call_target="tpu_custom_call", output_to_operand_aliasing={{0}: (8, {})} | custom-call | tf_op jit(solution)/shard_map/quantize/pallas_call | solution.py:262
  366.9 6.0 %quantize.9 = (bf16[1792,2048]{1,0:T(8,128)(2,1)}, f32[1792,256]{1,0:T(8,128)}) custom-call(s32[1]{0:T(128)} %bitcast.place_ref, bf16[1024,128]{1,0:T(8,128)(2,1)} %bitcast.118, bf16[1024,128]{1,0:T(8,128)(2,1)} %copy-done.20, bf16[1024,128]{1,0:T(8,128)(2,1)} %collective-permute-done.37.refs_2_, ...), custom_call_target="tpu_custom_call", output_to_operand_aliasing={{0}: (9, {}), {1}: (10, {})} | custom-call | tf_op jit(solution)/shard_map/quantize/pallas_call | solution.py:262
  373.6 4.1 %quantize.10 = (bf16[1792,2048]{1,0:T(8,128)(2,1)}, f32[1792,256]{1,0:T(8,128)}) custom-call(s32[1]{0:T(128)} %bitcast.place_ref, bf16[512,128]{1,0:T(8,128)(2,1)} %bitcast.127, bf16[512,128]{1,0:T(8,128)(2,1)} %copy-done.25, bf16[512,128]{1,0:T(8,128)(2,1)} %copy-done.26, ...), custom_call_target="tpu_custom_call", output_to_operand_aliasing={{0}: (9, {}), {1}: (10, {})} | custom-call | tf_op jit(solution)/shard_map/quantize/pallas_call | solution.py:262
  (196 shorter events, 59.0 us)
Async XLA Ops:
  14.6 33.8 %collective-permute-start.2 = (bf16[1024,128]{1,0:T(8,128)(2,1)}, bf16[1024,128]{1,0:T(8,128)(2,1)S(1)}, u32[]{:S(2)}, u32[]{:S(2)}) collective-permute-start(bf16[1024,128]{1,0:T(8,128)(2,1)} %get-tuple-element.135), channel_id=1, source_target_pairs={{0,1},{1,2},{2,3},{3,0},{4,5},{5,6},{6,7},{7,4},{8,9},{9,10},{10,1... | collective-permute-start | bytes 786440 | tf_op jit(solution)/shard_map/ppermute | solution.py:381
  20.3 22.3 %collective-permute-start.1 = (bf16[512,128]{1,0:T(8,128)(2,1)S(1)}, bf16[512,128]{1,0:T(8,128)(2,1)S(1)}, u32[]{:S(2)}, u32[]{:S(2)}) collective-permute-start(bf16[512,128]{1,0:T(8,128)(2,1)S(1)} %copy-done.46), channel_id=1, source_target_pairs={{0,1},{1,2},{2,3},{3,0},{4,5},{5,6},{6,7},{7,4},{8,9},{9,10},{10,1... | collective-permute-start | bytes 393224 | tf_op jit(solution)/shard_map/ppermute | solution.py:381
  22.0 21.7 %collective-permute-start.4 = (bf16[512,128]{1,0:T(8,128)(2,1)S(1)}, bf16[512,128]{1,0:T(8,128)(2,1)S(1)}, u32[]{:S(2)}, u32[]{:S(2)}) collective-permute-start(bf16[512,128]{1,0:T(8,128)(2,1)S(1)} %copy-done.45), channel_id=1, source_target_pairs={{0,2},{1,3},{2,0},{3,1},{4,6},{5,7},{6,4},{7,5},{8,10},{9,11},{10,... | collective-permute-start | bytes 393224 | tf_op jit(solution)/shard_map/ppermute | solution.py:381
  40.4 45.4 %collective-permute-start.5 = (bf16[1024,128]{1,0:T(8,128)(2,1)}, bf16[1024,128]{1,0:T(8,128)(2,1)S(1)}, u32[]{:S(2)}, u32[]{:S(2)}) collective-permute-start(bf16[1024,128]{1,0:T(8,128)(2,1)} %get-tuple-element.138), channel_id=1, source_target_pairs={{0,2},{1,3},{2,0},{3,1},{4,6},{5,7},{6,4},{7,5},{8,10},{9,11},{10,... | collective-permute-start | bytes 786440 | tf_op jit(solution)/shard_map/ppermute | solution.py:381
  42.6 67.4 %collective-permute-start.12 = (bf16[1792,128]{1,0:T(8,128)(2,1)}, bf16[1792,128]{1,0:T(8,128)(2,1)S(1)}, u32[]{:S(2)}, u32[]{:S(2)}) collective-permute-start(bf16[1792,128]{1,0:T(8,128)(2,1)} %get-tuple-element.146), channel_id=1, source_target_pairs={{0,1},{1,2},{2,3},{3,0},{4,5},{5,6},{6,7},{7,4},{8,9},{9,10},{10,1... | collective-permute-start | bytes 1376264 | tf_op jit(solution)/shard_map/ppermute | solution.py:381
  44.4 68.9 %collective-permute-start.15 = (bf16[1792,128]{1,0:T(8,128)(2,1)}, bf16[1792,128]{1,0:T(8,128)(2,1)S(1)}, u32[]{:S(2)}, u32[]{:S(2)}) collective-permute-start(bf16[1792,128]{1,0:T(8,128)(2,1)} %get-tuple-element.150), channel_id=1, source_target_pairs={{0,1},{1,2},{2,3},{3,0},{4,5},{5,6},{6,7},{7,4},{8,9},{9,10},{10,1... | collective-permute-start | bytes 1376264 | tf_op jit(solution)/shard_map/ppermute | solution.py:381
  45.6 67.7 %collective-permute-start.16 = (bf16[1792,128]{1,0:T(8,128)(2,1)}, bf16[1792,128]{1,0:T(8,128)(2,1)S(1)}, u32[]{:S(2)}, u32[]{:S(2)}) collective-permute-start(bf16[1792,128]{1,0:T(8,128)(2,1)} %get-tuple-element.151), channel_id=1, source_target_pairs={{0,2},{1,3},{2,0},{3,1},{4,6},{5,7},{6,4},{7,5},{8,10},{9,11},{10,... | collective-permute-start | bytes 1376264 | tf_op jit(solution)/shard_map/ppermute | solution.py:381
  48.3 65.6 %collective-permute-start.17 = (bf16[1792,128]{1,0:T(8,128)(2,1)}, bf16[1792,128]{1,0:T(8,128)(2,1)S(1)}, u32[]{:S(2)}, u32[]{:S(2)}) collective-permute-start(bf16[1792,128]{1,0:T(8,128)(2,1)} %get-tuple-element.152), channel_id=1, source_target_pairs={{0,3},{1,0},{2,1},{3,2},{4,7},{5,4},{6,5},{7,6},{8,11},{9,8},{10,9... | collective-permute-start | bytes 1376264 | tf_op jit(solution)/shard_map/ppermute | solution.py:381
  99.9 69.4 %collective-permute-start.13 = (bf16[1792,128]{1,0:T(8,128)(2,1)}, bf16[1792,128]{1,0:T(8,128)(2,1)S(1)}, u32[]{:S(2)}, u32[]{:S(2)}) collective-permute-start(bf16[1792,128]{1,0:T(8,128)(2,1)} %get-tuple-element.147), channel_id=1, source_target_pairs={{0,2},{1,3},{2,0},{3,1},{4,6},{5,7},{6,4},{7,5},{8,10},{9,11},{10,... | collective-permute-start | bytes 1376264 | tf_op jit(solution)/shard_map/ppermute | solution.py:381
  110.0 59.4 %collective-permute-start.14 = (bf16[1792,128]{1,0:T(8,128)(2,1)}, bf16[1792,128]{1,0:T(8,128)(2,1)S(1)}, u32[]{:S(2)}, u32[]{:S(2)}) collective-permute-start(bf16[1792,128]{1,0:T(8,128)(2,1)} %get-tuple-element.148), channel_id=1, source_target_pairs={{0,3},{1,0},{2,1},{3,2},{4,7},{5,4},{6,5},{7,6},{8,11},{9,8},{10,9... | collective-permute-start | bytes 1376264 | tf_op jit(solution)/shard_map/ppermute | solution.py:381
  113.3 65.1 %collective-permute-start.9 = (bf16[1792,128]{1,0:T(8,128)(2,1)}, bf16[1792,128]{1,0:T(8,128)(2,1)}, u32[]{:S(2)}, u32[]{:S(2)}) collective-permute-start(bf16[1792,128]{1,0:T(8,128)(2,1)} %get-tuple-element.142), channel_id=1, source_target_pairs={{0,1},{1,2},{2,3},{3,0},{4,5},{5,6},{6,7},{7,4},{8,9},{9,10},{10,1... | collective-permute-start | bytes 1376264 | tf_op jit(solution)/shard_map/ppermute | solution.py:381
  113.3 65.1 %collective-permute-start.10 = (bf16[1792,128]{1,0:T(8,128)(2,1)}, bf16[1792,128]{1,0:T(8,128)(2,1)}, u32[]{:S(2)}, u32[]{:S(2)}) collective-permute-start(bf16[1792,128]{1,0:T(8,128)(2,1)} %get-tuple-element.143), channel_id=1, source_target_pairs={{0,2},{1,3},{2,0},{3,1},{4,6},{5,7},{6,4},{7,5},{8,10},{9,11},{10,... | collective-permute-start | bytes 1376264 | tf_op jit(solution)/shard_map/ppermute | solution.py:381
  113.9 64.5 %collective-permute-start.11 = (bf16[1792,128]{1,0:T(8,128)(2,1)}, bf16[1792,128]{1,0:T(8,128)(2,1)}, u32[]{:S(2)}, u32[]{:S(2)}) collective-permute-start(bf16[1792,128]{1,0:T(8,128)(2,1)} %get-tuple-element.144), channel_id=1, source_target_pairs={{0,3},{1,0},{2,1},{3,2},{4,7},{5,4},{6,5},{7,6},{8,11},{9,8},{10,9... | collective-permute-start | bytes 1376264 | tf_op jit(solution)/shard_map/ppermute | solution.py:381
  190.1 22.9 %collective-permute-start.22 = (f32[16,128]{1,0:T(8,128)}, f32[16,128]{1,0:T(8,128)S(1)}, u32[]{:S(2)}, u32[]{:S(2)}) collective-permute-start(f32[16,128]{1,0:T(8,128)} %get-tuple-element.172), channel_id=1, source_target_pairs={{0,2},{1,3},{2,0},{3,1},{4,6},{5,7},{6,4},{7,5},{8,10},{9,11},{10,... | collective-permute-start | bytes 24584 | tf_op jit(solution)/shard_map/ppermute | solution.py:381
  190.1 55.3 %collective-permute-start.30 = (bf16[1792,128]{1,0:T(8,128)(2,1)S(1)}, bf16[1792,128]{1,0:T(8,128)(2,1)}, u32[]{:S(2)}, u32[]{:S(2)}) collective-permute-start(bf16[1792,128]{1,0:T(8,128)(2,1)S(1)} %bitcast.89), channel_id=1, source_target_pairs={{0,1},{1,2},{2,3},{3,0},{4,5},{5,6},{6,7},{7,4},{8,9},{9,10},{10,1... | collective-permute-start | bytes 1376264 | tf_op jit(solution)/shard_map/ppermute | solution.py:381
  190.8 55.1 %collective-permute-start.31 = (bf16[1792,128]{1,0:T(8,128)(2,1)S(1)}, bf16[1792,128]{1,0:T(8,128)(2,1)}, u32[]{:S(2)}, u32[]{:S(2)}) collective-permute-start(bf16[1792,128]{1,0:T(8,128)(2,1)S(1)} %bitcast.93), channel_id=1, source_target_pairs={{0,2},{1,3},{2,0},{3,1},{4,6},{5,7},{6,4},{7,5},{8,10},{9,11},{10,... | collective-permute-start | bytes 1376264 | tf_op jit(solution)/shard_map/ppermute | solution.py:381
  193.2 54.3 %collective-permute-start.32 = (bf16[1792,128]{1,0:T(8,128)(2,1)S(1)}, bf16[1792,128]{1,0:T(8,128)(2,1)}, u32[]{:S(2)}, u32[]{:S(2)}) collective-permute-start(bf16[1792,128]{1,0:T(8,128)(2,1)S(1)} %bitcast.97), channel_id=1, source_target_pairs={{0,3},{1,0},{2,1},{3,2},{4,7},{5,4},{6,5},{7,6},{8,11},{9,8},{10,9... | collective-permute-start | bytes 1376264 | tf_op jit(solution)/shard_map/ppermute | solution.py:381
  196.1 92.1 %collective-permute-start.24 = (bf16[1792,128]{1,0:T(8,128)(2,1)S(1)}, bf16[1792,128]{1,0:T(8,128)(2,1)}, u32[]{:S(2)}, u32[]{:S(2)}) collective-permute-start(bf16[1792,128]{1,0:T(8,128)(2,1)S(1)} %bitcast.105), channel_id=1, source_target_pairs={{0,1},{1,2},{2,3},{3,0},{4,5},{5,6},{6,7},{7,4},{8,9},{9,10},{10,1... | collective-permute-start | bytes 1376264 | tf_op jit(solution)/shard_map/ppermute | solution.py:381
  233.9 55.2 %collective-permute-start.25 = (bf16[1792,128]{1,0:T(8,128)(2,1)}, bf16[1792,128]{1,0:T(8,128)(2,1)}, u32[]{:S(2)}, u32[]{:S(2)}) collective-permute-start(bf16[1792,128]{1,0:T(8,128)(2,1)} %bitcast.106), channel_id=1, source_target_pairs={{0,2},{1,3},{2,0},{3,1},{4,6},{5,7},{6,4},{7,5},{8,10},{9,11},{10,... | collective-permute-start | bytes 1376264 | tf_op jit(solution)/shard_map/ppermute | solution.py:381
  245.5 45.1 %collective-permute-start.26 = (bf16[1792,128]{1,0:T(8,128)(2,1)}, bf16[1792,128]{1,0:T(8,128)(2,1)S(1)}, u32[]{:S(2)}, u32[]{:S(2)}) collective-permute-start(bf16[1792,128]{1,0:T(8,128)(2,1)} %bitcast.110), channel_id=1, source_target_pairs={{0,3},{1,0},{2,1},{3,2},{4,7},{5,4},{6,5},{7,6},{8,11},{9,8},{10,9... | collective-permute-start | bytes 1376264 | tf_op jit(solution)/shard_map/ppermute | solution.py:381
  246.0 44.7 %collective-permute-start.27 = (bf16[1792,128]{1,0:T(8,128)(2,1)S(1)}, bf16[1792,128]{1,0:T(8,128)(2,1)S(1)}, u32[]{:S(2)}, u32[]{:S(2)}) collective-permute-start(bf16[1792,128]{1,0:T(8,128)(2,1)S(1)} %bitcast.101), channel_id=1, source_target_pairs={{0,1},{1,2},{2,3},{3,0},{4,5},{5,6},{6,7},{7,4},{8,9},{9,10},{10,1... | collective-permute-start | bytes 1376264 | tf_op jit(solution)/shard_map/ppermute | solution.py:381
  247.5 29.1 %collective-permute-start.33 = (bf16[512,128]{1,0:T(8,128)(2,1)}, bf16[512,128]{1,0:T(8,128)(2,1)S(1)}, u32[]{:S(2)}, u32[]{:S(2)}) collective-permute-start(bf16[512,128]{1,0:T(8,128)(2,1)} %bitcast.151), channel_id=1, source_target_pairs={{0,1},{1,2},{2,3},{3,0},{4,5},{5,6},{6,7},{7,4},{8,9},{9,10},{10,1... | collective-permute-start | bytes 393224 | tf_op jit(solution)/shard_map/ppermute | solution.py:381
  277.3 51.6 %collective-permute-start.28 = (bf16[1792,128]{1,0:T(8,128)(2,1)S(1)}, bf16[1792,128]{1,0:T(8,128)(2,1)S(1)}, u32[]{:S(2)}, u32[]{:S(2)}) collective-permute-start(bf16[1792,128]{1,0:T(8,128)(2,1)S(1)} %bitcast.85), channel_id=1, source_target_pairs={{0,2},{1,3},{2,0},{3,1},{4,6},{5,7},{6,4},{7,5},{8,10},{9,11},{10,... | collective-permute-start | bytes 1376264 | tf_op jit(solution)/shard_map/ppermute | solution.py:381
  288.2 43.4 %collective-permute-start.29 = (bf16[1792,128]{1,0:T(8,128)(2,1)S(1)}, bf16[1792,128]{1,0:T(8,128)(2,1)}, u32[]{:S(2)}, u32[]{:S(2)}) collective-permute-start(bf16[1792,128]{1,0:T(8,128)(2,1)S(1)} %bitcast.81), channel_id=1, source_target_pairs={{0,3},{1,0},{2,1},{3,2},{4,7},{5,4},{6,5},{7,6},{8,11},{9,8},{10,9... | collective-permute-start | bytes 1376264 | tf_op jit(solution)/shard_map/ppermute | solution.py:381
  289.0 53.2 %collective-permute-start.36 = (bf16[1024,128]{1,0:T(8,128)(2,1)}, bf16[1024,128]{1,0:T(8,128)(2,1)S(1)}, u32[]{:S(2)}, u32[]{:S(2)}) collective-permute-start(bf16[1024,128]{1,0:T(8,128)(2,1)} %bitcast.141), channel_id=1, source_target_pairs={{0,1},{1,2},{2,3},{3,0},{4,5},{5,6},{6,7},{7,4},{8,9},{9,10},{10,1... | collective-permute-start | bytes 786440 | tf_op jit(solution)/shard_map/ppermute | solution.py:381
  290.5 52.3 %collective-permute-start.37 = (bf16[1024,128]{1,0:T(8,128)(2,1)}, bf16[1024,128]{1,0:T(8,128)(2,1)}, u32[]{:S(2)}, u32[]{:S(2)}) collective-permute-start(bf16[1024,128]{1,0:T(8,128)(2,1)} %bitcast.139), channel_id=1, source_target_pairs={{0,2},{1,3},{2,0},{3,1},{4,6},{5,7},{6,4},{7,5},{8,10},{9,11},{10,... | collective-permute-start | bytes 786440 | tf_op jit(solution)/shard_map/ppermute | solution.py:381
  290.6 53.3 %collective-permute-start.38 = (bf16[1024,128]{1,0:T(8,128)(2,1)S(1)}, bf16[1024,128]{1,0:T(8,128)(2,1)S(1)}, u32[]{:S(2)}, u32[]{:S(2)}) collective-permute-start(bf16[1024,128]{1,0:T(8,128)(2,1)S(1)} %bitcast.138), channel_id=1, source_target_pairs={{0,3},{1,0},{2,1},{3,2},{4,7},{5,4},{6,5},{7,6},{8,11},{9,8},{10,9... | collective-permute-start | bytes 786440 | tf_op jit(solution)/shard_map/ppermute | solution.py:381
  328.8 44.0 %collective-permute-start.34 = (bf16[512,128]{1,0:T(8,128)(2,1)S(1)}, bf16[512,128]{1,0:T(8,128)(2,1)S(1)}, u32[]{:S(2)}, u32[]{:S(2)}) collective-permute-start(bf16[512,128]{1,0:T(8,128)(2,1)S(1)} %bitcast.150), channel_id=1, source_target_pairs={{0,2},{1,3},{2,0},{3,1},{4,6},{5,7},{6,4},{7,5},{8,10},{9,11},{10,... | collective-permute-start | bytes 393224 | tf_op jit(solution)/shard_map/ppermute | solution.py:381
  331.6 41.3 %collective-permute-start.35 = (bf16[512,128]{1,0:T(8,128)(2,1)S(1)}, bf16[512,128]{1,0:T(8,128)(2,1)S(1)}, u32[]{:S(2)}, u32[]{:S(2)}) collective-permute-start(bf16[512,128]{1,0:T(8,128)(2,1)S(1)} %bitcast.148), channel_id=1, source_target_pairs={{0,3},{1,0},{2,1},{3,2},{4,7},{5,4},{6,5},{7,6},{8,11},{9,8},{10,9... | collective-permute-start | bytes 393224 | tf_op jit(solution)/shard_map/ppermute | solution.py:381
  342.2 35.4 %collective-permute-start.18 = (bf16[256,128]{1,0:T(8,128)(2,1)S(1)}, bf16[256,128]{1,0:T(8,128)(2,1)S(1)}, u32[]{:S(2)}, u32[]{:S(2)}) collective-permute-start(bf16[256,128]{1,0:T(8,128)(2,1)S(1)} %bitcast.162), channel_id=1, source_target_pairs={{0,1},{1,2},{2,3},{3,0},{4,5},{5,6},{6,7},{7,4},{8,9},{9,10},{10,1... | collective-permute-start | bytes 196616 | tf_op jit(solution)/shard_map/ppermute | solution.py:381
  342.9 34.8 %collective-permute-start.19 = (bf16[256,128]{1,0:T(8,128)(2,1)S(1)}, bf16[256,128]{1,0:T(8,128)(2,1)S(1)}, u32[]{:S(2)}, u32[]{:S(2)}) collective-permute-start(bf16[256,128]{1,0:T(8,128)(2,1)S(1)} %bitcast.160), channel_id=1, source_target_pairs={{0,2},{1,3},{2,0},{3,1},{4,6},{5,7},{6,4},{7,5},{8,10},{9,11},{10,... | collective-permute-start | bytes 196616 | tf_op jit(solution)/shard_map/ppermute | solution.py:381
  343.9 33.8 %collective-permute-start.20 = (bf16[256,128]{1,0:T(8,128)(2,1)S(1)}, bf16[256,128]{1,0:T(8,128)(2,1)S(1)}, u32[]{:S(2)}, u32[]{:S(2)}) collective-permute-start(bf16[256,128]{1,0:T(8,128)(2,1)S(1)} %bitcast.158), channel_id=1, source_target_pairs={{0,3},{1,0},{2,1},{3,2},{4,7},{5,4},{6,5},{7,6},{8,11},{9,8},{10,9... | collective-permute-start | bytes 196616 | tf_op jit(solution)/shard_map/ppermute | solution.py:381
  (58 other events, 1488.0 us)

commit v5 on v3

--- a/solution.py
+++ b/solution.py
@@ -12,7 +12,7 @@
 INNER = 256
 LOW = 16
 CHUNKS = 4
-AHEAD = 2
+AHEAD = 3
 OCTET = 8
 TILE2 = 448
 
@@ -381,10 +381,10 @@
         return lax.ppermute(x, "row", [(k, (k + shift) % ring) for k in range(ring)])
 
     column_args = (weights[0], left_bits, right_bits, place, ring, chunks)
-    small, middle = blocks_here // 7, blocks_here * 2 // 7
-    thirds = (small, middle, blocks_here - small - middle)
+    small = max(blocks_here * 2 // 7, 1)
+    parts = (small, blocks_here - small)
     early, whole, first_row = [], None, 0
-    for count in thirds:
+    for count in parts:
         count *= HB
         piece_rows, whole = column_transform(*column_args, first_row, count, math.gcd(first_row, count) or count, whole)
         early.append(piece_rows)

time: 378 us -> 386 us (1.021)
  waiting for transfers between devices: 96 us -> 101 us
  starting transfers between devices: 138 us -> 142 us
    all_to_all x1, waiting for transfers between devices: 6.59 us -> 13.4 us  [body(): every_error = lax.all_to_all(copies, ('expert', 'row'), 0, 0)]
    ppermute x36 -> x33, starting transfers between devices: 133 us -> 136 us  [send(): lax.ppermute(x, 'row', [(k, (k + shift) % ring) for k in range(ring)])]
    ppermute x36 -> x33, waiting for transfers between devices: 89.4 us -> 87.6 us  [send(): lax.ppermute(x, 'row', [(k, (k + shift) % ring) for k in range(ring)])]
    pallas_call x3 -> x2, Pallas kernels: 13.8 us -> 12.6 us  [column_transform(): pl.pallas_call(kernel, grid=(rows // tile,), in_specs=in_specs, out_specs...]
  transfers between devices with their start and end apart: 37 -> 34, of which waited for: 8 -> 8; matrix products, arithmetic and copies ran while one was open for 9% -> 9% of each run, Pallas kernels for 23% -> 19%
where the time goes in v5:
time: 386 us
  starting transfers between devices  142 us (37%)
  Pallas kernels  101 us (26%)
  waiting for transfers between devices  101 us (26%)
  other arithmetic  30.5 us (8%)
  local copies, waits for them, and re-layouts  8.06 us (2%)
    ppermute x33, starting transfers between devices, send(): lax.ppermute(x, 'row', [(k, (k + shift) % ring) for k in range(ring)])  136 us
    ppermute x33, waiting for transfers between devices, send(): lax.ppermute(x, 'row', [(k, (k + shift) % ring) for k in range(ring)])  87.6 us
    pallas_call x5, Pallas kernels, quantize(): pl.pallas_call(kernel, grid=(rows // tile,), in_specs=in_specs, out_specs...  32.6 us
    pallas_call x4, Pallas kernels, row_mix(): pl.pallas_call(kernel, out_shape=[jax.ShapeDtypeStruct((n, high, LOW, wid...  31.8 us
    pallas_call x2, Pallas kernels, lattice_sum(): pl.pallas_call(kernel, grid=(rows // tile,), in_specs=in_specs, out_specs...  23.7 us
    convert_element_type x1, other arithmetic, mixer_table(): return jnp.where(common & 1 == 0, table, -table).astype(jnp.bfloat16)  20.4 us
    all_to_all x1, waiting for transfers between devices, body(): every_error = lax.all_to_all(copies, ('expert', 'row'), 0, 0)  13.4 us
    pallas_call x2, Pallas kernels, column_transform(): pl.pallas_call(kernel, grid=(rows // tile,), in_specs=in_specs, out_specs...  12.6 us
  transfers between devices with their start and end apart: 34, of which 8 were waited for; matrix products, arithmetic and copies ran while one was open for 9% of the time, Pallas kernels for 19%

profile of v5, /device:TPU:0, one launch (start us, length us, event | category | flops | bytes accessed | tf_op | source)
XLA Modules:
  0.0 385.6 jit_solution(16689263188216881360)
XLA Ops:
  0.6 4.4 %column_transform.2 = (bf16[512,128]{1,0:T(8,128)(2,1)}, bf16[512,128]{1,0:T(8,128)(2,1)}, bf16[512,128]{1,0:T(8,128)(2,1)}, bf16[512,128]{1,0:T(8,128)(2,1)}, b...) custom-call(s32[1]{0:T(128)} %bitcast.place_ref, ...), custom_call_target="tpu_custom_call" | custom-call | tf_op jit(solution)/shard_map/column_transform/pallas_call | solution.py:104
  5.1 8.2 %column_transform.3 = (bf16[1280,128]{1,0:T(8,128)(2,1)}, bf16[1280,128]{1,0:T(8,128)(2,1)}, bf16[1280,128]{1,0:T(8,128)(2,1)}, bf16[1280,128]{1,0:T(8,128)(2,1)...) custom-call(s32[1]{0:T(128)} %bitcast.place_ref, ...), custom_call_target="tpu_custom_call", output_to_operand_aliasing={{4}: (4, {}), {5}: (5, {}), {6}: (6, {}), {7}: (7, {}), {8}... | custom-call | tf_op jit(solution)/shard_map/column_transform/pallas_call | solution.py:104
  22.2 7.9 %collective-permute-done = bf16[512,128]{1,0:T(8,128)(2,1)S(1)} collective-permute-done((bf16[512,128]{1,0:T(8,128)(2,1)S(1)}, bf16[512,128]{1,0:T(8,128)(2,1)S(1)}, u32[]{:S(2)}, u32[]{:S(2)}) %collective-permute-start) | collective-permute-done | bytes 131104 | tf_op jit(solution)/shard_map/ppermute | solution.py:381
  30.1 11.1 %collective-permute-start.9 = (bf16[1792,128]{1,0:T(8,128)(2,1)}, bf16[1792,128]{1,0:T(8,128)(2,1)S(1)}, u32[]{:S(2)}, u32[]{:S(2)}) collective-permute-start(bf16[1792,128]{1,0:T(8,128)(2,1)} %get-tuple-element.106), channel_id=1, source_target_pairs={{0,1},{1,2},{2,3},{3,0},{4,5},{5,6},{6,7},{7,4},{8,9},{9,10},{10,1... | collective-permute-start | bytes 1376264 | tf_op jit(solution)/shard_map/ppermute | solution.py:381
  45.7 18.8 %collective-permute-start.13 = (bf16[1792,128]{1,0:T(8,128)(2,1)}, bf16[1792,128]{1,0:T(8,128)(2,1)S(1)}, u32[]{:S(2)}, u32[]{:S(2)}) collective-permute-start(bf16[1792,128]{1,0:T(8,128)(2,1)} %get-tuple-element.111), channel_id=1, source_target_pairs={{0,2},{1,3},{2,0},{3,1},{4,6},{5,7},{6,4},{7,5},{8,10},{9,11},{10,... | collective-permute-start | bytes 1376264 | tf_op jit(solution)/shard_map/ppermute | solution.py:381
  67.9 13.3 %collective-permute-done.3 = bf16[1280,128]{1,0:T(8,128)(2,1)S(1)} collective-permute-done((bf16[1280,128]{1,0:T(8,128)(2,1)}, bf16[1280,128]{1,0:T(8,128)(2,1)S(1)}, u32[]{:S(2)}, u32[]{:S(2)}) %collective-permute-start.3) | collective-permute-done | bytes 327712 | tf_op jit(solution)/shard_map/ppermute | solution.py:381
  81.2 16.7 %collective-permute-done.5 = bf16[1280,128]{1,0:T(8,128)(2,1)S(1)} collective-permute-done((bf16[1280,128]{1,0:T(8,128)(2,1)}, bf16[1280,128]{1,0:T(8,128)(2,1)S(1)}, u32[]{:S(2)}, u32[]{:S(2)}) %collective-permute-start.5) | collective-permute-done | bytes 327712 | tf_op jit(solution)/shard_map/ppermute | solution.py:381
  98.7 9.5 %collective-permute-start.10 = (bf16[1792,128]{1,0:T(8,128)(2,1)}, bf16[1792,128]{1,0:T(8,128)(2,1)S(1)}, u32[]{:S(2)}, u32[]{:S(2)}) collective-permute-start(bf16[1792,128]{1,0:T(8,128)(2,1)} %get-tuple-element.107), channel_id=1, source_target_pairs={{0,2},{1,3},{2,0},{3,1},{4,6},{5,7},{6,4},{7,5},{8,10},{9,11},{10,... | collective-permute-start | bytes 1376264 | tf_op jit(solution)/shard_map/ppermute | solution.py:381
  112.2 3.5 collective-permute-start.8
  115.7 20.4 %fusion.42.refs_8_.refs_4_ = bf16[896,896]{1,0:T(8,128)(2,1)} fusion(s32[896]{0:T(1024)S(1)} %get-tuple-element.166, s32[896]{0:T(1024)S(1)} %get-tuple-element.167, s32[896]{0:T(1024)S(1)} %get-tuple-element.165, s32[896]{0:T(1024)S(1)} %get-tuple-element.172, s32[]{:T(128)} %axis_index.22, s32[896]{0:T(1024)S(1)} %get-tuple-element.168, ...), kind=kLoop, calls=%fused_computation.87 | loop fusion | flops 69042176 | bytes 1629828 | tf_op jit(solution)/shard_map/convert_element_type | solution.py:352
  137.9 7.9 %row_mix.4 = (bf16[14,8,16,128]{3,2,1,0:T(8,128)(2,1)}, bf16[14,8,16,128]{3,2,1,0:T(8,128)(2,1)}, bf16[14,8,16,128]{3,2,1,0:T(8,128)(2,1)}, bf16[14,8,16,128]{3,2,1,0:T(8,128)(2,1)}, f32[16,128]{1,0:T(8,128)}) custom-call(bf16[4,8,16,128]{3,2,1,0:T(8,128)(2,1)} %bitcast.128, bf16[10,8,16,128]{3,2,1,0:T(8,128)(2,1)} %bitcast.114, ...), custom_call_target="tpu_custom_call" | custom-call | tf_op jit(solution)/shard_map/row_mix/pallas_call | solution.py:160
  145.8 7.9 %row_mix.5 = (bf16[14,8,16,128]{3,2,1,0:T(8,128)(2,1)}, bf16[14,8,16,128]{3,2,1,0:T(8,128)(2,1)}, bf16[14,8,16,128]{3,2,1,0:T(8,128)(2,1)}, bf16[14,8,16,128]{3,2,1,0:T(8,128)(2,1)}, f32[16,128]{1,0:T(8,128)}) custom-call(bf16[14,8,16,128]{3,2,1,0:T(8,128)(2,1)} %bitcast.93, bf16[14,8,16,128]{3,2,1,0:T(8,128)(2,1)} %bitcast.102, ...), custom_call_target="tpu_custom_call" | custom-call | tf_op jit(solution)/shard_map/row_mix/pallas_call | solution.py:160
  154.6 8.0 %row_mix.6 = (bf16[14,8,16,128]{3,2,1,0:T(8,128)(2,1)}, bf16[14,8,16,128]{3,2,1,0:T(8,128)(2,1)}, bf16[14,8,16,128]{3,2,1,0:T(8,128)(2,1)}, bf16[14,8,16,128]{3,2,1,0:T(8,128)(2,1)}, f32[16,128]{1,0:T(8,128)}) custom-call(bf16[14,8,16,128]{3,2,1,0:T(8,128)(2,1)} %bitcast.94, bf16[14,8,16,128]{3,2,1,0:T(8,128)(2,1)} %bitcast.101, ...), custom_call_target="tpu_custom_call" | custom-call | tf_op jit(solution)/shard_map/row_mix/pallas_call | solution.py:160
  162.7 6.4 %collective-permute-done.7 = bf16[1792,128]{1,0:T(8,128)(2,1)} collective-permute-done((bf16[1792,128]{1,0:T(8,128)(2,1)}, bf16[1792,128]{1,0:T(8,128)(2,1)}, u32[]{:S(2)}, u32[]{:S(2)}) %collective-permute-start.7) | collective-permute-done | bytes 458784 | tf_op jit(solution)/shard_map/ppermute | solution.py:381
  169.1 8.0 %row_mix.7 = (bf16[7,8,16,128]{3,2,1,0:T(8,128)(2,1)}, bf16[7,8,16,128]{3,2,1,0:T(8,128)(2,1)}, bf16[7,8,16,128]{3,2,1,0:T(8,128)(2,1)}, bf16[7,8,16,128]{3,2,1,...) custom-call(bf16[14,8,16,128]{3,2,1,0:T(8,128)(2,1)} %bitcast.95, ...), custom_call_target="tpu_custom_call" | custom-call | tf_op jit(solution)/shard_map/row_mix/pallas_call | solution.py:160
  177.2 12.5 %collective-permute-start.20 = (f32[16,128]{1,0:T(8,128)}, f32[16,128]{1,0:T(8,128)S(1)}, u32[]{:S(2)}, u32[]{:S(2)}) collective-permute-start(f32[16,128]{1,0:T(8,128)} %get-tuple-element.128), channel_id=1, source_target_pairs={{0,3},{1,0},{2,1},{3,2},{4,7},{5,4},{6,5},{7,6},{8,11},{9,8},{10,9... | collective-permute-start | bytes 24584 | tf_op jit(solution)/shard_map/ppermute | solution.py:381
  198.2 5.5 %fusion.22 = (bf16[1024,1024]{1,0:T(8,128)(2,1)}, bf16[1024,1024]{1,0:T(8,128)(2,1)}) fusion(s32[1024]{0:T(1024)S(1)} %get-tuple-element.173, s32[1024]{0:T(1024)S(1)} %get-tuple-element.176, s32[1024]{0:T(1024)S(1)} %get-tuple-element.174, s32[1024]{0:T(1024)S(1)} %get-tuple-element.175, pred[1024]{0:T(1024)(128)(4,1)S(1)} %get-tuple-element.177, ...), kind=kLoop, calls=%fused_computation.67 | loop fusion | flops 83886080 | bytes 4212740 | tf_op jit(solution)/shard_map/convert_element_type | solution.py:362
  208.3 17.2 %collective-permute-done.28.refs_2_ = bf16[1792,128]{1,0:T(8,128)(2,1)} collective-permute-done((bf16[1792,128]{1,0:T(8,128)(2,1)S(1)}, bf16[1792,128]{1,0:T(8,128)(2,1)}, u32[]{:S(2)}, u32[]{:S(2)}) %collective-permute-start.28) | collective-permute-done | bytes 458784 | tf_op jit(solution)/shard_map/ppermute | solution.py:381
  225.6 26.3 %collective-permute-start.24 = (bf16[1792,128]{1,0:T(8,128)(2,1)S(1)}, bf16[1792,128]{1,0:T(8,128)(2,1)S(1)}, u32[]{:S(2)}, u32[]{:S(2)}) collective-permute-start(bf16[1792,128]{1,0:T(8,128)(2,1)S(1)} %bitcast.83), channel_id=1, source_target_pairs={{0,1},{1,2},{2,3},{3,0},{4,5},{5,6},{6,7},{7,4},{8,9},{9,10},{10,1... | collective-permute-start | bytes 1376264 | tf_op jit(solution)/shard_map/ppermute | solution.py:381
  251.9 4.0 %collective-permute-start.25 = (bf16[1792,128]{1,0:T(8,128)(2,1)S(1)}, bf16[1792,128]{1,0:T(8,128)(2,1)S(1)}, u32[]{:S(2)}, u32[]{:S(2)}) collective-permute-start(bf16[1792,128]{1,0:T(8,128)(2,1)S(1)} %bitcast.71), channel_id=1, source_target_pairs={{0,2},{1,3},{2,0},{3,1},{4,6},{5,7},{6,4},{7,5},{8,10},{9,11},{10,... | collective-permute-start | bytes 1376264 | tf_op jit(solution)/shard_map/ppermute | solution.py:381
  258.5 24.3 %collective-permute-done.22.refs_2_ = bf16[1792,128]{1,0:T(8,128)(2,1)} collective-permute-done((bf16[1792,128]{1,0:T(8,128)(2,1)}, bf16[1792,128]{1,0:T(8,128)(2,1)}, u32[]{:S(2)}, u32[]{:S(2)}) %collective-permute-start.22) | collective-permute-done | bytes 458784 | tf_op jit(solution)/shard_map/ppermute | solution.py:381
  282.8 10.3 %collective-permute-start.30 = (bf16[896,128]{1,0:T(8,128)(2,1)}, bf16[896,128]{1,0:T(8,128)(2,1)}, u32[]{:S(2)}, u32[]{:S(2)}) collective-permute-start(bf16[896,128]{1,0:T(8,128)(2,1)} %bitcast.43.refs_7_), channel_id=1, source_target_pairs={{0,1},{1,2},{2,3},{3,0},{4,5},{5,6},{6,7},{7,4},{8,9},{9,10},{10,1... | collective-permute-start | bytes 688136 | tf_op jit(solution)/shard_map/ppermute | solution.py:381
  294.1 11.8 %lattice_sum.2 = f32[16,128]{1,0:T(8,128)} custom-call(s32[1]{0:T(128)} %bitcast.place_ref, bf16[1792,128]{1,0:T(8,128)(2,1)} %bitcast.63, bf16[1792,128]{1,0:T(8,128)(2,1)} %bitcast.57, bf16[1792,128]{1,0:T(8,128)(2,1)} %bitcast.60, bf16[896,128]{1,0:T(8,128)(2,1)} %bitcast.98, bf16[1792,128]{1,0:T(8,128)(2,1)} %bitcast.72, bf16[1792,128]{1,0:T(8,128)(2,1)} %bitcast.81, ...), custom_call_target="tpu_custom_call" | custom-call | tf_op jit(solution)/shard_map/lattice_sum/pallas_call | solution.py:328
  305.9 11.9 %lattice_sum.3 = f32[16,128]{1,0:T(8,128)} custom-call(s32[1]{0:T(128)} %bitcast.place_ref, bf16[1792,128]{1,0:T(8,128)(2,1)} %bitcast.64, bf16[1792,128]{1,0:T(8,128)(2,1)} %bitcast.58, bf16[1792,128]{1,0:T(8,128)(2,1)} %bitcast.61, bf16[896,128]{1,0:T(8,128)(2,1)} %bitcast.96, bf16[1792,128]{1,0:T(8,128)(2,1)} %bitcast.73, bf16[1792,128]{1,0:T(8,128)(2,1)} %bitcast.82, ...), custom_call_target="tpu_custom_call" | custom-call | tf_op jit(solution)/shard_map/lattice_sum/pallas_call | solution.py:328
  317.9 3.4 collective-permute-start.16
  328.4 5.3 %all-to-all-start = ((f32[32,1,1]{2,1,0:T(1,128)}), f32[32,1,1]{2,1,0:T(1,128)S(1)}, u32[]{:S(2)}, u32[]{:S(2)}) async-start(f32[32,1,1]{2,1,0:T(1,128)} %broadcast_in_dim.40), calls=%async_computation | async-start | bytes 32768 | tf_op jit(solution)/shard_map/all_to_all | solution.py:452
  334.5 7.3 %quantize.5 = (bf16[1792,2048]{1,0:T(8,128)(2,1)}, f32[896,128]{1,0:T(8,128)}) custom-call(s32[1]{0:T(128)} %bitcast.place_ref, bf16[1792,128]{1,0:T(8,128)(2,1)} %bitcast.65, bf16[1792,128]{1,0:T(8,128)(2,1)} %collective-permute-done.27.refs_1_, bf16[1792,128]{1,0:T(8,128)(2,1)} %collective-permute-done.28.refs_2_, ...), custom_call_target="tpu_custom_call" | custom-call | tf_op jit(solution)/shard_map/quantize/pallas_call | solution.py:262
  341.9 13.4 %all-to-all-done = f32[32,1,1]{2,1,0:T(1,128)S(1)} async-done(((f32[32,1,1]{2,1,0:T(1,128)}), f32[32,1,1]{2,1,0:T(1,128)S(1)}, u32[]{:S(2)}, u32[]{:S(2)}) %all-to-all-start) | async-done | bytes 160 | tf_op jit(solution)/shard_map/all_to_all | solution.py:452
  357.5 7.6 %quantize.6 = (bf16[1792,2048]{1,0:T(8,128)(2,1)}, f32[1792,256]{1,0:T(8,128)}) custom-call(s32[1]{0:T(128)} %bitcast.place_ref, bf16[1792,128]{1,0:T(8,128)(2,1)} %bitcast.59, bf16[1792,128]{1,0:T(8,128)(2,1)} %copy-done.13, bf16[1792,128]{1,0:T(8,128)(2,1)} %copy-done.15, ...), custom_call_target="tpu_custom_call", output_to_operand_aliasing={{0}: (9, {})} | custom-call | tf_op jit(solution)/shard_map/quantize/pallas_call | solution.py:262
  365.1 7.4 %quantize.7 = (bf16[1792,2048]{1,0:T(8,128)(2,1)}, f32[896,128]{1,0:T(8,128)}) custom-call(s32[1]{0:T(128)} %bitcast.place_ref, bf16[1792,128]{1,0:T(8,128)(2,1)} %bitcast.62, bf16[1792,128]{1,0:T(8,128)(2,1)} %collective-permute-done.21.refs_1_, bf16[1792,128]{1,0:T(8,128)(2,1)} %collective-permute-done.22.refs_2_, ...), custom_call_target="tpu_custom_call", output_to_operand_aliasing={{0}: (8, {})} | custom-call | tf_op jit(solution)/shard_map/quantize/pallas_call | solution.py:262
  373.3 5.1 %quantize.8 = (bf16[1792,2048]{1,0:T(8,128)(2,1)}, f32[1792,256]{1,0:T(8,128)}) custom-call(s32[1]{0:T(128)} %bitcast.place_ref, bf16[896,128]{1,0:T(8,128)(2,1)} %bitcast.99, bf16[896,128]{1,0:T(8,128)(2,1)} %collective-permute-done.30.refs_1_, bf16[896,128]{1,0:T(8,128)(2,1)} %copy-done.25, ...), custom_call_target="tpu_custom_call", output_to_operand_aliasing={{0}: (9, {}), {1}: (10, {})} | custom-call | tf_op jit(solution)/shard_map/quantize/pallas_call | solution.py:262
  379.3 5.1 %quantize.9 = (bf16[1792,2048]{1,0:T(8,128)(2,1)}, f32[1792,256]{1,0:T(8,128)}) custom-call(s32[1]{0:T(128)} %bitcast.place_ref, bf16[896,128]{1,0:T(8,128)(2,1)} %bitcast.97, bf16[896,128]{1,0:T(8,128)(2,1)} %copy-done.22, bf16[896,128]{1,0:T(8,128)(2,1)} %copy-done.23, bf16[896,128]{1,0:T(8,128)(2,1)} %copy-done.24, ...), custom_call_target="tpu_custom_call", output_to_operand_aliasing={{0}: (9, {}), {1}: (10, {})} | custom-call | tf_op jit(solution)/shard_map/quantize/pallas_call | solution.py:262
  (153 shorter events, 51.4 us)
Async XLA Ops:
  13.3 51.2 %collective-permute-start.1 = (bf16[1280,128]{1,0:T(8,128)(2,1)}, bf16[1280,128]{1,0:T(8,128)(2,1)S(1)}, u32[]{:S(2)}, u32[]{:S(2)}) collective-permute-start(bf16[1280,128]{1,0:T(8,128)(2,1)} %get-tuple-element.97), channel_id=1, source_target_pairs={{0,1},{1,2},{2,3},{3,0},{4,5},{5,6},{6,7},{7,4},{8,9},{9,10},{10,1... | collective-permute-start | bytes 983048 | tf_op jit(solution)/shard_map/ppermute | solution.py:381
  16.3 13.7 %collective-permute-start = (bf16[512,128]{1,0:T(8,128)(2,1)S(1)}, bf16[512,128]{1,0:T(8,128)(2,1)S(1)}, u32[]{:S(2)}, u32[]{:S(2)}) collective-permute-start(bf16[512,128]{1,0:T(8,128)(2,1)S(1)} %copy-done.35), channel_id=1, source_target_pairs={{0,1},{1,2},{2,3},{3,0},{4,5},{5,6},{6,7},{7,4},{8,9},{9,10},{10,1... | collective-permute-start | bytes 393224 | tf_op jit(solution)/shard_map/ppermute | solution.py:381
  17.9 23.3 %collective-permute-start.2 = (bf16[512,128]{1,0:T(8,128)(2,1)S(1)}, bf16[512,128]{1,0:T(8,128)(2,1)S(1)}, u32[]{:S(2)}, u32[]{:S(2)}) collective-permute-start(bf16[512,128]{1,0:T(8,128)(2,1)S(1)} %copy-done.34), channel_id=1, source_target_pairs={{0,2},{1,3},{2,0},{3,1},{4,6},{5,7},{6,4},{7,5},{8,10},{9,11},{10,... | collective-permute-start | bytes 393224 | tf_op jit(solution)/shard_map/ppermute | solution.py:381
  19.0 26.1 %collective-permute-start.4 = (bf16[512,128]{1,0:T(8,128)(2,1)S(1)}, bf16[512,128]{1,0:T(8,128)(2,1)S(1)}, u32[]{:S(2)}, u32[]{:S(2)}) collective-permute-start(bf16[512,128]{1,0:T(8,128)(2,1)S(1)} %copy-done.33), channel_id=1, source_target_pairs={{0,3},{1,0},{2,1},{3,2},{4,7},{5,4},{6,5},{7,6},{8,11},{9,8},{10,9... | collective-permute-start | bytes 393224 | tf_op jit(solution)/shard_map/ppermute | solution.py:381
  21.8 59.4 %collective-permute-start.3 = (bf16[1280,128]{1,0:T(8,128)(2,1)}, bf16[1280,128]{1,0:T(8,128)(2,1)S(1)}, u32[]{:S(2)}, u32[]{:S(2)}) collective-permute-start(bf16[1280,128]{1,0:T(8,128)(2,1)} %get-tuple-element.99), channel_id=1, source_target_pairs={{0,2},{1,3},{2,0},{3,1},{4,6},{5,7},{6,4},{7,5},{8,10},{9,11},{10,... | collective-permute-start | bytes 983048 | tf_op jit(solution)/shard_map/ppermute | solution.py:381
  30.1 78.2 %collective-permute-start.9 = (bf16[1792,128]{1,0:T(8,128)(2,1)}, bf16[1792,128]{1,0:T(8,128)(2,1)S(1)}, u32[]{:S(2)}, u32[]{:S(2)}) collective-permute-start(bf16[1792,128]{1,0:T(8,128)(2,1)} %get-tuple-element.106), channel_id=1, source_target_pairs={{0,1},{1,2},{2,3},{3,0},{4,5},{5,6},{6,7},{7,4},{8,9},{9,10},{10,1... | collective-permute-start | bytes 1376264 | tf_op jit(solution)/shard_map/ppermute | solution.py:381
  41.8 69.7 %collective-permute-start.12 = (bf16[1792,128]{1,0:T(8,128)(2,1)}, bf16[1792,128]{1,0:T(8,128)(2,1)S(1)}, u32[]{:S(2)}, u32[]{:S(2)}) collective-permute-start(bf16[1792,128]{1,0:T(8,128)(2,1)} %get-tuple-element.110), channel_id=1, source_target_pairs={{0,1},{1,2},{2,3},{3,0},{4,5},{5,6},{6,7},{7,4},{8,9},{9,10},{10,1... | collective-permute-start | bytes 1376264 | tf_op jit(solution)/shard_map/ppermute | solution.py:381
  45.7 65.8 %collective-permute-start.13 = (bf16[1792,128]{1,0:T(8,128)(2,1)}, bf16[1792,128]{1,0:T(8,128)(2,1)S(1)}, u32[]{:S(2)}, u32[]{:S(2)}) collective-permute-start(bf16[1792,128]{1,0:T(8,128)(2,1)} %get-tuple-element.111), channel_id=1, source_target_pairs={{0,2},{1,3},{2,0},{3,1},{4,6},{5,7},{6,4},{7,5},{8,10},{9,11},{10,... | collective-permute-start | bytes 1376264 | tf_op jit(solution)/shard_map/ppermute | solution.py:381
  64.5 47.6 %collective-permute-start.14 = (bf16[1792,128]{1,0:T(8,128)(2,1)}, bf16[1792,128]{1,0:T(8,128)(2,1)S(1)}, u32[]{:S(2)}, u32[]{:S(2)}) collective-permute-start(bf16[1792,128]{1,0:T(8,128)(2,1)} %get-tuple-element.112), channel_id=1, source_target_pairs={{0,3},{1,0},{2,1},{3,2},{4,7},{5,4},{6,5},{7,6},{8,11},{9,8},{10,9... | collective-permute-start | bytes 1376264 | tf_op jit(solution)/shard_map/ppermute | solution.py:381
  81.2 16.8 %collective-permute-start.5 = (bf16[1280,128]{1,0:T(8,128)(2,1)}, bf16[1280,128]{1,0:T(8,128)(2,1)S(1)}, u32[]{:S(2)}, u32[]{:S(2)}) collective-permute-start(bf16[1280,128]{1,0:T(8,128)(2,1)} %get-tuple-element.101), channel_id=1, source_target_pairs={{0,3},{1,0},{2,1},{3,2},{4,7},{5,4},{6,5},{7,6},{8,11},{9,8},{10,9... | collective-permute-start | bytes 983048 | tf_op jit(solution)/shard_map/ppermute | solution.py:381
  98.7 55.0 %collective-permute-start.10 = (bf16[1792,128]{1,0:T(8,128)(2,1)}, bf16[1792,128]{1,0:T(8,128)(2,1)S(1)}, u32[]{:S(2)}, u32[]{:S(2)}) collective-permute-start(bf16[1792,128]{1,0:T(8,128)(2,1)} %get-tuple-element.107), channel_id=1, source_target_pairs={{0,2},{1,3},{2,0},{3,1},{4,6},{5,7},{6,4},{7,5},{8,10},{9,11},{10,... | collective-permute-start | bytes 1376264 | tf_op jit(solution)/shard_map/ppermute | solution.py:381
  108.2 45.5 %collective-permute-start.11 = (bf16[1792,128]{1,0:T(8,128)(2,1)}, bf16[1792,128]{1,0:T(8,128)(2,1)S(1)}, u32[]{:S(2)}, u32[]{:S(2)}) collective-permute-start(bf16[1792,128]{1,0:T(8,128)(2,1)} %get-tuple-element.108), channel_id=1, source_target_pairs={{0,3},{1,0},{2,1},{3,2},{4,7},{5,4},{6,5},{7,6},{8,11},{9,8},{10,9... | collective-permute-start | bytes 1376264 | tf_op jit(solution)/shard_map/ppermute | solution.py:381
  111.5 51.2 %collective-permute-start.6 = (bf16[1792,128]{1,0:T(8,128)(2,1)}, bf16[1792,128]{1,0:T(8,128)(2,1)S(1)}, u32[]{:S(2)}, u32[]{:S(2)}) collective-permute-start(bf16[1792,128]{1,0:T(8,128)(2,1)} %get-tuple-element.102), channel_id=1, source_target_pairs={{0,1},{1,2},{2,3},{3,0},{4,5},{5,6},{6,7},{7,4},{8,9},{9,10},{10,1... | collective-permute-start | bytes 1376264 | tf_op jit(solution)/shard_map/ppermute | solution.py:381
  111.6 57.5 %collective-permute-start.7 = (bf16[1792,128]{1,0:T(8,128)(2,1)}, bf16[1792,128]{1,0:T(8,128)(2,1)}, u32[]{:S(2)}, u32[]{:S(2)}) collective-permute-start(bf16[1792,128]{1,0:T(8,128)(2,1)} %get-tuple-element.103), channel_id=1, source_target_pairs={{0,2},{1,3},{2,0},{3,1},{4,6},{5,7},{6,4},{7,5},{8,10},{9,11},{10,... | collective-permute-start | bytes 1376264 | tf_op jit(solution)/shard_map/ppermute | solution.py:381
  112.2 56.9 %collective-permute-start.8 = (bf16[1792,128]{1,0:T(8,128)(2,1)}, bf16[1792,128]{1,0:T(8,128)(2,1)}, u32[]{:S(2)}, u32[]{:S(2)}) collective-permute-start(bf16[1792,128]{1,0:T(8,128)(2,1)} %get-tuple-element.104), channel_id=1, source_target_pairs={{0,3},{1,0},{2,1},{3,2},{4,7},{5,4},{6,5},{7,6},{8,11},{9,8},{10,9... | collective-permute-start | bytes 1376264 | tf_op jit(solution)/shard_map/ppermute | solution.py:381
  177.2 16.9 %collective-permute-start.20 = (f32[16,128]{1,0:T(8,128)}, f32[16,128]{1,0:T(8,128)S(1)}, u32[]{:S(2)}, u32[]{:S(2)}) collective-permute-start(f32[16,128]{1,0:T(8,128)} %get-tuple-element.128), channel_id=1, source_target_pairs={{0,3},{1,0},{2,1},{3,2},{4,7},{5,4},{6,5},{7,6},{8,11},{9,8},{10,9... | collective-permute-start | bytes 24584 | tf_op jit(solution)/shard_map/ppermute | solution.py:381
  190.3 15.5 %collective-permute-start.27 = (bf16[1792,128]{1,0:T(8,128)(2,1)S(1)}, bf16[1792,128]{1,0:T(8,128)(2,1)}, u32[]{:S(2)}, u32[]{:S(2)}) collective-permute-start(bf16[1792,128]{1,0:T(8,128)(2,1)S(1)} %bitcast.74), channel_id=1, source_target_pairs={{0,1},{1,2},{2,3},{3,0},{4,5},{5,6},{6,7},{7,4},{8,9},{9,10},{10,1... | collective-permute-start | bytes 1376264 | tf_op jit(solution)/shard_map/ppermute | solution.py:381
  193.2 32.3 %collective-permute-start.28 = (bf16[1792,128]{1,0:T(8,128)(2,1)S(1)}, bf16[1792,128]{1,0:T(8,128)(2,1)}, u32[]{:S(2)}, u32[]{:S(2)}) collective-permute-start(bf16[1792,128]{1,0:T(8,128)(2,1)S(1)} %bitcast.77), channel_id=1, source_target_pairs={{0,2},{1,3},{2,0},{3,1},{4,6},{5,7},{6,4},{7,5},{8,10},{9,11},{10,... | collective-permute-start | bytes 1376264 | tf_op jit(solution)/shard_map/ppermute | solution.py:381
  194.1 57.8 %collective-permute-start.29 = (bf16[1792,128]{1,0:T(8,128)(2,1)S(1)}, bf16[1792,128]{1,0:T(8,128)(2,1)}, u32[]{:S(2)}, u32[]{:S(2)}) collective-permute-start(bf16[1792,128]{1,0:T(8,128)(2,1)S(1)} %bitcast.80), channel_id=1, source_target_pairs={{0,3},{1,0},{2,1},{3,2},{4,7},{5,4},{6,5},{7,6},{8,11},{9,8},{10,9... | collective-permute-start | bytes 1376264 | tf_op jit(solution)/shard_map/ppermute | solution.py:381
  195.7 60.2 %collective-permute-start.21 = (bf16[1792,128]{1,0:T(8,128)(2,1)}, bf16[1792,128]{1,0:T(8,128)(2,1)}, u32[]{:S(2)}, u32[]{:S(2)}) collective-permute-start(bf16[1792,128]{1,0:T(8,128)(2,1)} %bitcast.87), channel_id=1, source_target_pairs={{0,1},{1,2},{2,3},{3,0},{4,5},{5,6},{6,7},{7,4},{8,9},{9,10},{10,1... | collective-permute-start | bytes 1376264 | tf_op jit(solution)/shard_map/ppermute | solution.py:381
  196.2 86.6 %collective-permute-start.22 = (bf16[1792,128]{1,0:T(8,128)(2,1)}, bf16[1792,128]{1,0:T(8,128)(2,1)}, u32[]{:S(2)}, u32[]{:S(2)}) collective-permute-start(bf16[1792,128]{1,0:T(8,128)(2,1)} %bitcast.90), channel_id=1, source_target_pairs={{0,2},{1,3},{2,0},{3,1},{4,6},{5,7},{6,4},{7,5},{8,10},{9,11},{10,... | collective-permute-start | bytes 1376264 | tf_op jit(solution)/shard_map/ppermute | solution.py:381
  205.8 111.9 %collective-permute-start.23 = (bf16[1792,128]{1,0:T(8,128)(2,1)S(1)}, bf16[1792,128]{1,0:T(8,128)(2,1)S(1)}, u32[]{:S(2)}, u32[]{:S(2)}) collective-permute-start(bf16[1792,128]{1,0:T(8,128)(2,1)S(1)} %bitcast.86), channel_id=1, source_target_pairs={{0,3},{1,0},{2,1},{3,2},{4,7},{5,4},{6,5},{7,6},{8,11},{9,8},{10,9... | collective-permute-start | bytes 1376264 | tf_op jit(solution)/shard_map/ppermute | solution.py:381
  225.6 92.3 %collective-permute-start.24 = (bf16[1792,128]{1,0:T(8,128)(2,1)S(1)}, bf16[1792,128]{1,0:T(8,128)(2,1)S(1)}, u32[]{:S(2)}, u32[]{:S(2)}) collective-permute-start(bf16[1792,128]{1,0:T(8,128)(2,1)S(1)} %bitcast.83), channel_id=1, source_target_pairs={{0,1},{1,2},{2,3},{3,0},{4,5},{5,6},{6,7},{7,4},{8,9},{9,10},{10,1... | collective-permute-start | bytes 1376264 | tf_op jit(solution)/shard_map/ppermute | solution.py:381
  251.9 69.4 %collective-permute-start.25 = (bf16[1792,128]{1,0:T(8,128)(2,1)S(1)}, bf16[1792,128]{1,0:T(8,128)(2,1)S(1)}, u32[]{:S(2)}, u32[]{:S(2)}) collective-permute-start(bf16[1792,128]{1,0:T(8,128)(2,1)S(1)} %bitcast.71), channel_id=1, source_target_pairs={{0,2},{1,3},{2,0},{3,1},{4,6},{5,7},{6,4},{7,5},{8,10},{9,11},{10,... | collective-permute-start | bytes 1376264 | tf_op jit(solution)/shard_map/ppermute | solution.py:381
  255.9 68.3 %collective-permute-start.26 = (bf16[1792,128]{1,0:T(8,128)(2,1)S(1)}, bf16[1792,128]{1,0:T(8,128)(2,1)}, u32[]{:S(2)}, u32[]{:S(2)}) collective-permute-start(bf16[1792,128]{1,0:T(8,128)(2,1)S(1)} %bitcast.68), channel_id=1, source_target_pairs={{0,3},{1,0},{2,1},{3,2},{4,7},{5,4},{6,5},{7,6},{8,11},{9,8},{10,9... | collective-permute-start | bytes 1376264 | tf_op jit(solution)/shard_map/ppermute | solution.py:381
  282.8 41.4 %collective-permute-start.30 = (bf16[896,128]{1,0:T(8,128)(2,1)}, bf16[896,128]{1,0:T(8,128)(2,1)}, u32[]{:S(2)}, u32[]{:S(2)}) collective-permute-start(bf16[896,128]{1,0:T(8,128)(2,1)} %bitcast.43.refs_7_), channel_id=1, source_target_pairs={{0,1},{1,2},{2,3},{3,0},{4,5},{5,6},{6,7},{7,4},{8,9},{9,10},{10,1... | collective-permute-start | bytes 688136 | tf_op jit(solution)/shard_map/ppermute | solution.py:381
  317.8 60.6 %collective-permute-start.15 = (bf16[896,128]{1,0:T(8,128)(2,1)}, bf16[896,128]{1,0:T(8,128)(2,1)S(1)}, u32[]{:S(2)}, u32[]{:S(2)}) collective-permute-start(bf16[896,128]{1,0:T(8,128)(2,1)} %bitcast.123), channel_id=1, source_target_pairs={{0,1},{1,2},{2,3},{3,0},{4,5},{5,6},{6,7},{7,4},{8,9},{9,10},{10,1... | collective-permute-start | bytes 688136 | tf_op jit(solution)/shard_map/ppermute | solution.py:381
  317.9 60.6 %collective-permute-start.16 = (bf16[896,128]{1,0:T(8,128)(2,1)}, bf16[896,128]{1,0:T(8,128)(2,1)S(1)}, u32[]{:S(2)}, u32[]{:S(2)}) collective-permute-start(bf16[896,128]{1,0:T(8,128)(2,1)} %bitcast.121), channel_id=1, source_target_pairs={{0,2},{1,3},{2,0},{3,1},{4,6},{5,7},{6,4},{7,5},{8,10},{9,11},{10,... | collective-permute-start | bytes 688136 | tf_op jit(solution)/shard_map/ppermute | solution.py:381
  321.3 57.1 %collective-permute-start.17 = (bf16[896,128]{1,0:T(8,128)(2,1)S(1)}, bf16[896,128]{1,0:T(8,128)(2,1)S(1)}, u32[]{:S(2)}, u32[]{:S(2)}) collective-permute-start(bf16[896,128]{1,0:T(8,128)(2,1)S(1)} %bitcast.119), channel_id=1, source_target_pairs={{0,3},{1,0},{2,1},{3,2},{4,7},{5,4},{6,5},{7,6},{8,11},{9,8},{10,9... | collective-permute-start | bytes 688136 | tf_op jit(solution)/shard_map/ppermute | solution.py:381
  324.2 48.3 %collective-permute-start.31 = (bf16[896,128]{1,0:T(8,128)(2,1)}, bf16[896,128]{1,0:T(8,128)(2,1)S(1)}, u32[]{:S(2)}, u32[]{:S(2)}) collective-permute-start(bf16[896,128]{1,0:T(8,128)(2,1)} %bitcast.127), channel_id=1, source_target_pairs={{0,2},{1,3},{2,0},{3,1},{4,6},{5,7},{6,4},{7,5},{8,10},{9,11},{10,... | collective-permute-start | bytes 688136 | tf_op jit(solution)/shard_map/ppermute | solution.py:381
  324.2 48.3 %collective-permute-start.32 = (bf16[896,128]{1,0:T(8,128)(2,1)}, bf16[896,128]{1,0:T(8,128)(2,1)S(1)}, u32[]{:S(2)}, u32[]{:S(2)}) collective-permute-start(bf16[896,128]{1,0:T(8,128)(2,1)} %bitcast.125), channel_id=1, source_target_pairs={{0,3},{1,0},{2,1},{3,2},{4,7},{5,4},{6,5},{7,6},{8,11},{9,8},{10,9... | collective-permute-start | bytes 688136 | tf_op jit(solution)/shard_map/ppermute | solution.py:381
  328.4 26.9 %all-to-all-start = ((f32[32,1,1]{2,1,0:T(1,128)}), f32[32,1,1]{2,1,0:T(1,128)S(1)}, u32[]{:S(2)}, u32[]{:S(2)}) async-start(f32[32,1,1]{2,1,0:T(1,128)} %broadcast_in_dim.40), calls=%async_computation | async-start | bytes 32768 | tf_op jit(solution)/shard_map/all_to_all | solution.py:452
  (38 other events, 1116.2 us)
